TPU v7x, 128 devices: a whole 4x4x4 slice. The times are simulated.
128 devices in a mesh: grp: 4 (over x), dom: 32 (over z, y, core).
Axes of the slice: x: 4, y: 4, z: 4, core: 2. Of those that a mesh axis runs over, the one named last changes fastest.
Arguments:
- displacement: float32 [4, 3, 64, 96, 128], P('grp', None, 'dom'), may hold values from -3 to 3
- velocity: float32 [4, 3, 64, 96, 128], P('grp', None, 'dom'), may hold values from -6 to 6
- external: float32 [4, 3, 64, 96, 128], P('grp', None, 'dom'), may hold values from -6 to 6
- mass: float32 [4, 64, 96, 128], P('grp', 'dom'), may hold values from 1 to 3
- elem_scale: float32 [4, 64, 96, 128], P('grp', 'dom'), may hold values from 0.05 to 0.5
- stiffness: float32 [4, 24, 24], P('grp'), as said below
- substeps: int32 [4], P('grp'), may hold values from 1 to 8
- own_nodes: int32 [4, 512], P('grp', 'dom'), may hold values from 0 to 24575, as said below
- peer_nodes: int32 [4, 512], P('grp', 'dom'), may hold values from 0 to 24575, as said below
- normals: float32 [4, 3, 512], P('grp', None, 'dom'), may hold values from -4 to 4
- schur_inverse: float32 [2048, 2048], P(('grp', 'dom')), as said below
Outputs:
- new_displacement: float32 [4, 3, 64, 96, 128], P('grp', None, 'dom')
- new_velocity: float32 [4, 3, 64, 96, 128], P('grp', None, 'dom')
Inputs may be any that keep to these rules, and one draw needn't show every extreme that they name: `own_nodes`: the 16 entries of one device's block are distinct. `peer_nodes`: the 16 entries of one device's block are distinct. `schur_inverse`: symmetric. `stiffness`: symmetric positive definite.
All inputs are finite; a program needn't handle non-finite values.
Results may differ from a plain program's by a relative error of at most 0.0001.
Values sent between devices are 32-bit elements; how exact they have to be, the bound alone decides.
No kernel may reach another device: no remote copies, remote signals or barrier semaphores. Data moves between devices by JAX's collectives and lax.ppermute only.
A program may use at most 64 MiB of HBM per device.

v0:
```python
import jax
import jax.numpy as jnp
from jax import lax
from jax.sharding import PartitionSpec as P

MAXSUB = 8


coarse_step = 0.4


def shifted(x, axis, by):
    length = lax.axis_size(axis)
    pairs = [(i, i + by) for i in range(length) if 0 <= i + by < length]
    return lax.ppermute(x, axis, pairs)


def shifted_2(block, axis, distance):
    devices = range(lax.axis_size(axis))
    route = [((i - distance) % len(devices), i) for i in devices]
    return lax.ppermute(block, axis, route)


def corner_stack(padded, planes):
    pieces = []
    for plane_off in (0, 1):
        for row_off in (0, 1):
            for col_off in (0, 1):
                block = padded[:, plane_off : plane_off + planes]
                block = jnp.roll(block, -row_off, axis=2)
                pieces.append(jnp.roll(block, -col_off, axis=3))
    return jnp.stack(pieces, 0).reshape(24, -1)


def element_forces(padded, scale, kmat):
    stacked = corner_stack(padded, scale.shape[0])
    forces = jnp.dot(
        kmat, stacked, precision=lax.Precision.HIGHEST, preferred_element_type=jnp.float32
    )
    forces = forces * scale.reshape(1, -1)
    return forces.reshape((8, 3) + scale.shape)


def assemble(forces):
    planes = forces.shape[2]
    total = jnp.zeros((3, planes + 1) + forces.shape[3:], jnp.float32)
    corner = 0
    for plane_off in (0, 1):
        for row_off in (0, 1):
            for col_off in (0, 1):
                part = jnp.roll(jnp.roll(forces[corner], row_off, axis=2), col_off, axis=3)
                total = total + jnp.pad(part, ((0, 0), (plane_off, 1 - plane_off), (0, 0), (0, 0)))
                corner = corner + 1
    return total


def on_device(
    displacement,
    velocity,
    external,
    mass,
    elem_scale,
    stiffness,
    substeps,
    own_nodes,
    peer_nodes,
    normals,
    schur_inverse,
):
    field = displacement[0]
    speed = velocity[0]
    loads = external[0]
    weight = mass[0]
    scale = elem_scale[0]
    kmat = stiffness[0]
    count = substeps[0]
    delta = coarse_step / count.astype(jnp.float32)

    def internal(state_field):
        upper = shifted(state_field[:, :1], "dom", -1)
        padded = jnp.concatenate([state_field, upper], 1)
        nodal = assemble(element_forces(padded, scale, kmat))
        carried = shifted(nodal[:, -1:], "dom", 1)
        return nodal[:, :-1] + jnp.pad(carried, ((0, 0), (0, nodal.shape[1] - 2), (0, 0), (0, 0)))

    def advance(step, state):
        state_field, state_speed = state
        accel = (loads - internal(state_field)) / weight
        next_speed = state_speed + delta * accel
        next_field = state_field + delta * next_speed
        active = step < count
        return (
            jnp.where(active, next_field, state_field),
            jnp.where(active, next_speed, state_speed),
        )

    field, speed = lax.fori_loop(0, MAXSUB, advance, (field, speed))
    flat_speed = speed.reshape(3, -1)
    masses = weight.reshape(-1)
    own = own_nodes[0]
    peer = peer_nodes[0]
    direction = normals[0]
    own_speed = flat_speed[:, own]
    far_speed = shifted_2(flat_speed[:, peer], "grp", -1)
    gap = jnp.sum(direction * (own_speed - far_speed), axis=0)
    multiplier = lax.psum_scatter(
        jnp.dot(
            schur_inverse.T,
            gap,
            precision=lax.Precision.HIGHEST,
            preferred_element_type=jnp.float32,
        ),
        ("grp", "dom"),
        scatter_dimension=0,
        tiled=True,
    )
    correction = multiplier[None, :] * direction
    incoming = shifted_2(correction, "grp", 1)
    flat_speed = flat_speed.at[:, own].add(-correction / masses[own][None, :])
    flat_speed = flat_speed.at[:, peer].add(incoming / masses[peer][None, :])
    return (field[None], flat_speed.reshape(speed.shape)[None])


def solution(mesh):
    return jax.shard_map(
        on_device,
        mesh=mesh,
        in_specs=(
            P("grp", None, "dom", None, None),
            P("grp", None, "dom", None, None),
            P("grp", None, "dom", None, None),
            P("grp", "dom", None, None),
            P("grp", "dom", None, None),
            P("grp", None, None),
            P("grp"),
            P("grp", "dom"),
            P("grp", "dom"),
            P("grp", None, "dom"),
            P(("grp", "dom"), None),
        ),
        out_specs=(P("grp", None, "dom", None, None), P("grp", None, "dom", None, None)),
        check_vma=False,
    )
```

profile of v0, /device:TPU:1, one launch (start us, length us, event | category | flops | bytes accessed | tf_op | source)
XLA Modules:
  0.0 312.3 jit_solution(7745012983853332474)
XLA Ops:
  4.0 176.3 %while.17 = (s32[]{:T(128)}, f32[3,2,96,128]{3,2,1,0:T(8,128)S(1)}, f32[3,2,96,128]{3,2,1,0:T(8,128)S(1)}, s32[]{:T(128)}, f32[]{:T(128)}, /*index=5*/f32[24,24]...) while((s32[]{:T(128)}, f32[3,2,96,128]{3,2,1,0:T(8,128)S(1)}, ...), condition=%wide.region_1.2_spmd, body=%wide.region_0.1_spmd.sunk | while | flops 175142016 | bytes 37897272 | solution.py:97
  4.0 3.3 %collective-permute-start = (f32[3,1,96,128]{3,2,1,0:T(8,128)S(1)}, f32[3,1,96,128]{3,2,1,0:T(8,128)S(1)}, u32[]{:S(2)}, u32[]{:S(2)}) collective-permute-start(f32[3,1,96,128]{3,2,1,0:T(8,128)S(1)} %slice.562), channel_id=1, source_target_pairs={{1,0},{2,1},{3,2},{4,3},{5,4},{6,5},{7,6},{8,7},{9,8},{10,9},{11,1... | collective-permute-start | bytes 442376 | tf_op jit(solution)/shard_map/while/body/eval_jaxpr/ppermute | solution.py:15
  17.0 2.2 fusion.62
  21.0 2.7 collective-permute-start.1
  26.0 1.9 collective-permute-start
  38.7 2.2 fusion.62
  42.7 2.7 collective-permute-start.1
  47.7 1.9 collective-permute-start
  60.4 2.2 fusion.62
  64.4 2.7 collective-permute-start.1
  69.4 1.9 collective-permute-start
  82.2 2.2 fusion.62
  86.2 2.7 collective-permute-start.1
  91.2 1.9 collective-permute-start
  103.9 2.2 fusion.62
  107.9 2.7 collective-permute-start.1
  112.9 1.9 collective-permute-start
  125.7 2.2 fusion.62
  129.7 2.7 collective-permute-start.1
  147.4 2.2 fusion.62
  151.4 2.7 collective-permute-start.1
  161.9 3.8 %collective-permute-done = f32[3,1,96,128]{3,2,1,0:T(8,128)S(1)} collective-permute-done((f32[3,1,96,128]{3,2,1,0:T(8,128)S(1)}, f32[3,1,96,128]{3,2,1,0:T(8,128)S(1)}, u32[]{:S(2)}, u32[]{:S(2)}) %collective-permute-start) | collective-permute-done | bytes 147488 | tf_op jit(solution)/shard_map/while/body/eval_jaxpr/ppermute | solution.py:15
  171.3 2.2 fusion.62
  175.3 2.7 collective-permute-start.1
  180.3 6.6 %copy.23 = f32[3,2,96,128]{0,3,2,1:T(8,128)} copy(f32[3,2,96,128]{3,2,1,0:T(8,128)S(1)} %get-tuple-element.224) | data formatting | bytes 589824 | tf_op jit(solution)/shard_map/while | solution.py:97
  186.9 5.1 %gather_fusion.1 = f32[16,3]{1,0:T(8,128)S(1)} fusion(f32[3,24576]{0,1:T(8,128)} %bitcast.191, s32[1024]{0:T(1024)S(1)} %pad_clamp_fusion), kind=kCustom, calls=%fused_computation.1 | custom fusion | bytes 448 | tf_op jit(solution)/shard_map/gather | solution.py:104
  192.1 2.5 collective-permute-start.2
  196.0 5.1 %gather_fusion = f32[16,3]{1,0:T(8,128)S(1)} fusion(f32[3,24576]{0,1:T(8,128)} %bitcast.192, s32[1024]{0:T(1024)S(1)} %pad_clamp_fusion.1), kind=kCustom, calls=%fused_computation | custom fusion | bytes 448 | tf_op jit(solution)/shard_map/gather | solution.py:103
  201.5 81.5 %all-reduce.9 = f32[2048]{0:T(1024)S(1)} all-reduce(f32[2048]{0:T(1024)S(1)} %bitcast.208), channel_id=2, replica_groups=mesh['grp'=4,'dom'=32] {'grp','dom'}, use_global_device_ids=true, to_apply=%region_3.4.clone | all-reduce | flops 2048 | bytes 16384
  284.5 9.7 %scatter_fusion = f32[3,24576]{0,1:T(8,128)} fusion(f32[3,24576]{0,1:T(8,128)} %bitcast.193, s32[16]{0:T(128)S(1)} %fusion.29, f32[16,3]{1,0:T(8,128)S(1)} %copy.25), kind=kCustom, calls=%fused_computation.4 | custom fusion | flops 48 | bytes 640 | tf_op jit(solution)/shard_map/scatter-add | solution.py:119
  294.3 9.7 %scatter_fusion.1 = f32[3,24576]{0,1:T(8,128)} fusion(f32[3,24576]{0,1:T(8,128)} %scatter_fusion, s32[16]{0:T(128)S(1)} %fusion.30, f32[16,3]{1,0:T(8,128)S(1)} %copy.26), kind=kCustom, calls=%fused_computation.5 | custom fusion | flops 48 | bytes 640 | tf_op jit(solution)/shard_map/scatter-add | solution.py:120
  304.0 8.3 %copy.27 = f32[1,3,2,96,128]{4,3,2,1,0:T(8,128)} copy(f32[1,3,2,96,128]{1,4,3,2,0:T(8,128)} %bitcast.194) | data formatting | bytes 589824
  (447 shorter events, 118.5 us)
Async XLA Ops:
  0.6 200.7 %copy-start = (f32[16,2048]{1,0:T(8,128)S(1)}, f32[16,2048]{1,0:T(8,128)}, u32[]{:S(2)}) copy-start(f32[16,2048]{1,0:T(8,128)} %param.23) | copy-start | bytes 393220
  4.0 7.4 %collective-permute-start = (f32[3,1,96,128]{3,2,1,0:T(8,128)S(1)}, f32[3,1,96,128]{3,2,1,0:T(8,128)S(1)}, u32[]{:S(2)}, u32[]{:S(2)}) collective-permute-start(f32[3,1,96,128]{3,2,1,0:T(8,128)S(1)} %slice.562), channel_id=1, source_target_pairs={{1,0},{2,1},{3,2},{4,3},{5,4},{6,5},{7,6},{8,7},{9,8},{10,9},{11,1... | collective-permute-start | bytes 442376 | tf_op jit(solution)/shard_map/while/body/eval_jaxpr/ppermute | solution.py:15
  20.5 5.2 %copy-start.2 = (f32[1,2,96,128]{3,2,1,0:T(8,128)S(1)}, f32[1,2,96,128]{3,2,1,0:T(8,128)}, u32[]{:S(2)}) copy-start(f32[1,2,96,128]{3,2,1,0:T(8,128)} %get-tuple-element.370) | copy-start | bytes 294916 | tf_op jit(solution)/shard_map/while
  21.0 4.8 %collective-permute-start.1 = (f32[3,1,96,128]{3,2,1,0:T(8,128)S(1)}, f32[3,1,96,128]{3,2,1,0:T(8,128)S(1)}, u32[]{:S(2)}, u32[]{:S(2)}) collective-permute-start(f32[3,1,96,128]{3,2,1,0:T(8,128)S(1)} %slice.573), channel_id=1, source_target_pairs={{0,1},{1,2},{2,3},{3,4},{4,5},{5,6},{6,7},{7,8},{8,9},{9,10},{10,1... | collective-permute-start | bytes 442376 | tf_op jit(solution)/shard_map/while/body/eval_jaxpr/ppermute | solution.py:15
  26.0 7.2 %collective-permute-start = (f32[3,1,96,128]{3,2,1,0:T(8,128)S(1)}, f32[3,1,96,128]{3,2,1,0:T(8,128)S(1)}, u32[]{:S(2)}, u32[]{:S(2)}) collective-permute-start(f32[3,1,96,128]{3,2,1,0:T(8,128)S(1)} %slice.562), channel_id=1, source_target_pairs={{1,0},{2,1},{3,2},{4,3},{5,4},{6,5},{7,6},{8,7},{9,8},{10,9},{11,1... | collective-permute-start | bytes 442376 | tf_op jit(solution)/shard_map/while/body/eval_jaxpr/ppermute | solution.py:15
  42.3 5.2 %copy-start.2 = (f32[1,2,96,128]{3,2,1,0:T(8,128)S(1)}, f32[1,2,96,128]{3,2,1,0:T(8,128)}, u32[]{:S(2)}) copy-start(f32[1,2,96,128]{3,2,1,0:T(8,128)} %get-tuple-element.370) | copy-start | bytes 294916 | tf_op jit(solution)/shard_map/while
  42.7 4.8 %collective-permute-start.1 = (f32[3,1,96,128]{3,2,1,0:T(8,128)S(1)}, f32[3,1,96,128]{3,2,1,0:T(8,128)S(1)}, u32[]{:S(2)}, u32[]{:S(2)}) collective-permute-start(f32[3,1,96,128]{3,2,1,0:T(8,128)S(1)} %slice.573), channel_id=1, source_target_pairs={{0,1},{1,2},{2,3},{3,4},{4,5},{5,6},{6,7},{7,8},{8,9},{9,10},{10,1... | collective-permute-start | bytes 442376 | tf_op jit(solution)/shard_map/while/body/eval_jaxpr/ppermute | solution.py:15
  47.7 7.2 %collective-permute-start = (f32[3,1,96,128]{3,2,1,0:T(8,128)S(1)}, f32[3,1,96,128]{3,2,1,0:T(8,128)S(1)}, u32[]{:S(2)}, u32[]{:S(2)}) collective-permute-start(f32[3,1,96,128]{3,2,1,0:T(8,128)S(1)} %slice.562), channel_id=1, source_target_pairs={{1,0},{2,1},{3,2},{4,3},{5,4},{6,5},{7,6},{8,7},{9,8},{10,9},{11,1... | collective-permute-start | bytes 442376 | tf_op jit(solution)/shard_map/while/body/eval_jaxpr/ppermute | solution.py:15
  64.0 5.2 %copy-start.2 = (f32[1,2,96,128]{3,2,1,0:T(8,128)S(1)}, f32[1,2,96,128]{3,2,1,0:T(8,128)}, u32[]{:S(2)}) copy-start(f32[1,2,96,128]{3,2,1,0:T(8,128)} %get-tuple-element.370) | copy-start | bytes 294916 | tf_op jit(solution)/shard_map/while
  64.4 4.8 %collective-permute-start.1 = (f32[3,1,96,128]{3,2,1,0:T(8,128)S(1)}, f32[3,1,96,128]{3,2,1,0:T(8,128)S(1)}, u32[]{:S(2)}, u32[]{:S(2)}) collective-permute-start(f32[3,1,96,128]{3,2,1,0:T(8,128)S(1)} %slice.573), channel_id=1, source_target_pairs={{0,1},{1,2},{2,3},{3,4},{4,5},{5,6},{6,7},{7,8},{8,9},{9,10},{10,1... | collective-permute-start | bytes 442376 | tf_op jit(solution)/shard_map/while/body/eval_jaxpr/ppermute | solution.py:15
  69.4 7.2 %collective-permute-start = (f32[3,1,96,128]{3,2,1,0:T(8,128)S(1)}, f32[3,1,96,128]{3,2,1,0:T(8,128)S(1)}, u32[]{:S(2)}, u32[]{:S(2)}) collective-permute-start(f32[3,1,96,128]{3,2,1,0:T(8,128)S(1)} %slice.562), channel_id=1, source_target_pairs={{1,0},{2,1},{3,2},{4,3},{5,4},{6,5},{7,6},{8,7},{9,8},{10,9},{11,1... | collective-permute-start | bytes 442376 | tf_op jit(solution)/shard_map/while/body/eval_jaxpr/ppermute | solution.py:15
  85.7 5.2 %copy-start.2 = (f32[1,2,96,128]{3,2,1,0:T(8,128)S(1)}, f32[1,2,96,128]{3,2,1,0:T(8,128)}, u32[]{:S(2)}) copy-start(f32[1,2,96,128]{3,2,1,0:T(8,128)} %get-tuple-element.370) | copy-start | bytes 294916 | tf_op jit(solution)/shard_map/while
  86.2 4.8 %collective-permute-start.1 = (f32[3,1,96,128]{3,2,1,0:T(8,128)S(1)}, f32[3,1,96,128]{3,2,1,0:T(8,128)S(1)}, u32[]{:S(2)}, u32[]{:S(2)}) collective-permute-start(f32[3,1,96,128]{3,2,1,0:T(8,128)S(1)} %slice.573), channel_id=1, source_target_pairs={{0,1},{1,2},{2,3},{3,4},{4,5},{5,6},{6,7},{7,8},{8,9},{9,10},{10,1... | collective-permute-start | bytes 442376 | tf_op jit(solution)/shard_map/while/body/eval_jaxpr/ppermute | solution.py:15
  91.2 7.2 %collective-permute-start = (f32[3,1,96,128]{3,2,1,0:T(8,128)S(1)}, f32[3,1,96,128]{3,2,1,0:T(8,128)S(1)}, u32[]{:S(2)}, u32[]{:S(2)}) collective-permute-start(f32[3,1,96,128]{3,2,1,0:T(8,128)S(1)} %slice.562), channel_id=1, source_target_pairs={{1,0},{2,1},{3,2},{4,3},{5,4},{6,5},{7,6},{8,7},{9,8},{10,9},{11,1... | collective-permute-start | bytes 442376 | tf_op jit(solution)/shard_map/while/body/eval_jaxpr/ppermute | solution.py:15
  107.5 5.2 %copy-start.2 = (f32[1,2,96,128]{3,2,1,0:T(8,128)S(1)}, f32[1,2,96,128]{3,2,1,0:T(8,128)}, u32[]{:S(2)}) copy-start(f32[1,2,96,128]{3,2,1,0:T(8,128)} %get-tuple-element.370) | copy-start | bytes 294916 | tf_op jit(solution)/shard_map/while
  107.9 4.8 %collective-permute-start.1 = (f32[3,1,96,128]{3,2,1,0:T(8,128)S(1)}, f32[3,1,96,128]{3,2,1,0:T(8,128)S(1)}, u32[]{:S(2)}, u32[]{:S(2)}) collective-permute-start(f32[3,1,96,128]{3,2,1,0:T(8,128)S(1)} %slice.573), channel_id=1, source_target_pairs={{0,1},{1,2},{2,3},{3,4},{4,5},{5,6},{6,7},{7,8},{8,9},{9,10},{10,1... | collective-permute-start | bytes 442376 | tf_op jit(solution)/shard_map/while/body/eval_jaxpr/ppermute | solution.py:15
  112.9 7.2 %collective-permute-start = (f32[3,1,96,128]{3,2,1,0:T(8,128)S(1)}, f32[3,1,96,128]{3,2,1,0:T(8,128)S(1)}, u32[]{:S(2)}, u32[]{:S(2)}) collective-permute-start(f32[3,1,96,128]{3,2,1,0:T(8,128)S(1)} %slice.562), channel_id=1, source_target_pairs={{1,0},{2,1},{3,2},{4,3},{5,4},{6,5},{7,6},{8,7},{9,8},{10,9},{11,1... | collective-permute-start | bytes 442376 | tf_op jit(solution)/shard_map/while/body/eval_jaxpr/ppermute | solution.py:15
  129.2 5.2 %copy-start.2 = (f32[1,2,96,128]{3,2,1,0:T(8,128)S(1)}, f32[1,2,96,128]{3,2,1,0:T(8,128)}, u32[]{:S(2)}) copy-start(f32[1,2,96,128]{3,2,1,0:T(8,128)} %get-tuple-element.370) | copy-start | bytes 294916 | tf_op jit(solution)/shard_map/while
  129.2 5.2 %copy-start.4 = (f32[3,2,96,128]{3,2,1,0:T(8,128)S(1)}, f32[3,2,96,128]{3,2,1,0:T(8,128)}, u32[]{:S(2)}) copy-start(f32[3,2,96,128]{3,2,1,0:T(8,128)} %get-tuple-element.369) | copy-start | bytes 884740 | tf_op jit(solution)/shard_map/while
  129.7 4.8 %collective-permute-start.1 = (f32[3,1,96,128]{3,2,1,0:T(8,128)S(1)}, f32[3,1,96,128]{3,2,1,0:T(8,128)S(1)}, u32[]{:S(2)}, u32[]{:S(2)}) collective-permute-start(f32[3,1,96,128]{3,2,1,0:T(8,128)S(1)} %slice.573), channel_id=1, source_target_pairs={{0,1},{1,2},{2,3},{3,4},{4,5},{5,6},{6,7},{7,8},{8,9},{9,10},{10,1... | collective-permute-start | bytes 442376 | tf_op jit(solution)/shard_map/while/body/eval_jaxpr/ppermute | solution.py:15
  134.7 7.2 %collective-permute-start = (f32[3,1,96,128]{3,2,1,0:T(8,128)S(1)}, f32[3,1,96,128]{3,2,1,0:T(8,128)S(1)}, u32[]{:S(2)}, u32[]{:S(2)}) collective-permute-start(f32[3,1,96,128]{3,2,1,0:T(8,128)S(1)} %slice.562), channel_id=1, source_target_pairs={{1,0},{2,1},{3,2},{4,3},{5,4},{6,5},{7,6},{8,7},{9,8},{10,9},{11,1... | collective-permute-start | bytes 442376 | tf_op jit(solution)/shard_map/while/body/eval_jaxpr/ppermute | solution.py:15
  151.0 5.2 %copy-start.2 = (f32[1,2,96,128]{3,2,1,0:T(8,128)S(1)}, f32[1,2,96,128]{3,2,1,0:T(8,128)}, u32[]{:S(2)}) copy-start(f32[1,2,96,128]{3,2,1,0:T(8,128)} %get-tuple-element.370) | copy-start | bytes 294916 | tf_op jit(solution)/shard_map/while
  151.4 4.8 %collective-permute-start.1 = (f32[3,1,96,128]{3,2,1,0:T(8,128)S(1)}, f32[3,1,96,128]{3,2,1,0:T(8,128)S(1)}, u32[]{:S(2)}, u32[]{:S(2)}) collective-permute-start(f32[3,1,96,128]{3,2,1,0:T(8,128)S(1)} %slice.573), channel_id=1, source_target_pairs={{0,1},{1,2},{2,3},{3,4},{4,5},{5,6},{6,7},{7,8},{8,9},{9,10},{10,1... | collective-permute-start | bytes 442376 | tf_op jit(solution)/shard_map/while/body/eval_jaxpr/ppermute | solution.py:15
  156.4 9.3 %collective-permute-start = (f32[3,1,96,128]{3,2,1,0:T(8,128)S(1)}, f32[3,1,96,128]{3,2,1,0:T(8,128)S(1)}, u32[]{:S(2)}, u32[]{:S(2)}) collective-permute-start(f32[3,1,96,128]{3,2,1,0:T(8,128)S(1)} %slice.562), channel_id=1, source_target_pairs={{1,0},{2,1},{3,2},{4,3},{5,4},{6,5},{7,6},{8,7},{9,8},{10,9},{11,1... | collective-permute-start | bytes 442376 | tf_op jit(solution)/shard_map/while/body/eval_jaxpr/ppermute | solution.py:15
  174.8 5.2 %copy-start.2 = (f32[1,2,96,128]{3,2,1,0:T(8,128)S(1)}, f32[1,2,96,128]{3,2,1,0:T(8,128)}, u32[]{:S(2)}) copy-start(f32[1,2,96,128]{3,2,1,0:T(8,128)} %get-tuple-element.370) | copy-start | bytes 294916 | tf_op jit(solution)/shard_map/while
  175.3 4.8 %collective-permute-start.1 = (f32[3,1,96,128]{3,2,1,0:T(8,128)S(1)}, f32[3,1,96,128]{3,2,1,0:T(8,128)S(1)}, u32[]{:S(2)}, u32[]{:S(2)}) collective-permute-start(f32[3,1,96,128]{3,2,1,0:T(8,128)S(1)} %slice.573), channel_id=1, source_target_pairs={{0,1},{1,2},{2,3},{3,4},{4,5},{5,6},{6,7},{7,8},{8,9},{9,10},{10,1... | collective-permute-start | bytes 442376 | tf_op jit(solution)/shard_map/while/body/eval_jaxpr/ppermute | solution.py:15
  180.3 6.7 %copy-start.1 = (f32[3,2,96,128]{3,2,1,0:T(8,128)}, f32[3,2,96,128]{3,2,1,0:T(8,128)S(1)}, u32[]{:S(2)}) copy-start(f32[3,2,96,128]{3,2,1,0:T(8,128)S(1)} %get-tuple-element.223) | copy-start | bytes 884740
  180.3 14.4 %copy-start.8 = (s32[1,16]{1,0:T(1,128)S(1)}, s32[1,16]{1,0:T(1,128)}, u32[]{:S(2)}) copy-start(s32[1,16]{1,0:T(1,128)} %param.20) | copy-start | bytes 196
  180.3 14.4 %copy-start.3 = (f32[1,2,96,128]{3,2,1,0:T(8,128)S(1)}, f32[1,2,96,128]{3,2,1,0:T(8,128)}, u32[]{:S(2)}) copy-start(f32[1,2,96,128]{3,2,1,0:T(8,128)} %get-tuple-element.372) | copy-start | bytes 294916
  180.3 20.8 %copy-start.7 = (f32[1,3,16]{2,0,1:T(1,128)S(1)}, f32[1,3,16]{2,0,1:T(1,128)}, u32[]{:S(2)}) copy-start(f32[1,3,16]{2,0,1:T(1,128)} %param.22) | copy-start | bytes 580
  192.1 9.1 %collective-permute-start.2 = (f32[3,16]{0,1:T(8,128)S(1)}, f32[3,16]{0,1:T(8,128)S(1)}, u32[]{:S(2)}, u32[]{:S(2)}) collective-permute-start(f32[3,16]{0,1:T(8,128)S(1)} %bitcast.210), channel_id=1, source_target_pairs={{32,0},{64,32},{96,64},{0,96},{33,1},{65,33},{97,65},{1,97},{34,2}... | collective-permute-start | bytes 584 | tf_op jit(solution)/shard_map/ppermute | solution.py:21
  283.2 11.1 %collective-permute-start.3 = (f32[3,16]{1,0:T(4,128)S(1)}, f32[3,16]{1,0:T(4,128)S(1)}, u32[]{:S(2)}, u32[]{:S(2)}) collective-permute-start(f32[3,16]{1,0:T(4,128)S(1)} %get-tuple-element.261), channel_id=1, source_target_pairs={{96,0},{0,32},{32,64},{64,96},{97,1},{1,33},{33,65},{65,97},{98,2}... | collective-permute-start | bytes 584 | tf_op jit(solution)/shard_map/ppermute | solution.py:21
  (23 other events, 67.4 us)
where the time goes:
time: 313 us; the launch traced here: 312 us
  blocking collectives  81.5 us (26%)
  other arithmetic  68.5 us (22%)
  local copies, waits for them, and re-layouts  67.2 us (21%)
  starting transfers between devices  42.1 us (13%)
  waiting for transfers between devices  25.9 us (8%)
  matrix products  17.8 us (6%)
  loops' own time  7.77 us (2%)
    unnamed x1, blocking collectives  81.5 us
    ppermute x16, starting transfers between devices, shifted(): return lax.ppermute(x, axis, pairs)  38.3 us
    while x40, other arithmetic  32.4 us
    ppermute x16, waiting for transfers between devices, shifted(): return lax.ppermute(x, axis, pairs)  25.9 us
    while x160, local copies, waits for them, and re-layouts  17.8 us
    dot_general x8, matrix products, element_forces(): jnp.dot(kmat, stacked, precision=lax.Precision.HIGHEST, preferred_element...  17.6 us
    reshape x8, local copies, waits for them, and re-layouts, corner_stack(): return jnp.stack(pieces, 0).reshape(24, -1)  15.3 us
    unnamed x15, local copies, waits for them, and re-layouts  10.3 us
  transfers between devices with their start and end apart: 18, of which 16 were waited for; matrix products, arithmetic and copies ran while one was open for 14% of the time, Pallas kernels for 0%

commit v1 on v0

v1 whole, which is shorter than its diff:
```python
import jax
import jax.numpy as jnp
import numpy as np
from jax import lax
from jax.experimental import pallas as pl
from jax.experimental.pallas import tpu as pltpu
from jax.sharding import PartitionSpec as P

MAXSUB = 8
COARSE = 0.4
ROWS = 96
COLS = 128
SLOTS = 18
WROW = 4 * SLOTS
DUP = 56
F32 = jnp.float32
VM = pl.BlockSpec(memory_space=pltpu.VMEM)
SM = pl.BlockSpec(memory_space=pltpu.SMEM)


def selectors():
    pick_row = np.zeros((128, 24), np.float32)
    pick_col = np.zeros((2, 24, 256), np.float32)
    keep = np.zeros((2, 128, 256), np.float32)
    cols = []
    for part in range(4):
        b = part % 2
        width = WROW if part < 2 else DUP
        for k in range(width):
            kind, i = divmod(k, SLOTS)
            used = part < 2 or kind < 2
            cols.append((b, kind % 2, i // 3 - 2, i % 3) if used else None)
    for k, slot in enumerate(cols):
        if slot is None:
            continue
        b, e, plane, comp = slot
        for a in (0, 1):
            pick_col[a, (4 * a + 2 * b + e) * 3 + comp, k] = 1.0
    for tile in range(2):
        for g in range(8):
            for q in range(6):
                comp, x = divmod(q, 2)
                plane = x if tile == 0 else (-1 if x == 0 else 2)
                layer = plane - g // 4
                m = tile * 64 + g * 8 + q
                pick_row[m, g * 3 + comp] = 1.0
                for k, slot in enumerate(cols):
                    if slot is not None and slot[2] - layer in (0, 1):
                        keep[slot[2] - layer, m, k] = 1.0
    return pick_row, pick_col, keep


PICK_ROW, PICK_COL, KEEP = selectors()


def step_size(count_ref):
    count = jnp.full((8, COLS), count_ref[0], jnp.int32).astype(F32)
    return COARSE / count


def lane_up(x):
    return pltpu.roll(x, COLS - 1, 1)


def lane_down(x):
    return pltpu.roll(x, 1, 1)


def pack_body(parity_ref, u, v, ext, mass, scale, x_out, d_out):
    odd = parity_ref[0] == 1
    for q in range(6):
        x_out[q] = u[q]
        d_out[q] = u[q]
    for p in range(2):
        x_out[6 + p] = scale[p]
        d_out[6 + p] = scale[p]
    for c in range(3):
        for base, src in ((8, v), (11, ext)):
            lo, hi = src[2 * c], src[2 * c + 1]
            x_out[base + c] = jnp.where(odd, hi, lo)
            d_out[base + c] = jnp.where(odd, lo, hi)
    x_out[14] = jnp.where(odd, mass[1], mass[0])
    d_out[14] = jnp.where(odd, mass[0], mass[1])


def every(i, stride):
    return pl.ds(i, ROWS, stride=stride)


def prep_body(count_ref, v, ext, mass, kmat, pick_row, pick_col, keep, w_out, e_out, m_out, a_out):
    dt = step_size(count_ref)[0:1]
    for p in range(2):
        inv = (dt * dt) / mass[p]
        for c in range(3):
            q = 2 * c + p
            w_out[every(q, 8), :] = dt * v[q]
            e_out[every(q, 8), :] = inv * ext[q]
            m_out[every(q, 8), :] = inv
    zero = jnp.zeros((ROWS, COLS), F32)
    for q in (6, 7):
        w_out[every(q, 8), :] = zero
        e_out[every(q, 8), :] = zero
        m_out[every(q, 8), :] = zero
    high = lax.Precision.HIGHEST
    rows = jnp.dot(pick_row[...], kmat[...], precision=high, preferred_element_type=F32)
    full = keep[0] * jnp.dot(rows, pick_col[0], precision=high, preferred_element_type=F32)
    full = full + keep[1] * jnp.dot(rows, pick_col[1], precision=high, preferred_element_type=F32)
    big = full.astype(jnp.bfloat16).astype(F32)
    slot = lax.broadcasted_iota(jnp.int32, (128, 256), 1)
    a_out[...] = jnp.where(slot < 2 * WROW, big, full - big)


def build(wk, i, arr):
    lo = arr - arr.astype(jnp.bfloat16).astype(F32)
    for kind, val in enumerate((arr, lane_up(arr), lo, lane_up(lo))):
        wk[every(kind * SLOTS + i, WROW), :] = val


def one_step(wk, a_ref, tiles, s0, s1, act, e, m, w_in, u_in, w_out, u_out):
    nt = len(tiles)
    lhs = a_ref[0 : 64 * nt, :]
    wk[ROWS * WROW : (ROWS + 1) * WROW, :] = wk[0:WROW, :]

    def finish(t, r, force):
        at = slice(8 * r, 8 * r + 8)
        w = w_in[t][at, :] + act * (e[t][at, :] - m[t][at, :] * force)
        if w_out[t] is not None:
            w_out[t][at, :] = w
        u_out[t][at, :] = u_in[t][at, :] + act * w

    carry = {}
    first = {}
    for i in range(ROWS // 2):
        sides = []
        for r in (i, i + ROWS // 2):
            base = r * WROW
            sides.append(
                jnp.concatenate(
                    [
                        wk[base : base + 2 * WROW, :],
                        wk[base : base + DUP, :],
                        wk[base + WROW : base + WROW + DUP, :],
                    ],
                    0,
                )
            )
        out = jnp.dot(lhs, jnp.concatenate(sides, 1), preferred_element_type=F32)
        for h in range(2):
            r = i + h * (ROWS // 2)
            at = slice(8 * r, 8 * r + 8)
            for n, t in enumerate(tiles):
                lower, upper = s0[t][at, :], s1[t][at, :]

                def block(g):
                    j = 64 * n + 8 * g
                    return out[j : j + 8, h * COLS : (h + 1) * COLS]

                part = []
                for b in range(2):
                    g0 = lower * block(2 * b) + upper * block(4 + 2 * b)
                    g1 = lower * block(2 * b + 1) + upper * block(5 + 2 * b)
                    part.append(g0 + lane_down(g1))
                if i == 0:
                    first[h, t] = part[0]
                else:
                    finish(t, r, part[0] + carry[h, t])
                carry[h, t] = part[1]
    for t in tiles:
        finish(t, 0, first[0, t] + carry[1, t])
        finish(t, ROWS // 2, first[1, t] + carry[0, t])


def two_steps(rnd, count_ref, u_nat, lower, upper, refs):
    wk, a_ref, s0, s1, e, m, w_in, w_tmp, u_cur, w_halo, u_mid, w_out, u_new, u_out, u_prev = refs
    act = [jnp.where(count_ref[0] > 2 * rnd + k, 1.0, 0.0).astype(F32) for k in range(2)]
    for c in range(3):
        for p in range(2):
            own = u_nat[2 * c + p]
            build(wk, (p + 2) * 3 + c, own)
            u_cur[0][every(2 * c + p, 8), :] = own
            low = lower(2 * c + p)
            build(wk, p * 3 + c, low)
            top = upper(2 * c + p)
            build(wk, (p + 4) * 3 + c, top)
            if p == 1:
                u_cur[1][every(2 * c, 8), :] = low
            else:
                u_cur[1][every(2 * c + 1, 8), :] = top
    if rnd > 0:
        for r in range(ROWS):
            at = slice(8 * r, 8 * r + 8)
            w_halo[at, :] = u_cur[1][at, :] - u_prev[at, :]
    one_step(wk, a_ref, (0, 1), s0, s1, act[0], e, m, (w_in, w_halo), u_cur, (w_tmp, None), u_mid)
    for c in range(3):
        for p in range(2):
            build(wk, (p + 2) * 3 + c, u_mid[0][every(2 * c + p, 8), :])
            build(wk, (1 if p == 0 else 4) * 3 + c, u_mid[1][every(2 * c + p, 8), :])
    one_step(wk, a_ref, (0,), s0, s1, act[1], e, m, (w_tmp,), (u_mid[0],), (w_out,), (u_new,))
    for q in range(6):
        u_out[q] = u_new[every(q, 8), :]


def first_body(
    count_ref, parity_ref, u_nat, scale, x_in, d_in, w_in, e_own, m_own, a_ref,
    u_out, w_out, u_keep, s_out, eh_out, mh_out,
    wk, w_tmp, u_cur, w_halo, u_mid, u_new,
):
    odd = parity_ref[0] == 1
    dt = step_size(count_ref)[0:1]

    def lower(k):
        return jnp.where(odd, d_in[k], x_in[k])

    def upper(k):
        return jnp.where(odd, x_in[k], d_in[k])

    layers = {-2: lower(6), -1: lower(7), 0: scale[0], 1: scale[1], 2: upper(6)}
    zero = jnp.zeros((ROWS, COLS), F32)
    for q in (6, 7):
        for ref in (s_out.at[0], s_out.at[1], s_out.at[2], s_out.at[3], eh_out, mh_out, w_halo, u_cur.at[0], u_cur.at[1]):
            ref[every(q, 8), :] = zero
    for c in range(3):
        for x in range(2):
            q = 2 * c + x
            outer = -1 if x == 0 else 2
            s_out.at[0][every(q, 8), :] = layers[x]
            s_out.at[1][every(q, 8), :] = layers[x - 1]
            s_out.at[2][every(q, 8), :] = layers[outer]
            s_out.at[3][every(q, 8), :] = layers[outer - 1]
            get = lower if x == 0 else upper
            weight = get(14)
            inv = jnp.where(weight > 0.0, (dt * dt) / jnp.where(weight > 0.0, weight, 1.0), 0.0)
            mh_out[every(q, 8), :] = inv
            eh_out[every(q, 8), :] = inv * get(11 + c)
            w_halo[every(q, 8), :] = dt * get(8 + c)
    s0 = (s_out.at[0], s_out.at[2])
    s1 = (s_out.at[1], s_out.at[3])
    refs = (
        wk, a_ref, s0, s1, (e_own, eh_out), (m_own, mh_out), w_in, w_tmp,
        (u_cur.at[0], u_cur.at[1]), w_halo, (u_mid, u_keep), w_out, u_new, u_out, None,
    )
    two_steps(0, count_ref, u_nat, lower, upper, refs)


def next_body(
    rnd,
    count_ref, parity_ref, u_nat, x_in, d_in, w_in, u_prev, s_in, e_own, eh, m_own, mh, a_ref,
    u_out, w_out, u_keep,
    wk, w_tmp, u_cur, w_halo, u_mid, u_new,
):
    odd = parity_ref[0] == 1

    def lower(k):
        return jnp.where(odd, d_in[k], x_in[k])

    def upper(k):
        return jnp.where(odd, x_in[k], d_in[k])

    zero = jnp.zeros((ROWS, COLS), F32)
    for q in (6, 7):
        for ref in (u_cur.at[0], u_cur.at[1]):
            ref[every(q, 8), :] = zero
    s0 = (s_in.at[0], s_in.at[2])
    s1 = (s_in.at[1], s_in.at[3])
    refs = (
        wk, a_ref, s0, s1, (e_own, eh), (m_own, mh), w_in, w_tmp,
        (u_cur.at[0], u_cur.at[1]), w_halo, (u_mid, u_keep), w_out, u_new, u_out, u_prev,
    )
    two_steps(rnd, count_ref, u_nat, lower, upper, refs)


def node_of(index):
    plane = index // (ROWS * COLS)
    row = (index // COLS) % ROWS
    return plane, row, index % COLS


def node_weights(plane, col, normal, j):
    sub = lax.broadcasted_iota(jnp.int32, (8, COLS), 0)
    lane = lax.broadcasted_iota(jnp.int32, (8, COLS), 1)
    weight = jnp.zeros((8, COLS), F32)
    for c in range(3):
        hit = (sub == 2 * c + plane) & (lane == col)
        weight = jnp.where(hit, normal[c, j], weight)
    return weight


def gap_body(count_ref, slice_ref, own, peer, normal, before, w_in, g_out, hits):
    dt = step_size(count_ref)
    eighth = slice_ref[0] % 8
    for side, nodes, vec, sign in ((0, own, normal, 1.0), (1, peer, before, -1.0)):
        for j in range(16):
            plane, row, col = node_of(nodes[j])
            tile = w_in[pl.ds(pl.multiple_of(row * 8, 8), 8), :]
            hits[side * 16 + j] = tile * node_weights(plane, col, vec, j)
        total = jnp.sum(hits[side * 16 : side * 16 + 16], axis=1)
        total = jnp.sum(total, axis=1, keepdims=True) * (sign / dt[0:1, 0:1])
        lane = lax.broadcasted_iota(jnp.int32, (16, COLS), 1)
        sub = lax.broadcasted_iota(jnp.int32, (16, COLS), 0)
        line = jnp.where(lane == sub + 16 * eighth, jnp.broadcast_to(total, (16, COLS)), 0.0)
        line = jnp.sum(line, axis=0, keepdims=True)
        g_out[:, side * COLS : (side + 1) * COLS] = jnp.broadcast_to(line, (128, COLS))


def final_body(
    count_ref, own, peer, normal, before, gathered, inv_own, inv_before, w_in, m_own, u_dummy,
    v_out, work, mult,
):
    dt = step_size(count_ref)
    mine = jnp.sum(gathered[:, 0:COLS].reshape(16, 8, COLS), axis=1)
    other = jnp.sum(gathered[:, COLS : 2 * COLS].reshape(16, 8, COLS), axis=1)
    gap = mine + jnp.concatenate([other[4:16], other[0:4]], 0)
    for side, rows in ((0, inv_own), (1, inv_before)):
        acc = jnp.zeros((16, COLS), F32)
        for k in range(16):
            acc = acc + rows[:, k * COLS : (k + 1) * COLS] * gap[k : k + 1, :]
        lam = jnp.sum(acc, axis=1, keepdims=True)
        mult[side * 16 : side * 16 + 16, :] = jnp.broadcast_to(lam, (16, COLS))
    work[...] = w_in[...]
    for side, nodes, vec, sign in ((0, own, normal, -1.0), (1, peer, before, 1.0)):
        for j in range(16):
            plane, row, col = node_of(nodes[j])
            at = pl.ds(pl.multiple_of(row * 8, 8), 8)
            k = side * 16 + j
            scaled = mult[k : k + 1, :] * (sign / dt[0:1])
            work[at, :] = work[at, :] + node_weights(plane, col, vec, j) * m_own[at, :] * scaled
    back = 1.0 / dt[0:1]
    for q in range(6):
        v_out[q] = work[every(q, 8), :] * back


def call(body, outs, scratch, ins, limit=24 * 1024 * 1024):
    return pl.pallas_call(
        body,
        out_shape=[jax.ShapeDtypeStruct(s, F32) for s in outs],
        in_specs=ins,
        out_specs=[VM] * len(outs),
        scratch_shapes=[pltpu.VMEM(s, F32) for s in scratch],
        compiler_params=pltpu.CompilerParams(vmem_limit_bytes=limit),
    )


TILE = (ROWS * 8, COLS)
PLANES = (6, ROWS, COLS)
WORK = [((ROWS + 1) * WROW, COLS), TILE, (2,) + TILE, TILE, TILE, TILE]
ACROSS = [(i, i + 1) for i in range(1, 31, 2)] + [(i + 1, i) for i in range(1, 31, 2)]
WITHIN = [(i, i ^ 1) for i in range(32)]
FROM_BEFORE = [(i, (i + 1) % 4) for i in range(4)]


def on_device(
    displacement, velocity, external, mass, elem_scale, stiffness, substeps,
    own_nodes, peer_nodes, normals, schur_inverse,
):
    field = displacement[0].reshape(PLANES)
    speed = velocity[0].reshape(PLANES)
    loads = external[0].reshape(PLANES)
    weight = mass[0]
    scale = elem_scale[0]
    place = lax.axis_index("dom").reshape(1)
    parity = place % 2
    own = own_nodes[0]
    peer = peer_nodes[0]
    normal = normals[0]

    def exchange(x, d):
        return lax.ppermute(x, "dom", ACROSS), lax.ppermute(d, "dom", WITHIN)

    msg = (15, ROWS, COLS)
    x, d = call(pack_body, [msg, msg], [], [SM] + [VM] * 5)(parity, field, speed, loads, weight, scale)
    x, d = exchange(x, d)
    inv_before = lax.ppermute(schur_inverse, "grp", FROM_BEFORE)
    before = lax.ppermute(normal, "grp", FROM_BEFORE)
    w, e_own, m_own, a = call(
        prep_body, [TILE, TILE, TILE, (128, 256)], [], [SM] + [VM] * 7
    )(substeps, speed, loads, weight, stiffness[0], PICK_ROW, PICK_COL, KEEP)
    u, w, kept, s, eh, mh = call(
        first_body, [PLANES, TILE, TILE, (4,) + TILE, TILE, TILE], WORK, [SM] * 2 + [VM] * 8
    )(substeps, parity, field, scale, x, d, w, e_own, m_own, a)
    for rnd in range(1, MAXSUB // 2):
        x, d = exchange(u, u)

        def body(*refs, rnd=rnd):
            return next_body(rnd, *refs)

        u, w, kept = call(body, [PLANES, TILE, TILE], WORK, [SM] * 2 + [VM] * 11)(
            substeps, parity, u, x, d, w, kept, s, e_own, eh, m_own, mh, a
        )
    (gap,) = call(gap_body, [(128, 2 * COLS)], [(32, 8, COLS)], [SM] * 6 + [VM])(
        substeps, place, own, peer, normal, before, w
    )
    gathered = lax.all_to_all(gap, ("grp", "dom"), 0, 0, tiled=True)
    (v,) = call(
        final_body, [PLANES], [TILE, (32, COLS)], [SM] * 5 + [VM] * 6
    )(substeps, own, peer, normal, before, gathered, schur_inverse, inv_before, w, m_own, m_own)
    shape = displacement.shape
    return u.reshape(shape), v.reshape(shape)


def solution(mesh):
    return jax.shard_map(
        on_device,
        mesh=mesh,
        in_specs=(
            P("grp", None, "dom", None, None),
            P("grp", None, "dom", None, None),
            P("grp", None, "dom", None, None),
            P("grp", "dom", None, None),
            P("grp", "dom", None, None),
            P("grp", None, None),
            P("grp"),
            P("grp", "dom"),
            P("grp", "dom"),
            P("grp", None, "dom"),
            P(("grp", "dom"), None),
        ),
        out_specs=(P("grp", None, "dom", None, None), P("grp", None, "dom", None, None)),
        check_vma=False,
    )
```

time: 313 us -> 91.5 us (0.29)
  other arithmetic: 68.5 us -> 0 us
  local copies, waits for them, and re-layouts: 67.2 us -> 10.9 us
  blocking collectives: 81.5 us -> 27.9 us
  starting transfers between devices: 42.1 us -> 18.7 us
  Pallas kernels: 0 us -> 20.1 us
  matrix products: 17.8 us -> 0 us
  waiting for transfers between devices: 25.9 us -> 11.7 us
  loops' own time: 7.77 us -> 0 us
    unnamed x1 -> x0, blocking collectives: 81.5 us -> none
    while x40 -> x0, other arithmetic: 32.4 us -> none
    all_to_all x0 -> x1, blocking collectives: none -> 27.9 us  [on_device(): gathered = lax.all_to_all(gap, ('grp', 'dom'), 0, 0, tiled=True)]
    while x161 -> x0, local copies, waits for them, and re-layouts: 24.4 us -> none
    ppermute x18 -> x10, starting transfers between devices: 42.1 us -> 18.7 us  [the longest x8 16.2 us: exchange(): return (lax.ppermute(x, 'dom', ACROSS), lax.ppermute(d, 'dom', WITHIN))]
    pallas_call x0 -> x8, Pallas kernels: none -> 20.1 us  [the longest x3 12 us: on_device(): call(body, [PLANES, TILE, TILE], WORK, [SM] * 2 + [VM] * 11)]
    scatter-add x2 -> x0, other arithmetic: 19.4 us -> none  [the longest x1 9.72 us: on_device(): flat_speed = flat_speed.at[:, peer].add(incoming / masses[peer][None, :])]
    dot_general x9 -> x0, matrix products: 17.8 us -> none  [the longest x8 17.6 us: element_forces(): jnp.dot(kmat, stacked, precision=lax.Precision.HIGHEST, preferred_element...]
  transfers between devices with their start and end apart: 18 -> 10, of which waited for: 16 -> 4; matrix products, arithmetic and copies ran while one was open for 14% -> 0% of each run, Pallas kernels for 0% -> 7%
where the time goes in v1:
time: 91.5 us; the launch traced here: 90.8 us
  blocking collectives  27.9 us (30%)
  Pallas kernels  20.1 us (22%)
  starting transfers between devices  18.7 us (20%)
  waiting for transfers between devices  11.7 us (13%)
  local copies, waits for them, and re-layouts  10.9 us (12%)
  between operations  1.45 us (2%)
    all_to_all x1, blocking collectives, on_device(): gathered = lax.all_to_all(gap, ('grp', 'dom'), 0, 0, tiled=True)  27.9 us
    ppermute x8, starting transfers between devices, exchange(): return (lax.ppermute(x, 'dom', ACROSS), lax.ppermute(d, 'dom', WITHIN))  16.2 us
    pallas_call x3, Pallas kernels, on_device(): call(body, [PLANES, TILE, TILE], WORK, [SM] * 2 + [VM] * 11)  12 us
    ppermute x8, waiting for transfers between devices, exchange(): return (lax.ppermute(x, 'dom', ACROSS), lax.ppermute(d, 'dom', WITHIN))  11.7 us
    unnamed x38, local copies, waits for them, and re-layouts  10.8 us
    pallas_call x1, Pallas kernels, on_device(): call(first_body, [PLANES, TILE, TILE, (4,) + TILE, TILE, TILE], WORK, [SM...  4.2 us
    pallas_call x1, Pallas kernels, on_device(): call(final_body, [PLANES], [TILE, (32, COLS)], [SM] * 5 + [VM] * 6)  1.86 us
  transfers between devices with their start and end apart: 10, of which 4 were waited for; matrix products, arithmetic and copies ran while one was open for 0% of the time, Pallas kernels for 7%

profile of v1, /device:TPU:1, one launch (start us, length us, event | category | flops | bytes accessed | tf_op | source)
XLA Modules:
  0.0 90.8 jit_solution(5649131043692856133)
XLA Ops:
  0.7 1.0 %copy-done = f32[1,3,2,96,128]{4,3,2,1,0:T(8,128)S(1)} copy-done((f32[1,3,2,96,128]{4,3,2,1,0:T(8,128)S(1)}, f32[1,3,2,96,128]{4,3,2,1,0:T(8,128)}, u32[]{:S(2)}) %copy-start) | copy-done | bytes 294936
  1.6 1.0 %copy-done.2 = f32[1,3,2,96,128]{4,3,2,1,0:T(8,128)S(1)} copy-done((f32[1,3,2,96,128]{4,3,2,1,0:T(8,128)S(1)}, f32[1,3,2,96,128]{4,3,2,1,0:T(8,128)}, u32[]{:S(2)}) %copy-start.2) | copy-done | bytes 294936
  2.6 1.0 %copy-done.4 = f32[1,3,2,96,128]{4,3,2,1,0:T(8,128)S(1)} copy-done((f32[1,3,2,96,128]{4,3,2,1,0:T(8,128)S(1)}, f32[1,3,2,96,128]{4,3,2,1,0:T(8,128)}, u32[]{:S(2)}) %copy-start.4) | copy-done | bytes 294936
  3.5 0.9 copy-done.6
  4.4 0.9 copy-done.8
  5.4 4.7 %collective-permute-start = (f32[15,96,128]{2,1,0:T(8,128)S(1)}, f32[15,96,128]{2,1,0:T(8,128)S(1)}, u32[]{:S(2)}, u32[]{:S(2)}) collective-permute-start(f32[15,96,128]{2,1,0:T(8,128)S(1)} %get-tuple-element.22), channel_id=1, source_target_pairs={{1,2},{3,4},{5,6},{7,8},{9,10},{11,12},{13,14},{15,16},{17,18},{19... | collective-permute-start | bytes 2211848 | tf_op jit(solution)/shard_map/ppermute | solution.py:367
  10.9 1.0 %copy-done.3 = f32[1,3,2,96,128]{4,3,2,1,0:T(8,128)S(1)} copy-done((f32[1,3,2,96,128]{4,3,2,1,0:T(8,128)S(1)}, f32[1,3,2,96,128]{4,3,2,1,0:T(8,128)}, u32[]{:S(2)}) %copy-start.3) | copy-done | bytes 294936
  11.8 1.0 %copy-done.5 = f32[1,3,2,96,128]{4,3,2,1,0:T(8,128)S(1)} copy-done((f32[1,3,2,96,128]{4,3,2,1,0:T(8,128)S(1)}, f32[1,3,2,96,128]{4,3,2,1,0:T(8,128)}, u32[]{:S(2)}) %copy-start.5) | copy-done | bytes 294936
  12.8 0.9 copy-done.9
  13.7 0.9 %copy-done.10 = f32[2,128,256]{2,1,0:T(8,128)S(1)} copy-done((f32[2,128,256]{2,1,0:T(8,128)S(1)}, f32[2,128,256]{2,1,0:T(8,128)}, u32[]{:S(2)}) %copy-start.10) | copy-done | bytes 262168
  14.7 0.8 copy-done.12
  15.5 0.8 copy-done.13
  16.3 0.7 copy-done.14
  17.0 0.7 shard_map.150
  17.8 1.5 %collective-permute-done.x_in = f32[15,96,128]{2,1,0:T(8,128)S(1)} collective-permute-done((f32[15,96,128]{2,1,0:T(8,128)S(1)}, f32[15,96,128]{2,1,0:T(8,128)S(1)}, u32[]{:S(2)}, u32[]{:S(2)}) %collective-permute-start) | collective-permute-done | bytes 737312 | tf_op jit(solution)/shard_map/ppermute | solution.py:367
  19.3 4.2 %shard_map.151 = (f32[6,96,128]{2,1,0:T(8,128)S(1)}, f32[768,128]{1,0:T(8,128)S(1)}, f32[768,128]{1,0:T(8,128)S(1)}, f32[4,768,128]{2,1,0:T(8,128)S(1)}, f32[768,128]{1,0:T(8,128)S(1)}, /*index=5*/f32[768,128]{1,0:T(8,128)S(1)}) custom-call(s32[1]{0:T(128)S(6)} %copy.23.count_ref.refs_0_, s32[1]{0:T(128)S(6)} %select_n.7.parity_ref.refs_1_, ...), custom_call_target="tpu_custom_call" | custom-call | tf_op jit(solution)/shard_map/pallas_call | solution.py:377
  23.5 3.6 %collective-permute-start.2 = (f32[6,96,128]{2,1,0:T(8,128)S(1)}, f32[6,96,128]{2,1,0:T(8,128)S(1)}, u32[]{:S(2)}, u32[]{:S(2)}) collective-permute-start(f32[6,96,128]{2,1,0:T(8,128)S(1)} %get-tuple-element.28.refs_2_), channel_id=1, source_target_pairs={{1,2},{3,4},{5,6},{7,8},{9,10},{11,12},{13,14},{15,16},{17,18},{19... | collective-permute-start | bytes 884744 | tf_op jit(solution)/shard_map/ppermute | solution.py:367
  27.2 4.3 %collective-permute-done.2.refs_3_ = f32[6,96,128]{2,1,0:T(8,128)S(1)} collective-permute-done((f32[6,96,128]{2,1,0:T(8,128)S(1)}, f32[6,96,128]{2,1,0:T(8,128)S(1)}, u32[]{:S(2)}, u32[]{:S(2)}) %collective-permute-start.2) | collective-permute-done | bytes 294944 | tf_op jit(solution)/shard_map/ppermute | solution.py:367
  31.5 3.8 %shard_map.152 = (f32[6,96,128]{2,1,0:T(8,128)S(1)}, f32[768,128]{1,0:T(8,128)S(1)}, f32[768,128]{1,0:T(8,128)S(1)}) custom-call(s32[1]{0:T(128)S(6)} %copy.23.count_ref.refs_0_, s32[1]{0:T(128)S(6)} %select_n.7.parity_ref.refs_1_, f32[6,96,128]{2,1,0:T(8,128)S(1)} %get-tuple-element.28.refs_2_, f32[6,96,128]{2,1,0:T(8,128)S(1)} %collective-permute-done.2.refs_3_, ...), custom_call_target="tpu_custom_call" | custom-call | tf_op jit(solution)/shard_map/pallas_call | solution.py:386
  35.3 3.6 %collective-permute-start.4 = (f32[6,96,128]{2,1,0:T(8,128)S(1)}, f32[6,96,128]{2,1,0:T(8,128)S(1)}, u32[]{:S(2)}, u32[]{:S(2)}) collective-permute-start(f32[6,96,128]{2,1,0:T(8,128)S(1)} %get-tuple-element.34.refs_2_), channel_id=1, source_target_pairs={{1,2},{3,4},{5,6},{7,8},{9,10},{11,12},{13,14},{15,16},{17,18},{19... | collective-permute-start | bytes 884744 | tf_op jit(solution)/shard_map/ppermute | solution.py:367
  39.0 0.3 collective-permute-start.5
  39.2 4.1 %collective-permute-done.4.refs_3_ = f32[6,96,128]{2,1,0:T(8,128)S(1)} collective-permute-done((f32[6,96,128]{2,1,0:T(8,128)S(1)}, f32[6,96,128]{2,1,0:T(8,128)S(1)}, u32[]{:S(2)}, u32[]{:S(2)}) %collective-permute-start.4) | collective-permute-done | bytes 294944 | tf_op jit(solution)/shard_map/ppermute | solution.py:367
  43.4 3.8 %shard_map.153 = (f32[6,96,128]{2,1,0:T(8,128)S(1)}, f32[768,128]{1,0:T(8,128)S(1)}, f32[768,128]{1,0:T(8,128)S(1)}) custom-call(s32[1]{0:T(128)S(6)} %copy.23.count_ref.refs_0_, s32[1]{0:T(128)S(6)} %select_n.7.parity_ref.refs_1_, f32[6,96,128]{2,1,0:T(8,128)S(1)} %get-tuple-element.34.refs_2_, f32[6,96,128]{2,1,0:T(8,128)S(1)} %collective-permute-done.4.refs_3_, ...), custom_call_target="tpu_custom_call" | custom-call | tf_op jit(solution)/shard_map/pallas_call | solution.py:386
  47.1 3.6 %collective-permute-start.6 = (f32[6,96,128]{2,1,0:T(8,128)S(1)}, f32[6,96,128]{2,1,0:T(8,128)S(1)}, u32[]{:S(2)}, u32[]{:S(2)}) collective-permute-start(f32[6,96,128]{2,1,0:T(8,128)S(1)} %get-tuple-element.37.refs_2_), channel_id=1, source_target_pairs={{1,2},{3,4},{5,6},{7,8},{9,10},{11,12},{13,14},{15,16},{17,18},{19... | collective-permute-start | bytes 884744 | tf_op jit(solution)/shard_map/ppermute | solution.py:367
  50.9 1.3 %collective-permute-start.9 = (f32[16,2048]{1,0:T(8,128)S(1)}, f32[16,2048]{1,0:T(8,128)S(1)}, u32[]{:S(2)}, u32[]{:S(2)}) collective-permute-start(f32[16,2048]{1,0:T(8,128)S(1)} %copy-done.11), channel_id=1, source_target_pairs={{0,32},{32,64},{64,96},{96,0},{1,33},{33,65},{65,97},{97,1},{2,34}... | collective-permute-start | bytes 393224 | tf_op jit(solution)/shard_map/ppermute | solution.py:372
  52.2 1.2 %collective-permute-start.8 = (f32[3,16]{1,0:T(4,128)S(1)}, f32[3,16]{1,0:T(4,128)S(1)}, u32[]{:S(2)}, u32[]{:S(2)}) collective-permute-start(f32[3,16]{1,0:T(4,128)S(1)} %bitcast.30), channel_id=1, source_target_pairs={{0,32},{32,64},{64,96},{96,0},{1,33},{33,65},{65,97},{97,1},{2,34}... | collective-permute-start | bytes 584 | tf_op jit(solution)/shard_map/ppermute | solution.py:373
  53.4 1.8 %collective-permute-done.6.refs_3_ = f32[6,96,128]{2,1,0:T(8,128)S(1)} collective-permute-done((f32[6,96,128]{2,1,0:T(8,128)S(1)}, f32[6,96,128]{2,1,0:T(8,128)S(1)}, u32[]{:S(2)}, u32[]{:S(2)}) %collective-permute-start.6) | collective-permute-done | bytes 294944 | tf_op jit(solution)/shard_map/ppermute | solution.py:367
  55.2 4.5 %shard_map.154 = (f32[6,96,128]{2,1,0:T(8,128)}, f32[768,128]{1,0:T(8,128)S(1)}, f32[768,128]{1,0:T(8,128)}) custom-call(s32[1]{0:T(128)S(6)} %copy.23.count_ref.refs_0_, s32[1]{0:T(128)S(6)} %select_n.7.parity_ref.refs_1_, f32[6,96,128]{2,1,0:T(8,128)S(1)} %get-tuple-element.37.refs_2_, f32[6,96,128]{2,1,0:T(8,128)S(1)} %collective-permute-done.6.refs_3_, ...), custom_call_target="tpu_custom_call" | custom-call | tf_op jit(solution)/shard_map/pallas_call | solution.py:386
  59.7 1.1 %shard_map.155 = f32[128,256]{1,0:T(8,128)S(1)} custom-call(s32[1]{0:T(128)S(6)} %copy.23.count_ref.refs_0_, s32[1]{0:T(128)} %bitcast.slice_ref, s32[16]{0:T(128)S(1)} %bitcast.34, s32[16]{0:T(128)S(1)} %bitcast.36, f32[3,16]{1,0:T(4,128)S(1)} %bitcast.31, f32[3,16]{1,0:T(4,128)S(1)} %collective-permute-done.8.before, f32[768,128]{1,0:T(8,128)S(1)} %get-tuple-element.41.w_in), custom_call_target="tpu_custom_call" | custom-call | tf_op jit(solution)/shard_map/pallas_call | solution.py:389
  60.8 0.1 copy.16
  61.0 27.9 %all_to_all.11 = f32[128,1,256]{2,1,0:T(1,128)S(1)} all-to-all(f32[128,1,256]{2,1,0:T(1,128)S(1)} %copy.16), channel_id=1, replica_groups=mesh['grp'=4,'dom'=32] {'grp','dom'}, dimensions={0} | all-to-all | bytes 262144 | tf_op jit(solution)/shard_map/all_to_all | solution.py:392
  88.9 1.9 %shard_map.156 = f32[6,96,128]{2,1,0:T(8,128)} custom-call(s32[1]{0:T(128)S(6)} %copy.23.count_ref.refs_0_, s32[16]{0:T(128)S(1)} %bitcast.35, s32[16]{0:T(128)S(1)} %bitcast.37, f32[3,16]{1,0:T(4,128)S(1)} %bitcast.32, f32[3,16]{1,0:T(4,128)S(1)} %collective-permute-done.8.before, f32[128,256]{1,0:T(8,128)S(1)} %bitcast.24, f32[16,2048]{1,0:T(8,128)S(1)} %copy-done.11, ...), custom_call_target="tpu_custom_call" | custom-call | tf_op jit(solution)/shard_map/pallas_call | solution.py:393
  (36 shorter events, 0.4 us)
Async XLA Ops:
  0.6 1.0 %copy-start = (f32[1,3,2,96,128]{4,3,2,1,0:T(8,128)S(1)}, f32[1,3,2,96,128]{4,3,2,1,0:T(8,128)}, u32[]{:S(2)}) copy-start(f32[1,3,2,96,128]{4,3,2,1,0:T(8,128)} %param.14) | copy-start | bytes 884740
  1.6 1.0 %copy-start.2 = (f32[1,3,2,96,128]{4,3,2,1,0:T(8,128)S(1)}, f32[1,3,2,96,128]{4,3,2,1,0:T(8,128)}, u32[]{:S(2)}) copy-start(f32[1,3,2,96,128]{4,3,2,1,0:T(8,128)} %param.15) | copy-start | bytes 884740
  2.6 1.0 %copy-start.4 = (f32[1,3,2,96,128]{4,3,2,1,0:T(8,128)S(1)}, f32[1,3,2,96,128]{4,3,2,1,0:T(8,128)}, u32[]{:S(2)}) copy-start(f32[1,3,2,96,128]{4,3,2,1,0:T(8,128)} %param.16) | copy-start | bytes 884740
  3.5 0.9 copy-start.6
  4.4 0.9 copy-start.8
  5.3 14.0 %copy-start.1 = (f32[1,3,2,96,128]{4,3,2,1,0:T(8,128)S(1)}, f32[1,3,2,96,128]{4,3,2,1,0:T(8,128)}, u32[]{:S(2)}) copy-start(f32[1,3,2,96,128]{4,3,2,1,0:T(8,128)} %param.14) | copy-start | bytes 884740
  5.3 14.0 %copy-start.7 = (f32[1,2,96,128]{3,2,1,0:T(8,128)S(1)}, f32[1,2,96,128]{3,2,1,0:T(8,128)}, u32[]{:S(2)}) copy-start(f32[1,2,96,128]{3,2,1,0:T(8,128)} %param.18) | copy-start | bytes 294916
  5.4 13.9 %collective-permute-start = (f32[15,96,128]{2,1,0:T(8,128)S(1)}, f32[15,96,128]{2,1,0:T(8,128)S(1)}, u32[]{:S(2)}, u32[]{:S(2)}) collective-permute-start(f32[15,96,128]{2,1,0:T(8,128)S(1)} %get-tuple-element.22), channel_id=1, source_target_pairs={{1,2},{3,4},{5,6},{7,8},{9,10},{11,12},{13,14},{15,16},{17,18},{19... | collective-permute-start | bytes 2211848 | tf_op jit(solution)/shard_map/ppermute | solution.py:367
  10.1 9.1 %collective-permute-start.1 = (f32[15,96,128]{2,1,0:T(8,128)S(1)}, f32[15,96,128]{2,1,0:T(8,128)S(1)}, u32[]{:S(2)}, u32[]{:S(2)}) collective-permute-start(f32[15,96,128]{2,1,0:T(8,128)S(1)} %get-tuple-element.23), channel_id=1, source_target_pairs={{0,1},{1,0},{2,3},{3,2},{4,5},{5,4},{6,7},{7,6},{8,9},{9,8},{10,11... | collective-permute-start | bytes 2211848 | tf_op jit(solution)/shard_map/ppermute | solution.py:367
  10.9 1.0 %copy-start.3 = (f32[1,3,2,96,128]{4,3,2,1,0:T(8,128)S(1)}, f32[1,3,2,96,128]{4,3,2,1,0:T(8,128)}, u32[]{:S(2)}) copy-start(f32[1,3,2,96,128]{4,3,2,1,0:T(8,128)} %param.15) | copy-start | bytes 884740
  11.8 1.0 %copy-start.5 = (f32[1,3,2,96,128]{4,3,2,1,0:T(8,128)S(1)}, f32[1,3,2,96,128]{4,3,2,1,0:T(8,128)}, u32[]{:S(2)}) copy-start(f32[1,3,2,96,128]{4,3,2,1,0:T(8,128)} %param.16) | copy-start | bytes 884740
  12.8 0.9 copy-start.9
  13.7 0.9 %copy-start.10 = (f32[2,128,256]{2,1,0:T(8,128)S(1)}, f32[2,128,256]{2,1,0:T(8,128)}, u32[]{:S(2)}) copy-start(f32[2,128,256]{2,1,0:T(8,128)} %constant.31.clone.keep) | copy-start | bytes 786436
  14.7 0.8 copy-start.12
  15.5 0.8 copy-start.13
  16.3 0.7 copy-start.14
  23.5 8.0 %collective-permute-start.2 = (f32[6,96,128]{2,1,0:T(8,128)S(1)}, f32[6,96,128]{2,1,0:T(8,128)S(1)}, u32[]{:S(2)}, u32[]{:S(2)}) collective-permute-start(f32[6,96,128]{2,1,0:T(8,128)S(1)} %get-tuple-element.28.refs_2_), channel_id=1, source_target_pairs={{1,2},{3,4},{5,6},{7,8},{9,10},{11,12},{13,14},{15,16},{17,18},{19... | collective-permute-start | bytes 884744 | tf_op jit(solution)/shard_map/ppermute | solution.py:367
  27.1 4.4 %collective-permute-start.3 = (f32[6,96,128]{2,1,0:T(8,128)S(1)}, f32[6,96,128]{2,1,0:T(8,128)S(1)}, u32[]{:S(2)}, u32[]{:S(2)}) collective-permute-start(f32[6,96,128]{2,1,0:T(8,128)S(1)} %get-tuple-element.28.refs_2_), channel_id=1, source_target_pairs={{0,1},{1,0},{2,3},{3,2},{4,5},{5,4},{6,7},{7,6},{8,9},{9,8},{10,11... | collective-permute-start | bytes 884744 | tf_op jit(solution)/shard_map/ppermute | solution.py:367
  35.3 8.0 %collective-permute-start.4 = (f32[6,96,128]{2,1,0:T(8,128)S(1)}, f32[6,96,128]{2,1,0:T(8,128)S(1)}, u32[]{:S(2)}, u32[]{:S(2)}) collective-permute-start(f32[6,96,128]{2,1,0:T(8,128)S(1)} %get-tuple-element.34.refs_2_), channel_id=1, source_target_pairs={{1,2},{3,4},{5,6},{7,8},{9,10},{11,12},{13,14},{15,16},{17,18},{19... | collective-permute-start | bytes 884744 | tf_op jit(solution)/shard_map/ppermute | solution.py:367
  39.0 4.4 %collective-permute-start.5 = (f32[6,96,128]{2,1,0:T(8,128)S(1)}, f32[6,96,128]{2,1,0:T(8,128)S(1)}, u32[]{:S(2)}, u32[]{:S(2)}) collective-permute-start(f32[6,96,128]{2,1,0:T(8,128)S(1)} %get-tuple-element.34.refs_2_), channel_id=1, source_target_pairs={{0,1},{1,0},{2,3},{3,2},{4,5},{5,4},{6,7},{7,6},{8,9},{9,8},{10,11... | collective-permute-start | bytes 884744 | tf_op jit(solution)/shard_map/ppermute | solution.py:367
  43.4 7.5 %copy-start.11 = (f32[16,2048]{1,0:T(8,128)S(1)}, f32[16,2048]{1,0:T(8,128)}, u32[]{:S(2)}) copy-start(f32[16,2048]{1,0:T(8,128)} %inv_own.1) | copy-start | bytes 393220
  43.4 8.8 %copy-start.17 = (f32[1,3,16]{2,0,1:T(1,128)S(1)}, f32[1,3,16]{2,0,1:T(1,128)}, u32[]{:S(2)}) copy-start(f32[1,3,16]{2,0,1:T(1,128)} %param.23) | copy-start | bytes 580
  47.1 8.0 %collective-permute-start.6 = (f32[6,96,128]{2,1,0:T(8,128)S(1)}, f32[6,96,128]{2,1,0:T(8,128)S(1)}, u32[]{:S(2)}, u32[]{:S(2)}) collective-permute-start(f32[6,96,128]{2,1,0:T(8,128)S(1)} %get-tuple-element.37.refs_2_), channel_id=1, source_target_pairs={{1,2},{3,4},{5,6},{7,8},{9,10},{11,12},{13,14},{15,16},{17,18},{19... | collective-permute-start | bytes 884744 | tf_op jit(solution)/shard_map/ppermute | solution.py:367
  50.8 4.4 %collective-permute-start.7 = (f32[6,96,128]{2,1,0:T(8,128)S(1)}, f32[6,96,128]{2,1,0:T(8,128)S(1)}, u32[]{:S(2)}, u32[]{:S(2)}) collective-permute-start(f32[6,96,128]{2,1,0:T(8,128)S(1)} %get-tuple-element.37.refs_2_), channel_id=1, source_target_pairs={{0,1},{1,0},{2,3},{3,2},{4,5},{5,4},{6,7},{7,6},{8,9},{9,8},{10,11... | collective-permute-start | bytes 884744 | tf_op jit(solution)/shard_map/ppermute | solution.py:367
  50.9 38.0 %collective-permute-start.9 = (f32[16,2048]{1,0:T(8,128)S(1)}, f32[16,2048]{1,0:T(8,128)S(1)}, u32[]{:S(2)}, u32[]{:S(2)}) collective-permute-start(f32[16,2048]{1,0:T(8,128)S(1)} %copy-done.11), channel_id=1, source_target_pairs={{0,32},{32,64},{64,96},{96,0},{1,33},{33,65},{65,97},{97,1},{2,34}... | collective-permute-start | bytes 393224 | tf_op jit(solution)/shard_map/ppermute | solution.py:372
  52.2 7.5 %collective-permute-start.8 = (f32[3,16]{1,0:T(4,128)S(1)}, f32[3,16]{1,0:T(4,128)S(1)}, u32[]{:S(2)}, u32[]{:S(2)}) collective-permute-start(f32[3,16]{1,0:T(4,128)S(1)} %bitcast.30), channel_id=1, source_target_pairs={{0,32},{32,64},{64,96},{96,0},{1,33},{33,65},{65,97},{97,1},{2,34}... | collective-permute-start | bytes 584 | tf_op jit(solution)/shard_map/ppermute | solution.py:373
  55.2 4.5 %copy-start.15 = (s32[1,16]{1,0:T(1,128)S(1)}, s32[1,16]{1,0:T(1,128)}, u32[]{:S(2)}) copy-start(s32[1,16]{1,0:T(1,128)} %param.21) | copy-start | bytes 196
  55.2 4.5 %copy-start.16 = (s32[1,16]{1,0:T(1,128)S(1)}, s32[1,16]{1,0:T(1,128)}, u32[]{:S(2)}) copy-start(s32[1,16]{1,0:T(1,128)} %param.22) | copy-start | bytes 196

commit v2 on v0

v2 whole, which is shorter than its diff:
```python
import jax
import jax.numpy as jnp
import numpy as np
from jax import lax
from jax.experimental import pallas as pl
from jax.experimental.pallas import tpu as pltpu
from jax.sharding import PartitionSpec as P

MAXSUB = 8
ROUNDS = MAXSUB // 2
COARSE = 0.4
ROWS = 96
HALF = ROWS // 2
COLS = 128
WROW = 56
STEP_PARTS = [(0, 48), (WROW, 48), (0, 16), (24, 16), (WROW, 16), (WROW + 24, 16)]
INNER_PARTS = [(0, 24), (WROW, 24), (0, 16), (WROW, 16)]
STEP_K, INNER_K = 256, 128
F32 = jnp.float32
VM = pl.BlockSpec(memory_space=pltpu.VMEM)
SM = pl.BlockSpec(memory_space=pltpu.SMEM)
HBM = pl.BlockSpec(memory_space=pl.ANY)


def describe(parts, width):
    cols = []
    for n, (start, size) in enumerate(parts):
        for at in range(start, start + size):
            b, at = divmod(at, WROW)
            outer, at = divmod(at, 24)
            kind, at = divmod(at, 6)
            x, comp = divmod(at, 3)
            plane = (-1 if x == 0 else 2) if outer else x
            cols.append((b, kind % 2, plane, comp) if n < 2 or kind < 2 else None)
    return cols + [None] * (width - len(cols))


def selectors():
    cols = describe(STEP_PARTS, STEP_K) + describe(INNER_PARTS, INNER_K)
    pick_row = np.zeros((96, 24), np.float32)
    pick_col = np.zeros((2, 24, len(cols)), np.float32)
    keep = np.zeros((2, 96, len(cols)), np.float32)
    for k, slot in enumerate(cols):
        if slot is not None:
            b, e, plane, comp = slot
            for a in (0, 1):
                pick_col[a, (4 * a + 2 * b + e) * 3 + comp, k] = 1.0
    for block in range(3):
        for be in range(4):
            for q in range(6):
                comp, x = divmod(q, 2)
                layer = 0 if block == 0 else (-1 if x == 0 else 1)
                a = 1 - x if block == 1 else x
                m = block * 32 + be * 8 + q
                pick_row[m, (4 * a + be) * 3 + comp] = 1.0
                for k, slot in enumerate(cols):
                    if slot is not None and slot[2] - layer in (0, 1):
                        keep[slot[2] - layer, m, k] = 1.0
    return pick_row, pick_col, keep


PICK_ROW, PICK_COL, KEEP = selectors()


def step_size(count_ref):
    count = jnp.full((8, COLS), count_ref[0], jnp.int32).astype(F32)
    return COARSE / count


def lane_up(x):
    return pltpu.roll(x, COLS - 1, 1)


def lane_down(x):
    return pltpu.roll(x, 1, 1)


def every(i, stride=8):
    return pl.ds(i, ROWS, stride=stride)


def tile(r):
    return slice(8 * r, 8 * r + 8)


def build(wk, outer, i, arr):
    lo = arr - arr.astype(jnp.bfloat16).astype(F32)
    for kind, val in enumerate((arr, lane_up(arr), lo, lane_up(lo))):
        wk[every(outer * 24 + kind * 6 + i, WROW), :] = val


def sweep(wk, lhs, parts, width, blocks, finish):
    wk[ROWS * WROW : (ROWS + 1) * WROW, :] = wk[0:WROW, :]
    pad = jnp.zeros((width - sum(n for _, n in parts), COLS), F32)
    carry = {}
    first = {}
    for i in range(HALF):
        sides = []
        for r in (i, i + HALF):
            base = r * WROW
            pieces = [wk[base + at : base + at + n, :] for at, n in parts]
            sides.append(jnp.concatenate(pieces + [pad], 0))
        out = jnp.dot(lhs, jnp.concatenate(sides, 1), preferred_element_type=F32)
        for h in range(2):
            r = i + h * HALF
            for n, terms in enumerate(blocks):
                part = []
                for b in range(2):
                    g = []
                    for e in range(2):
                        total = None
                        for offset, scale in terms:
                            j = offset + 16 * b + 8 * e
                            term = scale[tile(r), :] * out[j : j + 8, h * COLS : (h + 1) * COLS]
                            total = term if total is None else total + term
                        g.append(total)
                    part.append(g[0] + lane_down(g[1]))
                if i == 0:
                    first[h, n] = part[0]
                else:
                    finish(n, r, part[0] + carry[h, n])
                carry[h, n] = part[1]
    for n in range(len(blocks)):
        finish(n, 0, first[0, n] + carry[1, n])
        finish(n, HALF, first[1, n] + carry[0, n])


def inner_pass(wk, a_ref, si, e, m, u, w, ei_out, h_out):
    def finish(n, r, force):
        at = tile(r)
        rest = e[at, :] - m[at, :] * force
        ei_out[at, :] = rest
        h_out[at, :] = u[at, :] + (w[at, :] + rest)

    sweep(wk, a_ref[0:32, STEP_K:], INNER_PARTS, INNER_K, [[(0, si)]], finish)


def send_edges(odd, u, h, x_msg, d_msg):
    for base, src in ((0, u), (3, h)):
        for c in range(3):
            low, top = src[every(2 * c), :], src[every(2 * c + 1), :]
            x_msg[base + c] = jnp.where(odd, top, low)
            d_msg[base + c] = jnp.where(odd, low, top)


def prep_body(
    count_ref, parity_ref, kmat_h, row_h, col_h, keep_h, u_h, scale_h, v_h, mass_h, ext_h,
    x_msg, d_msg, u_t, w_t, e_t, m_t, ei_t, si_t, a_out,
    kmat, row, col, keep, u_n, scale, v_n, mass, ext_n, wk, h_t, sems,
):
    pairs = [
        (kmat_h, kmat), (row_h, row), (col_h, col), (keep_h, keep), (u_h, u_n),
        (scale_h, scale), (v_h, v_n), (mass_h, mass), (ext_h, ext_n),
    ]
    copies = [pltpu.make_async_copy(a, b, sems.at[n]) for n, (a, b) in enumerate(pairs)]
    for copy in copies:
        copy.start()
    for copy in copies:
        copy.wait()
    odd = parity_ref[0] == 1
    dt = step_size(count_ref)[0:1]
    high = lax.Precision.HIGHEST
    rows = jnp.dot(row[...], kmat[...], precision=high, preferred_element_type=F32)
    full = keep[0] * jnp.dot(rows, col[0], precision=high, preferred_element_type=F32)
    full = full + keep[1] * jnp.dot(rows, col[1], precision=high, preferred_element_type=F32)
    big = full.astype(jnp.bfloat16).astype(F32)
    slot = lax.broadcasted_iota(jnp.int32, full.shape, 1)
    main = (slot < 96) | ((slot >= STEP_K) & (slot < STEP_K + 48))
    a_out[...] = jnp.where(main, big, full - big)
    inv = [(dt * dt) / mass[p] for p in range(2)]
    for c in range(3):
        for p in range(2):
            q = 2 * c + p
            build(wk, 0, 3 * p + c, u_n[q])
            u_t[every(q), :] = u_n[q]
            w_t[every(q), :] = dt * v_n[q]
            e_t[every(q), :] = inv[p] * ext_n[q]
            m_t[every(q), :] = inv[p]
            si_t[every(q), :] = scale[0]
    inner_pass(wk, a_out, si_t, e_t, m_t, u_t, w_t, ei_t, h_t)
    send_edges(odd, u_t, h_t, x_msg, d_msg)
    x_msg[6] = jnp.where(odd, inv[1], inv[0])
    d_msg[6] = jnp.where(odd, inv[0], inv[1])
    x_msg[7] = scale[1]
    d_msg[7] = scale[1]


def round_body(rnd, *refs):
    refs = list(refs)
    take = lambda n: [refs.pop(0) for _ in range(n)]
    count_ref, parity_ref = take(2)
    last = rnd == ROUNDS - 1
    if last:
        place_ref, own, peer, normal, before = take(5)
    x_in, d_in, u_t, w_t, e_t, m_t, ei_t, si_t, a_ref = take(9)
    if rnd == 0:
        (scale,) = take(1)
    else:
        sx_t, mh_t = take(2)
    if last:
        u_out, w2, g_out = take(3)
    else:
        x_msg, d_msg, u2, w2, ei_out = take(5)
    if rnd == 0:
        sx_t, mh_t = take(2)
    wk, uh, hh, u1, u1h, w1, h_t = take(7)
    if last:
        u2, hits = take(2)
    odd = parity_ref[0] == 1

    def lower(k):
        return jnp.where(odd, d_in[k], x_in[k])

    def upper(k):
        return jnp.where(odd, x_in[k], d_in[k])

    act = [jnp.where(count_ref[0] > 2 * rnd + k, 1.0, 0.0).astype(F32) for k in range(2)]
    for c in range(3):
        for p, get in ((0, lower), (1, upper)):
            q = 2 * c + p
            build(wk, 0, 3 * p + c, u_t[every(q), :])
            outer = get(c)
            build(wk, 1, 3 * p + c, outer)
            uh[every(q), :] = outer
            hh[every(q), :] = get(3 + c)
            if rnd == 0:
                mh_t[every(q), :] = get(6)
                sx_t[every(q), :] = scale[1] if p else lower(7)

    def finish_first(n, r, force):
        at = tile(r)
        if n == 0:
            w = w_t[at, :] + act[0] * (ei_t[at, :] - m_t[at, :] * force)
            w1[at, :] = w
            u1[at, :] = u_t[at, :] + act[0] * w
        else:
            before = uh[at, :]
            u1h[at, :] = before + act[0] * ((hh[at, :] - mh_t[at, :] * force) - before)

    sweep(wk, a_ref[32:96, 0:STEP_K], STEP_PARTS, STEP_K, [[(0, sx_t)], [(32, sx_t)]], finish_first)
    for c in range(3):
        for p in range(2):
            build(wk, 0, 3 * p + c, u1[every(2 * c + p), :])
            build(wk, 1, 3 * p + c, u1h[every(2 * c + p), :])

    def finish_second(n, r, force):
        at = tile(r)
        w = w1[at, :] + act[1] * (e_t[at, :] - m_t[at, :] * force)
        w2[at, :] = w
        u2[at, :] = u1[at, :] + act[1] * w

    sweep(wk, a_ref[0:64, 0:STEP_K], STEP_PARTS, STEP_K, [[(0, si_t), (32, sx_t)]], finish_second)
    if last:
        for q in range(6):
            u_out[q] = u2[every(q), :]
        partial_gaps(count_ref, place_ref, own, peer, normal, before, w2, g_out, hits)
        return
    for c in range(3):
        for p in range(2):
            build(wk, 0, 3 * p + c, u2[every(2 * c + p), :])
    inner_pass(wk, a_ref, si_t, e_t, m_t, u2, w2, ei_out, h_t)
    send_edges(odd, u2, h_t, x_msg, d_msg)


def node_of(index):
    plane = index // (ROWS * COLS)
    row = (index // COLS) % ROWS
    return plane, pl.ds(pl.multiple_of(row * 8, 8), 8), index % COLS


def node_hits(plane, col):
    sub = lax.broadcasted_iota(jnp.int32, (8, COLS), 0)
    lane = lax.broadcasted_iota(jnp.int32, (8, COLS), 1)
    return [(sub == 2 * c + plane) & (lane == col) for c in range(3)]


def partial_gaps(count_ref, place_ref, own, peer, normal, before, w_in, g_out, hits):
    dt = step_size(count_ref)
    eighth = place_ref[0] % 8
    for side, nodes, vec, sign in ((0, own, normal, 1.0), (1, peer, before, -1.0)):
        for j in range(16):
            plane, at, col = node_of(nodes[j])
            value = w_in[at, :]
            total = jnp.zeros((8, COLS), F32)
            for c, hit in enumerate(node_hits(plane, col)):
                total = jnp.where(hit, value * vec[c, j], total)
            hits[side * 16 + j] = total
        total = jnp.sum(hits[side * 16 : side * 16 + 16], axis=1)
        total = jnp.sum(total, axis=1, keepdims=True) * (sign / dt[0:1, 0:1])
        lane = lax.broadcasted_iota(jnp.int32, (16, COLS), 1)
        sub = lax.broadcasted_iota(jnp.int32, (16, COLS), 0)
        line = jnp.where(lane == sub + 16 * eighth, jnp.broadcast_to(total, (16, COLS)), 0.0)
        line = jnp.sum(line, axis=0, keepdims=True)
        g_out[:, side * COLS : (side + 1) * COLS] = jnp.broadcast_to(line, (128, COLS))


def final_body(
    count_ref, own, peer, normal, before, gathered, inv_own, inv_before, w_in, m_own,
    v_out, work, mult,
):
    dt = step_size(count_ref)
    mine = jnp.sum(gathered[:, 0:COLS].reshape(16, 8, COLS), axis=1)
    other = jnp.sum(gathered[:, COLS : 2 * COLS].reshape(16, 8, COLS), axis=1)
    gap = mine + jnp.concatenate([other[4:16], other[0:4]], 0)
    for side, rows in ((0, inv_own), (1, inv_before)):
        acc = jnp.zeros((16, COLS), F32)
        for k in range(16):
            acc = acc + rows[:, k * COLS : (k + 1) * COLS] * gap[k : k + 1, :]
        lam = jnp.sum(acc, axis=1, keepdims=True)
        mult[side * 16 : side * 16 + 16, :] = jnp.broadcast_to(lam, (16, COLS))
    work[...] = w_in[...]
    for side, nodes, vec, sign in ((0, own, normal, -1.0), (1, peer, before, 1.0)):
        for j in range(16):
            plane, at, col = node_of(nodes[j])
            k = side * 16 + j
            value = work[at, :]
            change = m_own[at, :] * (mult[k : k + 1, :] * (sign / dt[0:1]))
            for c, hit in enumerate(node_hits(plane, col)):
                value = jnp.where(hit, value + change * vec[c, j], value)
            work[at, :] = value
    back = 1.0 / dt[0:1]
    for q in range(6):
        v_out[q] = work[every(q), :] * back


def call(body, outs, scratch, ins, limit=24 * 1024 * 1024):
    return pl.pallas_call(
        body,
        out_shape=[jax.ShapeDtypeStruct(s, F32) for s in outs],
        in_specs=ins,
        out_specs=[VM] * len(outs),
        scratch_shapes=[pltpu.VMEM(s, F32) if isinstance(s, tuple) else s for s in scratch],
        compiler_params=pltpu.CompilerParams(vmem_limit_bytes=limit),
    )


TILE = (ROWS * 8, COLS)
PLANES = (6, ROWS, COLS)
WORK = ((ROWS + 1) * WROW, COLS)
WIDTH = STEP_K + INNER_K
ACROSS = [(i, i + 1) for i in range(1, 31, 2)] + [(i + 1, i) for i in range(1, 31, 2)]
WITHIN = [(i, i ^ 1) for i in range(32)]
FROM_BEFORE = [(i, (i + 1) % 4) for i in range(4)]


def on_device(
    displacement, velocity, external, mass, elem_scale, stiffness, substeps,
    own_nodes, peer_nodes, normals, schur_inverse,
):
    field = displacement[0].reshape(PLANES)
    speed = velocity[0].reshape(PLANES)
    loads = external[0].reshape(PLANES)
    weight = mass[0]
    scale = elem_scale[0]
    place = lax.axis_index("dom").reshape(1)
    parity = place % 2
    own = own_nodes[0]
    peer = peer_nodes[0]
    normal = normals[0]

    first = (8, ROWS, COLS)
    pair = (2, ROWS, COLS)
    x, d, u, w, e, m, ei, si, a = call(
        prep_body,
        [first, first, TILE, TILE, TILE, TILE, TILE, TILE, (96, WIDTH)],
        [
            (24, 24), (96, 24), (2, 24, WIDTH), (2, 96, WIDTH), PLANES, pair, PLANES, pair, PLANES,
            WORK, TILE, pltpu.SemaphoreType.DMA((9,)),
        ],
        [SM] * 2 + [HBM] * 9,
    )(substeps, parity, stiffness[0], PICK_ROW, PICK_COL, KEEP, field, scale, speed, weight, loads)
    inv_before = before = None
    for rnd in range(ROUNDS):
        x = lax.ppermute(x, "dom", ACROSS)
        d = lax.ppermute(d, "dom", WITHIN)
        if rnd == 0:
            inv_before = lax.ppermute(schur_inverse, "grp", FROM_BEFORE)
            before = lax.ppermute(normal, "grp", FROM_BEFORE)
        last = rnd == ROUNDS - 1
        args = [substeps, parity]
        if last:
            args += [place, own, peer, normal, before]
        scalars = len(args)
        args += [x, d, u, w, e, m, ei, si, a]
        args += [scale] if rnd == 0 else [sx, mh]
        outs = [PLANES, TILE, (128, 2 * COLS)] if last else [PLANES, PLANES, TILE, TILE, TILE]
        outs += [TILE, TILE] if rnd == 0 else []
        scratch = [WORK] + [TILE] * 6 + ([TILE, (32, 8, COLS)] if last else [])

        def body(*refs, rnd=rnd):
            return round_body(rnd, *refs)

        got = call(body, outs, scratch, [SM] * scalars + [VM] * (len(args) - scalars))(*args)
        if last:
            u, w, gap = got
        else:
            x, d, u, w, ei = got[:5]
        if rnd == 0:
            sx, mh = got[5:]
    gathered = lax.all_to_all(gap, ("grp", "dom"), 0, 0, tiled=True)
    (v,) = call(final_body, [PLANES], [TILE, (32, COLS)], [SM] * 5 + [VM] * 5)(
        substeps, own, peer, normal, before, gathered, schur_inverse, inv_before, w, m
    )
    shape = displacement.shape
    return u.reshape(shape), v.reshape(shape)


def solution(mesh):
    return jax.shard_map(
        on_device,
        mesh=mesh,
        in_specs=(
            P("grp", None, "dom", None, None),
            P("grp", None, "dom", None, None),
            P("grp", None, "dom", None, None),
            P("grp", "dom", None, None),
            P("grp", "dom", None, None),
            P("grp", None, None),
            P("grp"),
            P("grp", "dom"),
            P("grp", "dom"),
            P("grp", None, "dom"),
            P(("grp", "dom"), None),
        ),
        out_specs=(P("grp", None, "dom", None, None), P("grp", None, "dom", None, None)),
        check_vma=False,
    )
```

time: 313 us -> 90.3 us (0.29)
  other arithmetic: 68.5 us -> 0 us
  local copies, waits for them, and re-layouts: 67.2 us -> 8.17 us
  blocking collectives: 81.5 us -> 25.9 us
  starting transfers between devices: 42.1 us -> 18.5 us
  Pallas kernels: 0 us -> 18 us
  matrix products: 17.8 us -> 0 us
  waiting for transfers between devices: 25.9 us -> 17.6 us
  loops' own time: 7.77 us -> 0 us
    unnamed x1 -> x0, blocking collectives: 81.5 us -> none
    while x40 -> x0, other arithmetic: 32.4 us -> none
    all_to_all x0 -> x1, blocking collectives: none -> 25.9 us  [on_device(): gathered = lax.all_to_all(gap, ('grp', 'dom'), 0, 0, tiled=True)]
    while x161 -> x0, local copies, waits for them, and re-layouts: 24.4 us -> none
    ppermute x18 -> x10, starting transfers between devices: 42.1 us -> 18.5 us  [the longest x4 15.5 us: on_device(): x = lax.ppermute(x, 'dom', ACROSS)]
    scatter-add x2 -> x0, other arithmetic: 19.4 us -> none  [the longest x1 9.72 us: on_device(): flat_speed = flat_speed.at[:, peer].add(incoming / masses[peer][None, :])]
    pallas_call x0 -> x6, Pallas kernels: none -> 18 us  [the longest x4 14 us: on_device(): call(body, outs, scratch, [SM] * scalars + [VM] * (len(args) - scalars))]
    dot_general x9 -> x0, matrix products: 17.8 us -> none  [the longest x8 17.6 us: element_forces(): jnp.dot(kmat, stacked, precision=lax.Precision.HIGHEST, preferred_element...]
  transfers between devices with their start and end apart: 18 -> 10, of which waited for: 16 -> 4; matrix products, arithmetic and copies ran while one was open for 14% -> 0% of each run, Pallas kernels for 0% -> 5%
where the time goes in v2:
time: 90.3 us; the launch traced here: 89.7 us
  blocking collectives  25.9 us (29%)
  starting transfers between devices  18.5 us (20%)
  Pallas kernels  18 us (20%)
  waiting for transfers between devices  17.6 us (19%)
  local copies, waits for them, and re-layouts  8.17 us (9%)
  between operations  1.46 us (2%)
    all_to_all x1, blocking collectives, on_device(): gathered = lax.all_to_all(gap, ('grp', 'dom'), 0, 0, tiled=True)  25.9 us
    ppermute x4, starting transfers between devices, on_device(): x = lax.ppermute(x, 'dom', ACROSS)  15.5 us
    pallas_call x4, Pallas kernels, on_device(): call(body, outs, scratch, [SM] * scalars + [VM] * (len(args) - scalars))  14 us
    ppermute x4, waiting for transfers between devices, on_device(): x = lax.ppermute(x, 'dom', ACROSS)  14 us
    unnamed x30, local copies, waits for them, and re-layouts  8.03 us
    ppermute x1, waiting for transfers between devices, on_device(): before = lax.ppermute(normal, 'grp', FROM_BEFORE)  3.64 us
    pallas_call x1, Pallas kernels, on_device(): call(prep_body, [first, first, TILE, TILE, TILE, TILE, TILE, TILE, (96, W...  2.09 us
    pallas_call x1, Pallas kernels, on_device(): call(final_body, [PLANES], [TILE, (32, COLS)], [SM] * 5 + [VM] * 5)  1.89 us
  transfers between devices with their start and end apart: 10, of which 4 were waited for; matrix products, arithmetic and copies ran while one was open for 0% of the time, Pallas kernels for 5%

profile of v2, /device:TPU:1, one launch (start us, length us, event | category | flops | bytes accessed | tf_op | source)
XLA Modules:
  0.0 89.7 jit_solution(14628415726496707869)
XLA Ops:
  1.3 0.0 copy-done.10
  1.3 0.9 copy-done
  2.2 1.0 %copy-done.2 = f32[1,3,2,96,128]{4,3,2,1,0:T(8,128)S(1)} copy-done((f32[1,3,2,96,128]{4,3,2,1,0:T(8,128)S(1)}, f32[1,3,2,96,128]{4,3,2,1,0:T(8,128)}, u32[]{:S(2)}) %copy-start.2) | copy-done | bytes 294936
  3.2 1.0 %copy-done.3 = f32[1,3,2,96,128]{4,3,2,1,0:T(8,128)S(1)} copy-done((f32[1,3,2,96,128]{4,3,2,1,0:T(8,128)S(1)}, f32[1,3,2,96,128]{4,3,2,1,0:T(8,128)}, u32[]{:S(2)}) %copy-start.3) | copy-done | bytes 294936
  4.2 1.0 %copy-done.4 = f32[1,3,2,96,128]{4,3,2,1,0:T(8,128)S(1)} copy-done((f32[1,3,2,96,128]{4,3,2,1,0:T(8,128)S(1)}, f32[1,3,2,96,128]{4,3,2,1,0:T(8,128)}, u32[]{:S(2)}) %copy-start.4) | copy-done | bytes 294936
  5.1 1.0 %copy-done.5 = f32[2,96,384]{2,1,0:T(8,128)S(1)} copy-done((f32[2,96,384]{2,1,0:T(8,128)S(1)}, f32[2,96,384]{2,1,0:T(8,128)}, u32[]{:S(2)}) %copy-start.5) | copy-done | bytes 294936
  6.1 0.9 copy-done.7
  7.0 0.9 copy-done.8
  7.9 0.8 copy-done.9
  8.7 2.1 %shard_map.149 = (f32[8,96,128]{2,1,0:T(8,128)S(1)}, f32[8,96,128]{2,1,0:T(8,128)S(1)}, f32[768,128]{1,0:T(8,128)S(1)}, f32[768,128]{1,0:T(8,128)S(1)}, f32[768,...) custom-call(s32[1]{0:T(128)S(6)} %copy.23.count_ref.refs_0_, ...), custom_call_target="tpu_custom_call" | custom-call | tf_op jit(solution)/shard_map/pallas_call | solution.py:363
  10.8 4.6 %collective-permute-start.1 = (f32[8,96,128]{2,1,0:T(8,128)S(1)}, f32[8,96,128]{2,1,0:T(8,128)S(1)}, u32[]{:S(2)}, u32[]{:S(2)}) collective-permute-start(f32[8,96,128]{2,1,0:T(8,128)S(1)} %get-tuple-element.31), channel_id=1, source_target_pairs={{1,2},{3,4},{5,6},{7,8},{9,10},{11,12},{13,14},{15,16},{17,18},{19... | collective-permute-start | bytes 1179656 | tf_op jit(solution)/shard_map/ppermute | solution.py:374
  15.4 0.1 collective-permute-start.2
  15.4 5.4 %collective-permute-done.1.refs_2_ = f32[8,96,128]{2,1,0:T(8,128)S(1)} collective-permute-done((f32[8,96,128]{2,1,0:T(8,128)S(1)}, f32[8,96,128]{2,1,0:T(8,128)S(1)}, u32[]{:S(2)}, u32[]{:S(2)}) %collective-permute-start.1) | collective-permute-done | bytes 393248 | tf_op jit(solution)/shard_map/ppermute | solution.py:374
  20.8 3.3 %shard_map.150 = (f32[6,96,128]{2,1,0:T(8,128)S(1)}, f32[6,96,128]{2,1,0:T(8,128)S(1)}, f32[768,128]{1,0:T(8,128)S(1)}, f32[768,128]{1,0:T(8,128)S(1)}, f32[768,...) custom-call(s32[1]{0:T(128)S(6)} %copy.23.count_ref.refs_0_, s32[1]{0:T(128)S(6)} %select_n.7.parity_ref.refs_1_, ...), custom_call_target="tpu_custom_call" | custom-call | tf_op jit(solution)/shard_map/pallas_call | solution.py:393
  24.1 3.6 %collective-permute-start.3 = (f32[6,96,128]{2,1,0:T(8,128)S(1)}, f32[6,96,128]{2,1,0:T(8,128)S(1)}, u32[]{:S(2)}, u32[]{:S(2)}) collective-permute-start(f32[6,96,128]{2,1,0:T(8,128)S(1)} %get-tuple-element.40), channel_id=1, source_target_pairs={{1,2},{3,4},{5,6},{7,8},{9,10},{11,12},{13,14},{15,16},{17,18},{19... | collective-permute-start | bytes 884744 | tf_op jit(solution)/shard_map/ppermute | solution.py:374
  27.8 0.1 collective-permute-start.4
  27.9 4.3 %collective-permute-done.3.refs_2_ = f32[6,96,128]{2,1,0:T(8,128)S(1)} collective-permute-done((f32[6,96,128]{2,1,0:T(8,128)S(1)}, f32[6,96,128]{2,1,0:T(8,128)S(1)}, u32[]{:S(2)}, u32[]{:S(2)}) %collective-permute-start.3) | collective-permute-done | bytes 294944 | tf_op jit(solution)/shard_map/ppermute | solution.py:374
  32.2 3.2 %shard_map.151 = (f32[6,96,128]{2,1,0:T(8,128)S(1)}, f32[6,96,128]{2,1,0:T(8,128)S(1)}, f32[768,128]{1,0:T(8,128)S(1)}, f32[768,128]{1,0:T(8,128)S(1)}, f32[768,128]{1,0:T(8,128)S(1)}) custom-call(s32[1]{0:T(128)S(6)} %copy.23.count_ref.refs_0_, s32[1]{0:T(128)S(6)} %select_n.7.parity_ref.refs_1_, f32[6,96,128]{2,1,0:T(8,128)S(1)} %collective-permute-done.3.refs_2_, ...), custom_call_target="tpu_custom_call" | custom-call | tf_op jit(solution)/shard_map/pallas_call | solution.py:393
  35.4 3.6 %collective-permute-start.5 = (f32[6,96,128]{2,1,0:T(8,128)S(1)}, f32[6,96,128]{2,1,0:T(8,128)S(1)}, u32[]{:S(2)}, u32[]{:S(2)}) collective-permute-start(f32[6,96,128]{2,1,0:T(8,128)S(1)} %get-tuple-element.47), channel_id=1, source_target_pairs={{1,2},{3,4},{5,6},{7,8},{9,10},{11,12},{13,14},{15,16},{17,18},{19... | collective-permute-start | bytes 884744 | tf_op jit(solution)/shard_map/ppermute | solution.py:374
  39.1 0.1 collective-permute-start.6
  39.2 4.3 %collective-permute-done.5.refs_2_ = f32[6,96,128]{2,1,0:T(8,128)S(1)} collective-permute-done((f32[6,96,128]{2,1,0:T(8,128)S(1)}, f32[6,96,128]{2,1,0:T(8,128)S(1)}, u32[]{:S(2)}, u32[]{:S(2)}) %collective-permute-start.5) | collective-permute-done | bytes 294944 | tf_op jit(solution)/shard_map/ppermute | solution.py:374
  43.5 3.2 %shard_map.152 = (f32[6,96,128]{2,1,0:T(8,128)S(1)}, f32[6,96,128]{2,1,0:T(8,128)S(1)}, f32[768,128]{1,0:T(8,128)S(1)}, f32[768,128]{1,0:T(8,128)S(1)}, f32[768,128]{1,0:T(8,128)S(1)}) custom-call(s32[1]{0:T(128)S(6)} %copy.23.count_ref.refs_0_, s32[1]{0:T(128)S(6)} %select_n.7.parity_ref.refs_1_, f32[6,96,128]{2,1,0:T(8,128)S(1)} %collective-permute-done.5.refs_2_, ...), custom_call_target="tpu_custom_call" | custom-call | tf_op jit(solution)/shard_map/pallas_call | solution.py:393
  46.7 3.6 %collective-permute-start.7 = (f32[6,96,128]{2,1,0:T(8,128)S(1)}, f32[6,96,128]{2,1,0:T(8,128)S(1)}, u32[]{:S(2)}, u32[]{:S(2)}) collective-permute-start(f32[6,96,128]{2,1,0:T(8,128)S(1)} %get-tuple-element.52), channel_id=1, source_target_pairs={{1,2},{3,4},{5,6},{7,8},{9,10},{11,12},{13,14},{15,16},{17,18},{19... | collective-permute-start | bytes 884744 | tf_op jit(solution)/shard_map/ppermute | solution.py:374
  50.4 0.1 collective-permute-start.8
  50.5 1.5 %collective-permute-start.9 = (f32[16,2048]{1,0:T(8,128)S(1)}, f32[16,2048]{1,0:T(8,128)S(1)}, u32[]{:S(2)}, u32[]{:S(2)}) collective-permute-start(f32[16,2048]{1,0:T(8,128)S(1)} %copy-done.6), channel_id=1, source_target_pairs={{0,32},{32,64},{64,96},{96,0},{1,33},{33,65},{65,97},{97,1},{2,34}... | collective-permute-start | bytes 393224 | tf_op jit(solution)/shard_map/ppermute | solution.py:377
  51.9 1.2 %collective-permute-start = (f32[3,16]{1,0:T(4,128)S(1)}, f32[3,16]{1,0:T(4,128)S(1)}, u32[]{:S(2)}, u32[]{:S(2)}) collective-permute-start(f32[3,16]{1,0:T(4,128)S(1)} %bitcast.26), channel_id=1, source_target_pairs={{0,32},{32,64},{64,96},{96,0},{1,33},{33,65},{65,97},{97,1},{2,34}... | collective-permute-start | bytes 584 | tf_op jit(solution)/shard_map/ppermute | solution.py:378
  53.2 3.6 %collective-permute-done.refs_6_.before = f32[3,16]{1,0:T(4,128)S(1)} collective-permute-done((f32[3,16]{1,0:T(4,128)S(1)}, f32[3,16]{1,0:T(4,128)S(1)}, u32[]{:S(2)}, u32[]{:S(2)}) %collective-permute-start) | collective-permute-done | bytes 224 | tf_op jit(solution)/shard_map/ppermute | solution.py:378
  56.8 0.6 copy-done.11
  57.5 4.2 %shard_map.153 = (f32[6,96,128]{2,1,0:T(8,128)}, f32[768,128]{1,0:T(8,128)S(1)}, f32[128,256]{1,0:T(8,128)S(1)}) custom-call(s32[1]{0:T(128)S(6)} %copy.23.count_ref.refs_0_, s32[1]{0:T(128)S(6)} %select_n.7.parity_ref.refs_1_, s32[1]{0:T(128)} %bitcast.refs_2_, s32[16]{0:T(128)S(1)} %bitcast.30, s32[16]{0:T(128)S(1)} %bitcast.32, f32[3,16]{1,0:T(4,128)S(1)} %bitcast.27, ...), custom_call_target="tpu_custom_call" | custom-call | tf_op jit(solution)/shard_map/pallas_call | solution.py:393
  61.7 0.1 copy.16
  61.9 25.9 %all_to_all.11 = f32[128,1,256]{2,1,0:T(1,128)S(1)} all-to-all(f32[128,1,256]{2,1,0:T(1,128)S(1)} %copy.16), channel_id=1, replica_groups=mesh['grp'=4,'dom'=32] {'grp','dom'}, dimensions={0} | all-to-all | bytes 262144 | tf_op jit(solution)/shard_map/all_to_all | solution.py:400
  87.8 1.9 %shard_map.154 = f32[6,96,128]{2,1,0:T(8,128)} custom-call(s32[1]{0:T(128)S(6)} %copy.23.count_ref.refs_0_, s32[16]{0:T(128)S(1)} %bitcast.31, s32[16]{0:T(128)S(1)} %bitcast.33, f32[3,16]{1,0:T(4,128)S(1)} %bitcast.28, f32[3,16]{1,0:T(4,128)S(1)} %collective-permute-done.refs_6_.before, f32[128,256]{1,0:T(8,128)S(1)} %bitcast.18, f32[16,2048]{1,0:T(8,128)S(1)} %copy-done.6, ...), custom_call_target="tpu_custom_call" | custom-call | tf_op jit(solution)/shard_map/pallas_call | solution.py:401
  (26 shorter events, 0.1 us)
Async XLA Ops:
  0.6 0.7 copy-start.10
  1.3 0.9 copy-start
  2.2 1.0 %copy-start.2 = (f32[1,3,2,96,128]{4,3,2,1,0:T(8,128)S(1)}, f32[1,3,2,96,128]{4,3,2,1,0:T(8,128)}, u32[]{:S(2)}) copy-start(f32[1,3,2,96,128]{4,3,2,1,0:T(8,128)} %param.14) | copy-start | bytes 884740
  3.2 1.0 %copy-start.3 = (f32[1,3,2,96,128]{4,3,2,1,0:T(8,128)S(1)}, f32[1,3,2,96,128]{4,3,2,1,0:T(8,128)}, u32[]{:S(2)}) copy-start(f32[1,3,2,96,128]{4,3,2,1,0:T(8,128)} %param.15) | copy-start | bytes 884740
  4.2 1.0 %copy-start.4 = (f32[1,3,2,96,128]{4,3,2,1,0:T(8,128)S(1)}, f32[1,3,2,96,128]{4,3,2,1,0:T(8,128)}, u32[]{:S(2)}) copy-start(f32[1,3,2,96,128]{4,3,2,1,0:T(8,128)} %param.16) | copy-start | bytes 884740
  5.1 1.0 %copy-start.5 = (f32[2,96,384]{2,1,0:T(8,128)S(1)}, f32[2,96,384]{2,1,0:T(8,128)}, u32[]{:S(2)}) copy-start(f32[2,96,384]{2,1,0:T(8,128)} %constant.31.clone.keep_h) | copy-start | bytes 884740
  6.1 0.9 copy-start.7
  7.0 0.9 copy-start.8
  7.9 0.8 copy-start.9
  8.7 12.1 %copy-start.1 = (f32[1,2,96,128]{3,2,1,0:T(8,128)S(1)}, f32[1,2,96,128]{3,2,1,0:T(8,128)}, u32[]{:S(2)}) copy-start(f32[1,2,96,128]{3,2,1,0:T(8,128)} %param.18) | copy-start | bytes 294916
  10.8 10.0 %collective-permute-start.1 = (f32[8,96,128]{2,1,0:T(8,128)S(1)}, f32[8,96,128]{2,1,0:T(8,128)S(1)}, u32[]{:S(2)}, u32[]{:S(2)}) collective-permute-start(f32[8,96,128]{2,1,0:T(8,128)S(1)} %get-tuple-element.31), channel_id=1, source_target_pairs={{1,2},{3,4},{5,6},{7,8},{9,10},{11,12},{13,14},{15,16},{17,18},{19... | collective-permute-start | bytes 1179656 | tf_op jit(solution)/shard_map/ppermute | solution.py:374
  15.4 5.4 %collective-permute-start.2 = (f32[8,96,128]{2,1,0:T(8,128)S(1)}, f32[8,96,128]{2,1,0:T(8,128)S(1)}, u32[]{:S(2)}, u32[]{:S(2)}) collective-permute-start(f32[8,96,128]{2,1,0:T(8,128)S(1)} %get-tuple-element.32), channel_id=1, source_target_pairs={{0,1},{1,0},{2,3},{3,2},{4,5},{5,4},{6,7},{7,6},{8,9},{9,8},{10,11... | collective-permute-start | bytes 1179656 | tf_op jit(solution)/shard_map/ppermute | solution.py:375
  24.1 8.0 %collective-permute-start.3 = (f32[6,96,128]{2,1,0:T(8,128)S(1)}, f32[6,96,128]{2,1,0:T(8,128)S(1)}, u32[]{:S(2)}, u32[]{:S(2)}) collective-permute-start(f32[6,96,128]{2,1,0:T(8,128)S(1)} %get-tuple-element.40), channel_id=1, source_target_pairs={{1,2},{3,4},{5,6},{7,8},{9,10},{11,12},{13,14},{15,16},{17,18},{19... | collective-permute-start | bytes 884744 | tf_op jit(solution)/shard_map/ppermute | solution.py:374
  27.8 4.4 %collective-permute-start.4 = (f32[6,96,128]{2,1,0:T(8,128)S(1)}, f32[6,96,128]{2,1,0:T(8,128)S(1)}, u32[]{:S(2)}, u32[]{:S(2)}) collective-permute-start(f32[6,96,128]{2,1,0:T(8,128)S(1)} %get-tuple-element.41), channel_id=1, source_target_pairs={{0,1},{1,0},{2,3},{3,2},{4,5},{5,4},{6,7},{7,6},{8,9},{9,8},{10,11... | collective-permute-start | bytes 884744 | tf_op jit(solution)/shard_map/ppermute | solution.py:375
  35.4 8.0 %collective-permute-start.5 = (f32[6,96,128]{2,1,0:T(8,128)S(1)}, f32[6,96,128]{2,1,0:T(8,128)S(1)}, u32[]{:S(2)}, u32[]{:S(2)}) collective-permute-start(f32[6,96,128]{2,1,0:T(8,128)S(1)} %get-tuple-element.47), channel_id=1, source_target_pairs={{1,2},{3,4},{5,6},{7,8},{9,10},{11,12},{13,14},{15,16},{17,18},{19... | collective-permute-start | bytes 884744 | tf_op jit(solution)/shard_map/ppermute | solution.py:374
  39.1 4.4 %collective-permute-start.6 = (f32[6,96,128]{2,1,0:T(8,128)S(1)}, f32[6,96,128]{2,1,0:T(8,128)S(1)}, u32[]{:S(2)}, u32[]{:S(2)}) collective-permute-start(f32[6,96,128]{2,1,0:T(8,128)S(1)} %get-tuple-element.48), channel_id=1, source_target_pairs={{0,1},{1,0},{2,3},{3,2},{4,5},{5,4},{6,7},{7,6},{8,9},{9,8},{10,11... | collective-permute-start | bytes 884744 | tf_op jit(solution)/shard_map/ppermute | solution.py:375
  43.5 7.0 %copy-start.6 = (f32[16,2048]{1,0:T(8,128)S(1)}, f32[16,2048]{1,0:T(8,128)}, u32[]{:S(2)}) copy-start(f32[16,2048]{1,0:T(8,128)} %inv_own.1) | copy-start | bytes 393220
  46.7 5.2 %copy-start.13 = (f32[1,3,16]{2,0,1:T(1,128)S(1)}, f32[1,3,16]{2,0,1:T(1,128)}, u32[]{:S(2)}) copy-start(f32[1,3,16]{2,0,1:T(1,128)} %param.23) | copy-start | bytes 580
  46.7 10.1 %collective-permute-start.7 = (f32[6,96,128]{2,1,0:T(8,128)S(1)}, f32[6,96,128]{2,1,0:T(8,128)S(1)}, u32[]{:S(2)}, u32[]{:S(2)}) collective-permute-start(f32[6,96,128]{2,1,0:T(8,128)S(1)} %get-tuple-element.52), channel_id=1, source_target_pairs={{1,2},{3,4},{5,6},{7,8},{9,10},{11,12},{13,14},{15,16},{17,18},{19... | collective-permute-start | bytes 884744 | tf_op jit(solution)/shard_map/ppermute | solution.py:374
  50.4 6.4 %collective-permute-start.8 = (f32[6,96,128]{2,1,0:T(8,128)S(1)}, f32[6,96,128]{2,1,0:T(8,128)S(1)}, u32[]{:S(2)}, u32[]{:S(2)}) collective-permute-start(f32[6,96,128]{2,1,0:T(8,128)S(1)} %get-tuple-element.53), channel_id=1, source_target_pairs={{0,1},{1,0},{2,3},{3,2},{4,5},{5,4},{6,7},{7,6},{8,9},{9,8},{10,11... | collective-permute-start | bytes 884744 | tf_op jit(solution)/shard_map/ppermute | solution.py:375
  50.5 37.3 %collective-permute-start.9 = (f32[16,2048]{1,0:T(8,128)S(1)}, f32[16,2048]{1,0:T(8,128)S(1)}, u32[]{:S(2)}, u32[]{:S(2)}) collective-permute-start(f32[16,2048]{1,0:T(8,128)S(1)} %copy-done.6), channel_id=1, source_target_pairs={{0,32},{32,64},{64,96},{96,0},{1,33},{33,65},{65,97},{97,1},{2,34}... | collective-permute-start | bytes 393224 | tf_op jit(solution)/shard_map/ppermute | solution.py:377
  51.9 4.9 %collective-permute-start = (f32[3,16]{1,0:T(4,128)S(1)}, f32[3,16]{1,0:T(4,128)S(1)}, u32[]{:S(2)}, u32[]{:S(2)}) collective-permute-start(f32[3,16]{1,0:T(4,128)S(1)} %bitcast.26), channel_id=1, source_target_pairs={{0,32},{32,64},{64,96},{96,0},{1,33},{33,65},{65,97},{97,1},{2,34}... | collective-permute-start | bytes 584 | tf_op jit(solution)/shard_map/ppermute | solution.py:378
  56.8 0.7 copy-start.11
  56.8 0.7 copy-start.12

commit v3 on v2

--- a/solution.py
+++ b/solution.py
@@ -12,31 +12,30 @@
 ROWS = 96
 HALF = ROWS // 2
 COLS = 128
-WROW = 56
-STEP_PARTS = [(0, 48), (WROW, 48), (0, 16), (24, 16), (WROW, 16), (WROW + 24, 16)]
-INNER_PARTS = [(0, 24), (WROW, 24), (0, 16), (WROW, 16)]
 STEP_K, INNER_K = 256, 128
 F32 = jnp.float32
 VM = pl.BlockSpec(memory_space=pltpu.VMEM)
 SM = pl.BlockSpec(memory_space=pltpu.SMEM)
-HBM = pl.BlockSpec(memory_space=pl.ANY)
-
-
-def describe(parts, width):
+HBM = pl.BlockSpec(memory_space=pltpu.HBM)
+
+
+def describe():
     cols = []
-    for n, (start, size) in enumerate(parts):
-        for at in range(start, start + size):
-            b, at = divmod(at, WROW)
-            outer, at = divmod(at, 24)
-            kind, at = divmod(at, 6)
-            x, comp = divmod(at, 3)
-            plane = (-1 if x == 0 else 2) if outer else x
-            cols.append((b, kind % 2, plane, comp) if n < 2 or kind < 2 else None)
-    return cols + [None] * (width - len(cols))
+    for b, kinds in ((0, 4), (1, 4), (0, 2), (1, 2)):
+        for kind in range(kinds):
+            for q in range(16):
+                x, comp = q % 2, (q % 8) // 2
+                plane = x if q < 8 else (-1 if x == 0 else 2)
+                cols.append((b, kind % 2, plane, comp) if q % 8 < 6 else None)
+    cols += [None] * (STEP_K - len(cols))
+    for kind in range(6):
+        for q in range(16):
+            cols.append((q // 8, kind % 2, q % 2, (q % 8) // 2) if q % 8 < 6 else None)
+    return cols + [None] * (STEP_K + INNER_K - len(cols))
 
 
 def selectors():
-    cols = describe(STEP_PARTS, STEP_K) + describe(INNER_PARTS, INNER_K)
+    cols = describe()
     pick_row = np.zeros((96, 24), np.float32)
     pick_col = np.zeros((2, 24, len(cols)), np.float32)
     keep = np.zeros((2, 96, len(cols)), np.float32)
@@ -83,24 +82,44 @@
     return slice(8 * r, 8 * r + 8)
 
 
-def build(wk, outer, i, arr):
-    lo = arr - arr.astype(jnp.bfloat16).astype(F32)
-    for kind, val in enumerate((arr, lane_up(arr), lo, lane_up(lo))):
-        wk[every(outer * 24 + kind * 6 + i, WROW), :] = val
-
-
-def sweep(wk, lhs, parts, width, blocks, finish):
-    wk[ROWS * WROW : (ROWS + 1) * WROW, :] = wk[0:WROW, :]
-    pad = jnp.zeros((width - sum(n for _, n in parts), COLS), F32)
+def split(u):
+    hi = u.astype(jnp.bfloat16)
+    lo = (u - hi.astype(F32)).astype(jnp.bfloat16)
+    return [hi, lane_up(hi), lo, lane_up(lo)]
+
+
+def step_rows(own, outer):
+    done = {}
+
+    def one(r):
+        r %= ROWS
+        if r not in done:
+            done[r] = split(jnp.concatenate([own[tile(r), :], outer[tile(r), :]], 0))
+        return done[r]
+
+    def rows(r):
+        here, there = one(r), one(r + 1)
+        pad = jnp.zeros((64, COLS), jnp.bfloat16)
+        return jnp.concatenate(here + there + here[:2] + there[:2] + [pad], 0)
+
+    return rows
+
+
+def inner_rows(own):
+    def rows(r):
+        parts = split(jnp.concatenate([own[tile(r), :], own[tile((r + 1) % ROWS), :]], 0))
+        pad = jnp.zeros((32, COLS), jnp.bfloat16)
+        return jnp.concatenate(parts + parts[:2] + [pad], 0)
+
+    return rows
+
+
+def sweep(rows, lhs, blocks, finish):
     carry = {}
     first = {}
     for i in range(HALF):
-        sides = []
-        for r in (i, i + HALF):
-            base = r * WROW
-            pieces = [wk[base + at : base + at + n, :] for at, n in parts]
-            sides.append(jnp.concatenate(pieces + [pad], 0))
-        out = jnp.dot(lhs, jnp.concatenate(sides, 1), preferred_element_type=F32)
+        rhs = jnp.concatenate([rows(i), rows(i + HALF)], 1)
+        out = jnp.dot(lhs, rhs, preferred_element_type=F32)
         for h in range(2):
             r = i + h * HALF
             for n, terms in enumerate(blocks):
@@ -125,14 +144,14 @@
         finish(n, HALF, first[1, n] + carry[0, n])
 
 
-def inner_pass(wk, a_ref, si, e, m, u, w, ei_out, h_out):
+def inner_pass(a_ref, si, e, m, u, w, ei_out, h_out):
     def finish(n, r, force):
         at = tile(r)
         rest = e[at, :] - m[at, :] * force
         ei_out[at, :] = rest
         h_out[at, :] = u[at, :] + (w[at, :] + rest)
 
-    sweep(wk, a_ref[0:32, STEP_K:], INNER_PARTS, INNER_K, [[(0, si)]], finish)
+    sweep(inner_rows(u), a_ref[0:32, STEP_K:], [[(0, si)]], finish)
 
 
 def send_edges(odd, u, h, x_msg, d_msg):
@@ -146,7 +165,7 @@
 def prep_body(
     count_ref, parity_ref, kmat_h, row_h, col_h, keep_h, u_h, scale_h, v_h, mass_h, ext_h,
     x_msg, d_msg, u_t, w_t, e_t, m_t, ei_t, si_t, a_out,
-    kmat, row, col, keep, u_n, scale, v_n, mass, ext_n, wk, h_t, sems,
+    kmat, row, col, keep, u_n, scale, v_n, mass, ext_n, h_t, sems,
 ):
     pairs = [
         (kmat_h, kmat), (row_h, row), (col_h, col), (keep_h, keep), (u_h, u_n),
@@ -165,19 +184,22 @@
     full = full + keep[1] * jnp.dot(rows, col[1], precision=high, preferred_element_type=F32)
     big = full.astype(jnp.bfloat16).astype(F32)
     slot = lax.broadcasted_iota(jnp.int32, full.shape, 1)
-    main = (slot < 96) | ((slot >= STEP_K) & (slot < STEP_K + 48))
-    a_out[...] = jnp.where(main, big, full - big)
+    main = (slot < 128) | ((slot >= STEP_K) & (slot < STEP_K + 64))
+    a_out[...] = jnp.where(main, big, full - big).astype(jnp.bfloat16)
     inv = [(dt * dt) / mass[p] for p in range(2)]
+    blank = jnp.zeros((ROWS, COLS), F32)
+    for q in (6, 7):
+        for ref in (u_t, w_t, e_t, m_t, si_t):
+            ref[every(q), :] = blank
     for c in range(3):
         for p in range(2):
             q = 2 * c + p
-            build(wk, 0, 3 * p + c, u_n[q])
             u_t[every(q), :] = u_n[q]
             w_t[every(q), :] = dt * v_n[q]
             e_t[every(q), :] = inv[p] * ext_n[q]
             m_t[every(q), :] = inv[p]
             si_t[every(q), :] = scale[0]
-    inner_pass(wk, a_out, si_t, e_t, m_t, u_t, w_t, ei_t, h_t)
+    inner_pass(a_out, si_t, e_t, m_t, u_t, w_t, ei_t, h_t)
     send_edges(odd, u_t, h_t, x_msg, d_msg)
     x_msg[6] = jnp.where(odd, inv[1], inv[0])
     d_msg[6] = jnp.where(odd, inv[0], inv[1])
@@ -203,7 +225,7 @@
         x_msg, d_msg, u2, w2, ei_out = take(5)
     if rnd == 0:
         sx_t, mh_t = take(2)
-    wk, uh, hh, u1, u1h, w1, h_t = take(7)
+    uh, hh, u1, u1h, w1, h_t = take(6)
     if last:
         u2, hits = take(2)
     odd = parity_ref[0] == 1
@@ -214,14 +236,15 @@
     def upper(k):
         return jnp.where(odd, x_in[k], d_in[k])
 
+    blank = jnp.zeros((ROWS, COLS), F32)
+    for q in (6, 7):
+        for ref in (uh, hh) + ((mh_t, sx_t) if rnd == 0 else ()):
+            ref[every(q), :] = blank
     act = [jnp.where(count_ref[0] > 2 * rnd + k, 1.0, 0.0).astype(F32) for k in range(2)]
     for c in range(3):
         for p, get in ((0, lower), (1, upper)):
             q = 2 * c + p
-            build(wk, 0, 3 * p + c, u_t[every(q), :])
-            outer = get(c)
-            build(wk, 1, 3 * p + c, outer)
-            uh[every(q), :] = outer
+            uh[every(q), :] = get(c)
             hh[every(q), :] = get(3 + c)
             if rnd == 0:
                 mh_t[every(q), :] = get(6)
@@ -237,11 +260,7 @@
             before = uh[at, :]
             u1h[at, :] = before + act[0] * ((hh[at, :] - mh_t[at, :] * force) - before)
 
-    sweep(wk, a_ref[32:96, 0:STEP_K], STEP_PARTS, STEP_K, [[(0, sx_t)], [(32, sx_t)]], finish_first)
-    for c in range(3):
-        for p in range(2):
-            build(wk, 0, 3 * p + c, u1[every(2 * c + p), :])
-            build(wk, 1, 3 * p + c, u1h[every(2 * c + p), :])
+    sweep(step_rows(u_t, uh), a_ref[32:96, 0:STEP_K], [[(0, sx_t)], [(32, sx_t)]], finish_first)
 
     def finish_second(n, r, force):
         at = tile(r)
@@ -249,16 +268,13 @@
         w2[at, :] = w
         u2[at, :] = u1[at, :] + act[1] * w
 
-    sweep(wk, a_ref[0:64, 0:STEP_K], STEP_PARTS, STEP_K, [[(0, si_t), (32, sx_t)]], finish_second)
+    sweep(step_rows(u1, u1h), a_ref[0:64, 0:STEP_K], [[(0, si_t), (32, sx_t)]], finish_second)
     if last:
         for q in range(6):
             u_out[q] = u2[every(q), :]
         partial_gaps(count_ref, place_ref, own, peer, normal, before, w2, g_out, hits)
         return
-    for c in range(3):
-        for p in range(2):
-            build(wk, 0, 3 * p + c, u2[every(2 * c + p), :])
-    inner_pass(wk, a_ref, si_t, e_t, m_t, u2, w2, ei_out, h_t)
+    inner_pass(a_ref, si_t, e_t, m_t, u2, w2, ei_out, h_t)
     send_edges(odd, u2, h_t, x_msg, d_msg)
 
 
@@ -326,7 +342,7 @@
 def call(body, outs, scratch, ins, limit=24 * 1024 * 1024):
     return pl.pallas_call(
         body,
-        out_shape=[jax.ShapeDtypeStruct(s, F32) for s in outs],
+        out_shape=[s if isinstance(s, jax.ShapeDtypeStruct) else jax.ShapeDtypeStruct(s, F32) for s in outs],
         in_specs=ins,
         out_specs=[VM] * len(outs),
         scratch_shapes=[pltpu.VMEM(s, F32) if isinstance(s, tuple) else s for s in scratch],
@@ -336,7 +352,6 @@
 
 TILE = (ROWS * 8, COLS)
 PLANES = (6, ROWS, COLS)
-WORK = ((ROWS + 1) * WROW, COLS)
 WIDTH = STEP_K + INNER_K
 ACROSS = [(i, i + 1) for i in range(1, 31, 2)] + [(i + 1, i) for i in range(1, 31, 2)]
 WITHIN = [(i, i ^ 1) for i in range(32)]
@@ -360,12 +375,13 @@
 
     first = (8, ROWS, COLS)
     pair = (2, ROWS, COLS)
+    weights = jax.ShapeDtypeStruct((96, WIDTH), jnp.bfloat16)
     x, d, u, w, e, m, ei, si, a = call(
         prep_body,
-        [first, first, TILE, TILE, TILE, TILE, TILE, TILE, (96, WIDTH)],
+        [first, first, TILE, TILE, TILE, TILE, TILE, TILE, weights],
         [
             (24, 24), (96, 24), (2, 24, WIDTH), (2, 96, WIDTH), PLANES, pair, PLANES, pair, PLANES,
-            WORK, TILE, pltpu.SemaphoreType.DMA((9,)),
+            TILE, pltpu.SemaphoreType.DMA((9,)),
         ],
         [SM] * 2 + [HBM] * 9,
     )(substeps, parity, stiffness[0], PICK_ROW, PICK_COL, KEEP, field, scale, speed, weight, loads)
@@ -376,6 +392,7 @@
         if rnd == 0:
             inv_before = lax.ppermute(schur_inverse, "grp", FROM_BEFORE)
             before = lax.ppermute(normal, "grp", FROM_BEFORE)
+            x, d, inv_before, before = lax.optimization_barrier((x, d, inv_before, before))
         last = rnd == ROUNDS - 1
         args = [substeps, parity]
         if last:
@@ -385,7 +402,7 @@
         args += [scale] if rnd == 0 else [sx, mh]
         outs = [PLANES, TILE, (128, 2 * COLS)] if last else [PLANES, PLANES, TILE, TILE, TILE]
         outs += [TILE, TILE] if rnd == 0 else []
-        scratch = [WORK] + [TILE] * 6 + ([TILE, (32, 8, COLS)] if last else [])
+        scratch = [TILE] * 6 + ([TILE, (32, 8, COLS)] if last else [])
 
         def body(*refs, rnd=rnd):
             return round_body(rnd, *refs)

time: 90.3 us -> 89.9 us (level)
  waiting for transfers between devices: 17.6 us -> 16.2 us
    ppermute x4, waiting for transfers between devices: 14 us -> 12.7 us  [on_device(): x = lax.ppermute(x, 'dom', ACROSS)]
  transfers between devices with their start and end apart: 10 -> 10, of which waited for: 4 -> 4; matrix products, arithmetic and copies ran while one was open for 0% -> 0% of each run, Pallas kernels for 5% -> 0%
where the time goes in v3:
time: 89.9 us; the launch traced here: 89.3 us
  blocking collectives  26.6 us (30%)
  starting transfers between devices  19.2 us (21%)
  Pallas kernels  17.7 us (20%)
  waiting for transfers between devices  16.2 us (18%)
  local copies, waits for them, and re-layouts  8.18 us (9%)
  between operations  1.46 us (2%)
    all_to_all x1, blocking collectives, on_device(): gathered = lax.all_to_all(gap, ('grp', 'dom'), 0, 0, tiled=True)  26.6 us
    ppermute x4, starting transfers between devices, on_device(): x = lax.ppermute(x, 'dom', ACROSS)  16.2 us
    pallas_call x4, Pallas kernels, on_device(): call(body, outs, scratch, [SM] * scalars + [VM] * (len(args) - scalars))  13.7 us
    ppermute x4, waiting for transfers between devices, on_device(): x = lax.ppermute(x, 'dom', ACROSS)  12.7 us
    unnamed x30, local copies, waits for them, and re-layouts  8.04 us
    ppermute x1, waiting for transfers between devices, on_device(): before = lax.ppermute(normal, 'grp', FROM_BEFORE)  3.46 us
    pallas_call x1, Pallas kernels, on_device(): call(prep_body, [first, first, TILE, TILE, TILE, TILE, TILE, TILE, weight...  2.12 us
    pallas_call x1, Pallas kernels, on_device(): call(final_body, [PLANES], [TILE, (32, COLS)], [SM] * 5 + [VM] * 5)  1.88 us
  transfers between devices with their start and end apart: 10, of which 4 were waited for; matrix products, arithmetic and copies ran while one was open for 0% of the time, Pallas kernels for 0%

profile of v3, /device:TPU:1, one launch (start us, length us, event | category | flops | bytes accessed | tf_op | source)
XLA Modules:
  0.0 89.3 jit_solution(2258213296921109628)
XLA Ops:
  1.3 0.0 copy-done.10
  1.3 0.9 copy-done
  2.2 1.0 %copy-done.2 = f32[1,3,2,96,128]{4,3,2,1,0:T(8,128)S(1)} copy-done((f32[1,3,2,96,128]{4,3,2,1,0:T(8,128)S(1)}, f32[1,3,2,96,128]{4,3,2,1,0:T(8,128)}, u32[]{:S(2)}) %copy-start.2) | copy-done | bytes 294936
  3.2 1.0 %copy-done.3 = f32[1,3,2,96,128]{4,3,2,1,0:T(8,128)S(1)} copy-done((f32[1,3,2,96,128]{4,3,2,1,0:T(8,128)S(1)}, f32[1,3,2,96,128]{4,3,2,1,0:T(8,128)}, u32[]{:S(2)}) %copy-start.3) | copy-done | bytes 294936
  4.2 1.0 %copy-done.4 = f32[1,3,2,96,128]{4,3,2,1,0:T(8,128)S(1)} copy-done((f32[1,3,2,96,128]{4,3,2,1,0:T(8,128)S(1)}, f32[1,3,2,96,128]{4,3,2,1,0:T(8,128)}, u32[]{:S(2)}) %copy-start.4) | copy-done | bytes 294936
  5.1 1.0 %copy-done.5 = f32[2,96,384]{2,1,0:T(8,128)S(1)} copy-done((f32[2,96,384]{2,1,0:T(8,128)S(1)}, f32[2,96,384]{2,1,0:T(8,128)}, u32[]{:S(2)}) %copy-start.5) | copy-done | bytes 294936
  6.1 0.9 copy-done.7
  7.0 0.9 copy-done.8
  7.9 0.8 copy-done.9
  8.7 2.1 %shard_map.149 = (f32[8,96,128]{2,1,0:T(8,128)S(1)}, f32[8,96,128]{2,1,0:T(8,128)S(1)}, f32[768,128]{1,0:T(8,128)S(1)}, f32[768,128]{1,0:T(8,128)S(1)}, f32[768,...) custom-call(s32[1]{0:T(128)S(6)} %copy.23.count_ref.refs_0_, ...), custom_call_target="tpu_custom_call" | custom-call | tf_op jit(solution)/shard_map/pallas_call | solution.py:379
  10.8 4.6 %collective-permute-start = (f32[8,96,128]{2,1,0:T(8,128)S(1)}, f32[8,96,128]{2,1,0:T(8,128)S(1)}, u32[]{:S(2)}, u32[]{:S(2)}) collective-permute-start(f32[8,96,128]{2,1,0:T(8,128)S(1)} %get-tuple-element.35), channel_id=1, source_target_pairs={{1,2},{3,4},{5,6},{7,8},{9,10},{11,12},{13,14},{15,16},{17,18},{19... | collective-permute-start | bytes 1179656 | tf_op jit(solution)/shard_map/ppermute | solution.py:390
  15.4 0.1 collective-permute-start.1
  15.5 1.3 %collective-permute-start.2 = (f32[16,2048]{1,0:T(8,128)S(1)}, f32[16,2048]{1,0:T(8,128)S(1)}, u32[]{:S(2)}, u32[]{:S(2)}) collective-permute-start(f32[16,2048]{1,0:T(8,128)S(1)} %copy-done.6), channel_id=1, source_target_pairs={{0,32},{32,64},{64,96},{96,0},{1,33},{33,65},{65,97},{97,1},{2,34}... | collective-permute-start | bytes 393224 | tf_op jit(solution)/shard_map/ppermute | solution.py:393
  16.8 1.2 %collective-permute-start.3 = (f32[3,16]{1,0:T(4,128)S(1)}, f32[3,16]{1,0:T(4,128)S(1)}, u32[]{:S(2)}, u32[]{:S(2)}) collective-permute-start(f32[3,16]{1,0:T(4,128)S(1)} %bitcast.26), channel_id=1, source_target_pairs={{0,32},{32,64},{64,96},{96,0},{1,33},{33,65},{65,97},{97,1},{2,34}... | collective-permute-start | bytes 584 | tf_op jit(solution)/shard_map/ppermute | solution.py:394
  18.0 3.5 %collective-permute-done.3.refs_6_.before = f32[3,16]{1,0:T(4,128)S(1)} collective-permute-done((f32[3,16]{1,0:T(4,128)S(1)}, f32[3,16]{1,0:T(4,128)S(1)}, u32[]{:S(2)}, u32[]{:S(2)}) %collective-permute-start.3) | collective-permute-done | bytes 224 | tf_op jit(solution)/shard_map/ppermute | solution.py:394
  21.5 3.2 %shard_map.150 = (f32[6,96,128]{2,1,0:T(8,128)S(1)}, f32[6,96,128]{2,1,0:T(8,128)S(1)}, f32[768,128]{1,0:T(8,128)S(1)}, f32[768,128]{1,0:T(8,128)S(1)}, f32[768,...) custom-call(s32[1]{0:T(128)S(6)} %copy.23.count_ref.refs_0_, s32[1]{0:T(128)S(6)} %select_n.7.parity_ref.refs_1_, ...), custom_call_target="tpu_custom_call" | custom-call | tf_op jit(solution)/shard_map/pallas_call | solution.py:410
  24.7 4.4 %collective-permute-start.4 = (f32[6,96,128]{2,1,0:T(8,128)S(1)}, f32[6,96,128]{2,1,0:T(8,128)S(1)}, u32[]{:S(2)}, u32[]{:S(2)}) collective-permute-start(f32[6,96,128]{2,1,0:T(8,128)S(1)} %get-tuple-element.47), channel_id=1, source_target_pairs={{1,2},{3,4},{5,6},{7,8},{9,10},{11,12},{13,14},{15,16},{17,18},{19... | collective-permute-start | bytes 884744 | tf_op jit(solution)/shard_map/ppermute | solution.py:390
  29.0 0.1 collective-permute-start.5
  29.1 4.3 %collective-permute-done.4.refs_2_ = f32[6,96,128]{2,1,0:T(8,128)S(1)} collective-permute-done((f32[6,96,128]{2,1,0:T(8,128)S(1)}, f32[6,96,128]{2,1,0:T(8,128)S(1)}, u32[]{:S(2)}, u32[]{:S(2)}) %collective-permute-start.4) | collective-permute-done | bytes 294944 | tf_op jit(solution)/shard_map/ppermute | solution.py:390
  33.4 3.1 %shard_map.151 = (f32[6,96,128]{2,1,0:T(8,128)S(1)}, f32[6,96,128]{2,1,0:T(8,128)S(1)}, f32[768,128]{1,0:T(8,128)S(1)}, f32[768,128]{1,0:T(8,128)S(1)}, f32[768,128]{1,0:T(8,128)S(1)}) custom-call(s32[1]{0:T(128)S(6)} %copy.23.count_ref.refs_0_, s32[1]{0:T(128)S(6)} %select_n.7.parity_ref.refs_1_, f32[6,96,128]{2,1,0:T(8,128)S(1)} %collective-permute-done.4.refs_2_, ...), custom_call_target="tpu_custom_call" | custom-call | tf_op jit(solution)/shard_map/pallas_call | solution.py:410
  36.6 3.6 %collective-permute-start.6 = (f32[6,96,128]{2,1,0:T(8,128)S(1)}, f32[6,96,128]{2,1,0:T(8,128)S(1)}, u32[]{:S(2)}, u32[]{:S(2)}) collective-permute-start(f32[6,96,128]{2,1,0:T(8,128)S(1)} %get-tuple-element.54), channel_id=1, source_target_pairs={{1,2},{3,4},{5,6},{7,8},{9,10},{11,12},{13,14},{15,16},{17,18},{19... | collective-permute-start | bytes 884744 | tf_op jit(solution)/shard_map/ppermute | solution.py:390
  40.2 0.1 collective-permute-start.7
  40.3 4.3 %collective-permute-done.6.refs_2_ = f32[6,96,128]{2,1,0:T(8,128)S(1)} collective-permute-done((f32[6,96,128]{2,1,0:T(8,128)S(1)}, f32[6,96,128]{2,1,0:T(8,128)S(1)}, u32[]{:S(2)}, u32[]{:S(2)}) %collective-permute-start.6) | collective-permute-done | bytes 294944 | tf_op jit(solution)/shard_map/ppermute | solution.py:390
  44.6 3.1 %shard_map.152 = (f32[6,96,128]{2,1,0:T(8,128)S(1)}, f32[6,96,128]{2,1,0:T(8,128)S(1)}, f32[768,128]{1,0:T(8,128)S(1)}, f32[768,128]{1,0:T(8,128)S(1)}, f32[768,128]{1,0:T(8,128)S(1)}) custom-call(s32[1]{0:T(128)S(6)} %copy.23.count_ref.refs_0_, s32[1]{0:T(128)S(6)} %select_n.7.parity_ref.refs_1_, f32[6,96,128]{2,1,0:T(8,128)S(1)} %collective-permute-done.6.refs_2_, ...), custom_call_target="tpu_custom_call" | custom-call | tf_op jit(solution)/shard_map/pallas_call | solution.py:410
  47.7 3.6 %collective-permute-start.8 = (f32[6,96,128]{2,1,0:T(8,128)S(1)}, f32[6,96,128]{2,1,0:T(8,128)S(1)}, u32[]{:S(2)}, u32[]{:S(2)}) collective-permute-start(f32[6,96,128]{2,1,0:T(8,128)S(1)} %get-tuple-element.59), channel_id=1, source_target_pairs={{1,2},{3,4},{5,6},{7,8},{9,10},{11,12},{13,14},{15,16},{17,18},{19... | collective-permute-start | bytes 884744 | tf_op jit(solution)/shard_map/ppermute | solution.py:390
  51.3 0.3 collective-permute-start.9
  51.6 4.1 %collective-permute-done.8.refs_7_ = f32[6,96,128]{2,1,0:T(8,128)S(1)} collective-permute-done((f32[6,96,128]{2,1,0:T(8,128)S(1)}, f32[6,96,128]{2,1,0:T(8,128)S(1)}, u32[]{:S(2)}, u32[]{:S(2)}) %collective-permute-start.8) | collective-permute-done | bytes 294944 | tf_op jit(solution)/shard_map/ppermute | solution.py:390
  55.7 0.7 copy-done.11
  56.4 4.3 %shard_map.153 = (f32[6,96,128]{2,1,0:T(8,128)}, f32[768,128]{1,0:T(8,128)S(1)}, f32[128,256]{1,0:T(8,128)S(1)}) custom-call(s32[1]{0:T(128)S(6)} %copy.23.count_ref.refs_0_, s32[1]{0:T(128)S(6)} %select_n.7.parity_ref.refs_1_, s32[1]{0:T(128)} %bitcast.refs_2_, s32[16]{0:T(128)S(1)} %bitcast.30, s32[16]{0:T(128)S(1)} %bitcast.32, f32[3,16]{1,0:T(4,128)S(1)} %bitcast.27, ...), custom_call_target="tpu_custom_call" | custom-call | tf_op jit(solution)/shard_map/pallas_call | solution.py:410
  60.7 0.1 copy.16
  60.8 26.6 %all_to_all.11 = f32[128,1,256]{2,1,0:T(1,128)S(1)} all-to-all(f32[128,1,256]{2,1,0:T(1,128)S(1)} %copy.16), channel_id=1, replica_groups=mesh['grp'=4,'dom'=32] {'grp','dom'}, dimensions={0} | all-to-all | bytes 262144 | tf_op jit(solution)/shard_map/all_to_all | solution.py:417
  87.4 1.9 %shard_map.154 = f32[6,96,128]{2,1,0:T(8,128)} custom-call(s32[1]{0:T(128)S(6)} %copy.23.count_ref.refs_0_, s32[16]{0:T(128)S(1)} %bitcast.31, s32[16]{0:T(128)S(1)} %bitcast.33, f32[3,16]{1,0:T(4,128)S(1)} %bitcast.28, f32[3,16]{1,0:T(4,128)S(1)} %collective-permute-done.3.refs_6_.before, f32[128,256]{1,0:T(8,128)S(1)} %bitcast.18, ...), custom_call_target="tpu_custom_call" | custom-call | tf_op jit(solution)/shard_map/pallas_call | solution.py:418
  (26 shorter events, 0.1 us)
Async XLA Ops:
  0.6 0.7 copy-start.10
  1.3 0.9 copy-start
  2.2 1.0 %copy-start.2 = (f32[1,3,2,96,128]{4,3,2,1,0:T(8,128)S(1)}, f32[1,3,2,96,128]{4,3,2,1,0:T(8,128)}, u32[]{:S(2)}) copy-start(f32[1,3,2,96,128]{4,3,2,1,0:T(8,128)} %param.14) | copy-start | bytes 884740
  3.2 1.0 %copy-start.3 = (f32[1,3,2,96,128]{4,3,2,1,0:T(8,128)S(1)}, f32[1,3,2,96,128]{4,3,2,1,0:T(8,128)}, u32[]{:S(2)}) copy-start(f32[1,3,2,96,128]{4,3,2,1,0:T(8,128)} %param.15) | copy-start | bytes 884740
  4.2 1.0 %copy-start.4 = (f32[1,3,2,96,128]{4,3,2,1,0:T(8,128)S(1)}, f32[1,3,2,96,128]{4,3,2,1,0:T(8,128)}, u32[]{:S(2)}) copy-start(f32[1,3,2,96,128]{4,3,2,1,0:T(8,128)} %param.16) | copy-start | bytes 884740
  5.1 1.0 %copy-start.5 = (f32[2,96,384]{2,1,0:T(8,128)S(1)}, f32[2,96,384]{2,1,0:T(8,128)}, u32[]{:S(2)}) copy-start(f32[2,96,384]{2,1,0:T(8,128)} %constant.31.clone.keep_h) | copy-start | bytes 884740
  6.1 0.9 copy-start.7
  7.0 0.9 copy-start.8
  7.9 0.8 copy-start.9
  8.7 6.8 %copy-start.6 = (f32[16,2048]{1,0:T(8,128)S(1)}, f32[16,2048]{1,0:T(8,128)}, u32[]{:S(2)}) copy-start(f32[16,2048]{1,0:T(8,128)} %inv_own.1) | copy-start | bytes 393220
  8.7 12.8 %copy-start.1 = (f32[1,2,96,128]{3,2,1,0:T(8,128)S(1)}, f32[1,2,96,128]{3,2,1,0:T(8,128)}, u32[]{:S(2)}) copy-start(f32[1,2,96,128]{3,2,1,0:T(8,128)} %param.18) | copy-start | bytes 294916
  10.8 6.0 %copy-start.13 = (f32[1,3,16]{2,0,1:T(1,128)S(1)}, f32[1,3,16]{2,0,1:T(1,128)}, u32[]{:S(2)}) copy-start(f32[1,3,16]{2,0,1:T(1,128)} %param.23) | copy-start | bytes 580
  10.8 10.7 %collective-permute-start = (f32[8,96,128]{2,1,0:T(8,128)S(1)}, f32[8,96,128]{2,1,0:T(8,128)S(1)}, u32[]{:S(2)}, u32[]{:S(2)}) collective-permute-start(f32[8,96,128]{2,1,0:T(8,128)S(1)} %get-tuple-element.35), channel_id=1, source_target_pairs={{1,2},{3,4},{5,6},{7,8},{9,10},{11,12},{13,14},{15,16},{17,18},{19... | collective-permute-start | bytes 1179656 | tf_op jit(solution)/shard_map/ppermute | solution.py:390
  15.4 6.1 %collective-permute-start.1 = (f32[8,96,128]{2,1,0:T(8,128)S(1)}, f32[8,96,128]{2,1,0:T(8,128)S(1)}, u32[]{:S(2)}, u32[]{:S(2)}) collective-permute-start(f32[8,96,128]{2,1,0:T(8,128)S(1)} %get-tuple-element.36), channel_id=1, source_target_pairs={{0,1},{1,0},{2,3},{3,2},{4,5},{5,4},{6,7},{7,6},{8,9},{9,8},{10,11... | collective-permute-start | bytes 1179656 | tf_op jit(solution)/shard_map/ppermute | solution.py:391
  15.5 6.0 %collective-permute-start.2 = (f32[16,2048]{1,0:T(8,128)S(1)}, f32[16,2048]{1,0:T(8,128)S(1)}, u32[]{:S(2)}, u32[]{:S(2)}) collective-permute-start(f32[16,2048]{1,0:T(8,128)S(1)} %copy-done.6), channel_id=1, source_target_pairs={{0,32},{32,64},{64,96},{96,0},{1,33},{33,65},{65,97},{97,1},{2,34}... | collective-permute-start | bytes 393224 | tf_op jit(solution)/shard_map/ppermute | solution.py:393
  16.8 4.7 %collective-permute-start.3 = (f32[3,16]{1,0:T(4,128)S(1)}, f32[3,16]{1,0:T(4,128)S(1)}, u32[]{:S(2)}, u32[]{:S(2)}) collective-permute-start(f32[3,16]{1,0:T(4,128)S(1)} %bitcast.26), channel_id=1, source_target_pairs={{0,32},{32,64},{64,96},{96,0},{1,33},{33,65},{65,97},{97,1},{2,34}... | collective-permute-start | bytes 584 | tf_op jit(solution)/shard_map/ppermute | solution.py:394
  24.7 8.8 %collective-permute-start.4 = (f32[6,96,128]{2,1,0:T(8,128)S(1)}, f32[6,96,128]{2,1,0:T(8,128)S(1)}, u32[]{:S(2)}, u32[]{:S(2)}) collective-permute-start(f32[6,96,128]{2,1,0:T(8,128)S(1)} %get-tuple-element.47), channel_id=1, source_target_pairs={{1,2},{3,4},{5,6},{7,8},{9,10},{11,12},{13,14},{15,16},{17,18},{19... | collective-permute-start | bytes 884744 | tf_op jit(solution)/shard_map/ppermute | solution.py:390
  29.0 4.4 %collective-permute-start.5 = (f32[6,96,128]{2,1,0:T(8,128)S(1)}, f32[6,96,128]{2,1,0:T(8,128)S(1)}, u32[]{:S(2)}, u32[]{:S(2)}) collective-permute-start(f32[6,96,128]{2,1,0:T(8,128)S(1)} %get-tuple-element.48), channel_id=1, source_target_pairs={{0,1},{1,0},{2,3},{3,2},{4,5},{5,4},{6,7},{7,6},{8,9},{9,8},{10,11... | collective-permute-start | bytes 884744 | tf_op jit(solution)/shard_map/ppermute | solution.py:391
  36.6 8.0 %collective-permute-start.6 = (f32[6,96,128]{2,1,0:T(8,128)S(1)}, f32[6,96,128]{2,1,0:T(8,128)S(1)}, u32[]{:S(2)}, u32[]{:S(2)}) collective-permute-start(f32[6,96,128]{2,1,0:T(8,128)S(1)} %get-tuple-element.54), channel_id=1, source_target_pairs={{1,2},{3,4},{5,6},{7,8},{9,10},{11,12},{13,14},{15,16},{17,18},{19... | collective-permute-start | bytes 884744 | tf_op jit(solution)/shard_map/ppermute | solution.py:390
  40.2 4.4 %collective-permute-start.7 = (f32[6,96,128]{2,1,0:T(8,128)S(1)}, f32[6,96,128]{2,1,0:T(8,128)S(1)}, u32[]{:S(2)}, u32[]{:S(2)}) collective-permute-start(f32[6,96,128]{2,1,0:T(8,128)S(1)} %get-tuple-element.55), channel_id=1, source_target_pairs={{0,1},{1,0},{2,3},{3,2},{4,5},{5,4},{6,7},{7,6},{8,9},{9,8},{10,11... | collective-permute-start | bytes 884744 | tf_op jit(solution)/shard_map/ppermute | solution.py:391
  47.7 8.0 %collective-permute-start.8 = (f32[6,96,128]{2,1,0:T(8,128)S(1)}, f32[6,96,128]{2,1,0:T(8,128)S(1)}, u32[]{:S(2)}, u32[]{:S(2)}) collective-permute-start(f32[6,96,128]{2,1,0:T(8,128)S(1)} %get-tuple-element.59), channel_id=1, source_target_pairs={{1,2},{3,4},{5,6},{7,8},{9,10},{11,12},{13,14},{15,16},{17,18},{19... | collective-permute-start | bytes 884744 | tf_op jit(solution)/shard_map/ppermute | solution.py:390
  51.3 4.4 %collective-permute-start.9 = (f32[6,96,128]{2,1,0:T(8,128)S(1)}, f32[6,96,128]{2,1,0:T(8,128)S(1)}, u32[]{:S(2)}, u32[]{:S(2)}) collective-permute-start(f32[6,96,128]{2,1,0:T(8,128)S(1)} %get-tuple-element.60), channel_id=1, source_target_pairs={{0,1},{1,0},{2,3},{3,2},{4,5},{5,4},{6,7},{7,6},{8,9},{9,8},{10,11... | collective-permute-start | bytes 884744 | tf_op jit(solution)/shard_map/ppermute | solution.py:391
  55.7 0.7 copy-start.11
  55.7 0.7 copy-start.12

commit v4 on v3

--- a/solution.py
+++ b/solution.py
@@ -213,21 +213,22 @@
     count_ref, parity_ref = take(2)
     last = rnd == ROUNDS - 1
     if last:
-        place_ref, own, peer, normal, before = take(5)
+        (place_ref,) = take(1)
     x_in, d_in, u_t, w_t, e_t, m_t, ei_t, si_t, a_ref = take(9)
     if rnd == 0:
         (scale,) = take(1)
     else:
         sx_t, mh_t = take(2)
     if last:
-        u_out, w2, g_out = take(3)
+        pick, share = take(2)
+        u_out, v_out, g_out = take(3)
     else:
         x_msg, d_msg, u2, w2, ei_out = take(5)
     if rnd == 0:
         sx_t, mh_t = take(2)
     uh, hh, u1, u1h, w1, h_t = take(6)
     if last:
-        u2, hits = take(2)
+        u2, w2 = take(2)
     odd = parity_ref[0] == 1
 
     def lower(k):
@@ -272,71 +273,83 @@
     if last:
         for q in range(6):
             u_out[q] = u2[every(q), :]
-        partial_gaps(count_ref, place_ref, own, peer, normal, before, w2, g_out, hits)
+            v_out[q] = w2[every(q), :] / step_size(count_ref)[0:1]
+        partial_gaps(place_ref, pick, share, v_out, g_out)
         return
     inner_pass(a_ref, si_t, e_t, m_t, u2, w2, ei_out, h_t)
     send_edges(odd, u2, h_t, x_msg, d_msg)
 
 
-def node_of(index):
-    plane = index // (ROWS * COLS)
-    row = (index // COLS) % ROWS
-    return plane, pl.ds(pl.multiple_of(row * 8, 8), 8), index % COLS
-
-
-def node_hits(plane, col):
-    sub = lax.broadcasted_iota(jnp.int32, (8, COLS), 0)
-    lane = lax.broadcasted_iota(jnp.int32, (8, COLS), 1)
-    return [(sub == 2 * c + plane) & (lane == col) for c in range(3)]
-
-
-def partial_gaps(count_ref, place_ref, own, peer, normal, before, w_in, g_out, hits):
-    dt = step_size(count_ref)
-    eighth = place_ref[0] % 8
+def thirds(x):
+    parts = []
+    for _ in range(3):
+        part = x.astype(jnp.bfloat16)
+        parts.append(part)
+        x = x - part.astype(F32)
+    return parts
+
+
+def chosen(onehot, values):
+    return sum(jnp.dot(onehot, part, preferred_element_type=F32) for part in thirds(values))
+
+
+def node_body(own, peer, normal, before, mass, pick, pick_t, share, change):
+    sub = lax.broadcasted_iota(jnp.int32, (16, 16), 0)
+    eye = sub == lax.broadcasted_iota(jnp.int32, (16, 16), 1)
+    lane = lax.broadcasted_iota(jnp.int32, (16, COLS), 1)
+    weights = jnp.concatenate([mass[0], mass[1]], 1)
+
+    def column(line):
+        return jnp.sum(jnp.where(eye, jnp.broadcast_to(line, (16, 16)), 0.0), axis=1, keepdims=True)
+
     for side, nodes, vec, sign in ((0, own, normal, 1.0), (1, peer, before, -1.0)):
-        for j in range(16):
-            plane, at, col = node_of(nodes[j])
-            value = w_in[at, :]
-            total = jnp.zeros((8, COLS), F32)
-            for c, hit in enumerate(node_hits(plane, col)):
-                total = jnp.where(hit, value * vec[c, j], total)
-            hits[side * 16 + j] = total
-        total = jnp.sum(hits[side * 16 : side * 16 + 16], axis=1)
-        total = jnp.sum(total, axis=1, keepdims=True) * (sign / dt[0:1, 0:1])
-        lane = lax.broadcasted_iota(jnp.int32, (16, COLS), 1)
-        sub = lax.broadcasted_iota(jnp.int32, (16, COLS), 0)
-        line = jnp.where(lane == sub + 16 * eighth, jnp.broadcast_to(total, (16, COLS)), 0.0)
-        line = jnp.sum(line, axis=0, keepdims=True)
-        g_out[:, side * COLS : (side + 1) * COLS] = jnp.broadcast_to(line, (128, COLS))
-
-
-def final_body(
-    count_ref, own, peer, normal, before, gathered, inv_own, inv_before, w_in, m_own,
-    v_out, work, mult,
-):
-    dt = step_size(count_ref)
+        at = slice(16 * side, 16 * side + 16)
+        index = column(nodes[...].astype(F32)).astype(jnp.int32)
+        plane = jnp.where(index >= ROWS * COLS, 1, 0)
+        rest = index - plane * (ROWS * COLS)
+        row = rest // COLS
+        col = rest - row * COLS
+        onehot = jnp.where(lane == row, 1.0, 0.0)
+        pick[at, :] = onehot[:, 0:ROWS].astype(jnp.bfloat16)
+        heavy = chosen(onehot[:, 0:ROWS].astype(jnp.bfloat16), weights)
+        hits = [(lane == col) & (plane == p) for p in range(2)]
+        total = jnp.where(hits[0], heavy[:, 0:COLS], 0.0) + jnp.where(hits[1], heavy[:, COLS:], 0.0)
+        total = jnp.sum(total, axis=1, keepdims=True)
+        for c in range(3):
+            value = sign * column(vec[c : c + 1, :])
+            for p in range(2):
+                q = 2 * c + p
+                part = jnp.where(hits[p], value, 0.0)
+                share[at, q * COLS : (q + 1) * COLS] = part
+                change[at, q * COLS : (q + 1) * COLS] = -part / total
+        pick_t[side] = jnp.transpose(onehot)[0:ROWS].astype(jnp.bfloat16)
+
+
+def partial_gaps(place_ref, pick, share, v, g_out):
+    values = jnp.concatenate([v[q] for q in range(6)], 1)
+    total = jnp.sum(chosen(pick[...], values) * share[...], axis=1, keepdims=True)
+    lane = lax.broadcasted_iota(jnp.int32, (32, COLS), 1)
+    sub = lax.broadcasted_iota(jnp.int32, (32, COLS), 0)
+    line = jnp.where(lane == sub % 16 + 16 * (place_ref[0] % 8), jnp.broadcast_to(total, (32, COLS)), 0.0)
+    for side in range(2):
+        part = jnp.sum(line[16 * side : 16 * side + 16], axis=0, keepdims=True)
+        g_out[:, side * COLS : (side + 1) * COLS] = jnp.broadcast_to(part, (128, COLS))
+
+
+def final_body(gathered, inv_own, inv_before, pick_t, change, v_in, v_out):
     mine = jnp.sum(gathered[:, 0:COLS].reshape(16, 8, COLS), axis=1)
     other = jnp.sum(gathered[:, COLS : 2 * COLS].reshape(16, 8, COLS), axis=1)
     gap = mine + jnp.concatenate([other[4:16], other[0:4]], 0)
+    total = None
     for side, rows in ((0, inv_own), (1, inv_before)):
         acc = jnp.zeros((16, COLS), F32)
         for k in range(16):
             acc = acc + rows[:, k * COLS : (k + 1) * COLS] * gap[k : k + 1, :]
         lam = jnp.sum(acc, axis=1, keepdims=True)
-        mult[side * 16 : side * 16 + 16, :] = jnp.broadcast_to(lam, (16, COLS))
-    work[...] = w_in[...]
-    for side, nodes, vec, sign in ((0, own, normal, -1.0), (1, peer, before, 1.0)):
-        for j in range(16):
-            plane, at, col = node_of(nodes[j])
-            k = side * 16 + j
-            value = work[at, :]
-            change = m_own[at, :] * (mult[k : k + 1, :] * (sign / dt[0:1]))
-            for c, hit in enumerate(node_hits(plane, col)):
-                value = jnp.where(hit, value + change * vec[c, j], value)
-            work[at, :] = value
-    back = 1.0 / dt[0:1]
+        part = chosen(pick_t[side], change[16 * side : 16 * side + 16, :] * lam)
+        total = part if total is None else total + part
     for q in range(6):
-        v_out[q] = work[every(q), :] * back
+        v_out[q] = v_in[q] + total[:, q * COLS : (q + 1) * COLS]
 
 
 def call(body, outs, scratch, ins, limit=24 * 1024 * 1024):
@@ -356,6 +369,10 @@
 ACROSS = [(i, i + 1) for i in range(1, 31, 2)] + [(i + 1, i) for i in range(1, 31, 2)]
 WITHIN = [(i, i ^ 1) for i in range(32)]
 FROM_BEFORE = [(i, (i + 1) % 4) for i in range(4)]
+
+
+def far(x):
+    return pltpu.with_memory_space_constraint(jnp.asarray(x), pltpu.HBM)
 
 
 def on_device(
@@ -369,8 +386,6 @@
     scale = elem_scale[0]
     place = lax.axis_index("dom").reshape(1)
     parity = place % 2
-    own = own_nodes[0]
-    peer = peer_nodes[0]
     normal = normals[0]
 
     first = (8, ROWS, COLS)
@@ -384,7 +399,7 @@
             TILE, pltpu.SemaphoreType.DMA((9,)),
         ],
         [SM] * 2 + [HBM] * 9,
-    )(substeps, parity, stiffness[0], PICK_ROW, PICK_COL, KEEP, field, scale, speed, weight, loads)
+    )(substeps, parity, *(far(v) for v in (stiffness[0], PICK_ROW, PICK_COL, KEEP, field, scale, speed, weight, loads)))
     inv_before = before = None
     for rnd in range(ROUNDS):
         x = lax.ppermute(x, "dom", ACROSS)
@@ -393,30 +408,38 @@
             inv_before = lax.ppermute(schur_inverse, "grp", FROM_BEFORE)
             before = lax.ppermute(normal, "grp", FROM_BEFORE)
             x, d, inv_before, before = lax.optimization_barrier((x, d, inv_before, before))
+        if rnd == 1:
+            b16 = lambda *shape: jax.ShapeDtypeStruct(shape, jnp.bfloat16)
+            nodes = call(
+                node_body, [b16(32, ROWS), b16(2, ROWS, 16), (32, 6 * COLS), (32, 6 * COLS)], [], [VM] * 5
+            )(own_nodes, peer_nodes, normal, before, weight)
+            x, d, *nodes = lax.optimization_barrier((x, d, *nodes))
+            pick, pick_t, share, change = nodes
         last = rnd == ROUNDS - 1
         args = [substeps, parity]
         if last:
-            args += [place, own, peer, normal, before]
+            args += [place]
         scalars = len(args)
         args += [x, d, u, w, e, m, ei, si, a]
         args += [scale] if rnd == 0 else [sx, mh]
-        outs = [PLANES, TILE, (128, 2 * COLS)] if last else [PLANES, PLANES, TILE, TILE, TILE]
+        args += [pick, share] if last else []
+        outs = [PLANES, PLANES, (128, 2 * COLS)] if last else [PLANES, PLANES, TILE, TILE, TILE]
         outs += [TILE, TILE] if rnd == 0 else []
-        scratch = [TILE] * 6 + ([TILE, (32, 8, COLS)] if last else [])
+        scratch = [TILE] * (8 if last else 6)
 
         def body(*refs, rnd=rnd):
             return round_body(rnd, *refs)
 
         got = call(body, outs, scratch, [SM] * scalars + [VM] * (len(args) - scalars))(*args)
         if last:
-            u, w, gap = got
+            u, v, gap = got
         else:
             x, d, u, w, ei = got[:5]
         if rnd == 0:
             sx, mh = got[5:]
     gathered = lax.all_to_all(gap, ("grp", "dom"), 0, 0, tiled=True)
-    (v,) = call(final_body, [PLANES], [TILE, (32, COLS)], [SM] * 5 + [VM] * 5)(
-        substeps, own, peer, normal, before, gathered, schur_inverse, inv_before, w, m
+    (v,) = call(final_body, [PLANES], [], [VM] * 6)(
+        gathered, schur_inverse, inv_before, pick_t, change, v
     )
     shape = displacement.shape
     return u.reshape(shape), v.reshape(shape)

time: 89.9 us -> 80.6 us (0.90)
  local copies, waits for them, and re-layouts: 8.18 us -> 0.18 us
    unnamed x30 -> x14, local copies, waits for them, and re-layouts: 8.04 us -> 0.04 us
    pallas_call x4, Pallas kernels: 13.7 us -> 12.6 us  [on_device(): call(body, outs, scratch, [SM] * scalars + [VM] * (len(args) - scalars))]
    pallas_call x1 -> x2, Pallas kernels: 1.88 us -> 1.57 us  [the longest x1 1.21 us: on_device(): call(final_body, [PLANES], [], [VM] * 6)]
where the time goes in v4:
time: 80.6 us; the launch traced here: 80.3 us
  blocking collectives  26.6 us (33%)
  starting transfers between devices  19.3 us (24%)
  Pallas kernels  17 us (21%)
  waiting for transfers between devices  15.8 us (20%)
  between operations  1.49 us (2%)
    all_to_all x1, blocking collectives, on_device(): gathered = lax.all_to_all(gap, ('grp', 'dom'), 0, 0, tiled=True)  26.6 us
    ppermute x4, starting transfers between devices, on_device(): x = lax.ppermute(x, 'dom', ACROSS)  16.2 us
    pallas_call x4, Pallas kernels, on_device(): call(body, outs, scratch, [SM] * scalars + [VM] * (len(args) - scalars))  12.6 us
    ppermute x4, waiting for transfers between devices, on_device(): x = lax.ppermute(x, 'dom', ACROSS)  12.3 us
    ppermute x1, waiting for transfers between devices, on_device(): before = lax.ppermute(normal, 'grp', FROM_BEFORE)  3.45 us
    pallas_call x1, Pallas kernels, on_device(): call(prep_body, [first, first, TILE, TILE, TILE, TILE, TILE, TILE, weight...  2.84 us
  transfers between devices with their start and end apart: 10, of which 4 were waited for; matrix products, arithmetic and copies ran while one was open for 0% of the time, Pallas kernels for 0%

profile of v4, /device:TPU:1, one launch (start us, length us, event | category | flops | bytes accessed | tf_op | source)
XLA Modules:
  0.0 80.3 jit_solution(14773654667026567347)
XLA Ops:
  1.3 2.8 %shard_map.149 = (f32[8,96,128]{2,1,0:T(8,128)S(1)}, f32[8,96,128]{2,1,0:T(8,128)S(1)}, f32[768,128]{1,0:T(8,128)S(1)}, f32[768,128]{1,0:T(8,128)S(1)}, f32[768,...) custom-call(s32[1]{0:T(128)S(6)} %copy.23.count_ref.refs_0_, ...), custom_call_target="tpu_custom_call" | custom-call | tf_op jit(solution)/shard_map/pallas_call | solution.py:394
  4.2 0.0 copy-start.5
  4.2 4.6 %collective-permute-start = (f32[8,96,128]{2,1,0:T(8,128)S(1)}, f32[8,96,128]{2,1,0:T(8,128)S(1)}, u32[]{:S(2)}, u32[]{:S(2)}) collective-permute-start(f32[8,96,128]{2,1,0:T(8,128)S(1)} %get-tuple-element.45), channel_id=1, source_target_pairs={{1,2},{3,4},{5,6},{7,8},{9,10},{11,12},{13,14},{15,16},{17,18},{19... | collective-permute-start | bytes 1179656 | tf_op jit(solution)/shard_map/ppermute | solution.py:405
  8.8 0.1 collective-permute-start.1
  8.9 1.3 %collective-permute-start.2 = (f32[16,2048]{1,0:T(8,128)S(1)}, f32[16,2048]{1,0:T(8,128)S(1)}, u32[]{:S(2)}, u32[]{:S(2)}) collective-permute-start(f32[16,2048]{1,0:T(8,128)S(1)} %copy-done.2), channel_id=1, source_target_pairs={{0,32},{32,64},{64,96},{96,0},{1,33},{33,65},{65,97},{97,1},{2,34}... | collective-permute-start | bytes 393224 | tf_op jit(solution)/shard_map/ppermute | solution.py:408
  10.1 1.2 %collective-permute-start.3 = (f32[3,16]{1,0:T(4,128)S(1)}, f32[3,16]{1,0:T(4,128)S(1)}, u32[]{:S(2)}, u32[]{:S(2)}) collective-permute-start(f32[3,16]{1,0:T(4,128)S(1)} %bitcast.22), channel_id=1, source_target_pairs={{0,32},{32,64},{64,96},{96,0},{1,33},{33,65},{65,97},{97,1},{2,34}... | collective-permute-start | bytes 584 | tf_op jit(solution)/shard_map/ppermute | solution.py:409
  11.4 3.5 %collective-permute-done.3.before = f32[3,16]{1,0:T(4,128)S(1)} collective-permute-done((f32[3,16]{1,0:T(4,128)S(1)}, f32[3,16]{1,0:T(4,128)S(1)}, u32[]{:S(2)}, u32[]{:S(2)}) %collective-permute-start.3) | collective-permute-done | bytes 224 | tf_op jit(solution)/shard_map/ppermute | solution.py:409
  14.8 0.0 collective-permute-done.2.inv_before
  14.8 0.0 collective-permute-done.refs_2_
  14.8 0.0 collective-permute-done.1.refs_3_
  14.8 0.0 copy-start.1
  14.8 3.2 %shard_map.150 = (f32[6,96,128]{2,1,0:T(8,128)S(1)}, f32[6,96,128]{2,1,0:T(8,128)S(1)}, f32[768,128]{1,0:T(8,128)S(1)}, f32[768,128]{1,0:T(8,128)S(1)}, f32[768,...) custom-call(s32[1]{0:T(128)S(6)} %copy.23.count_ref.refs_0_, s32[1]{0:T(128)S(6)} %select_n.7.parity_ref.refs_1_, ...), custom_call_target="tpu_custom_call" | custom-call | tf_op jit(solution)/shard_map/pallas_call | solution.py:433
  18.0 0.0 copy-start.3
  18.1 0.0 copy-start.4
  18.1 4.4 %collective-permute-start.4 = (f32[6,96,128]{2,1,0:T(8,128)S(1)}, f32[6,96,128]{2,1,0:T(8,128)S(1)}, u32[]{:S(2)}, u32[]{:S(2)}) collective-permute-start(f32[6,96,128]{2,1,0:T(8,128)S(1)} %get-tuple-element.56), channel_id=1, source_target_pairs={{1,2},{3,4},{5,6},{7,8},{9,10},{11,12},{13,14},{15,16},{17,18},{19... | collective-permute-start | bytes 884744 | tf_op jit(solution)/shard_map/ppermute | solution.py:405
  22.5 0.1 collective-permute-start.5
  22.6 0.4 shard_map.151
  22.9 3.9 %collective-permute-done.4.refs_2_ = f32[6,96,128]{2,1,0:T(8,128)S(1)} collective-permute-done((f32[6,96,128]{2,1,0:T(8,128)S(1)}, f32[6,96,128]{2,1,0:T(8,128)S(1)}, u32[]{:S(2)}, u32[]{:S(2)}) %collective-permute-start.4) | collective-permute-done | bytes 294944 | tf_op jit(solution)/shard_map/ppermute | solution.py:405
  26.8 0.0 collective-permute-done.5.refs_3_
  26.8 3.1 %shard_map.152 = (f32[6,96,128]{2,1,0:T(8,128)S(1)}, f32[6,96,128]{2,1,0:T(8,128)S(1)}, f32[768,128]{1,0:T(8,128)S(1)}, f32[768,128]{1,0:T(8,128)S(1)}, f32[768,128]{1,0:T(8,128)S(1)}) custom-call(s32[1]{0:T(128)S(6)} %copy.23.count_ref.refs_0_, s32[1]{0:T(128)S(6)} %select_n.7.parity_ref.refs_1_, f32[6,96,128]{2,1,0:T(8,128)S(1)} %collective-permute-done.4.refs_2_, ...), custom_call_target="tpu_custom_call" | custom-call | tf_op jit(solution)/shard_map/pallas_call | solution.py:433
  30.0 3.6 %collective-permute-start.6 = (f32[6,96,128]{2,1,0:T(8,128)S(1)}, f32[6,96,128]{2,1,0:T(8,128)S(1)}, u32[]{:S(2)}, u32[]{:S(2)}) collective-permute-start(f32[6,96,128]{2,1,0:T(8,128)S(1)} %get-tuple-element.70), channel_id=1, source_target_pairs={{1,2},{3,4},{5,6},{7,8},{9,10},{11,12},{13,14},{15,16},{17,18},{19... | collective-permute-start | bytes 884744 | tf_op jit(solution)/shard_map/ppermute | solution.py:405
  33.6 0.1 collective-permute-start.7
  33.7 4.3 %collective-permute-done.6.refs_2_ = f32[6,96,128]{2,1,0:T(8,128)S(1)} collective-permute-done((f32[6,96,128]{2,1,0:T(8,128)S(1)}, f32[6,96,128]{2,1,0:T(8,128)S(1)}, u32[]{:S(2)}, u32[]{:S(2)}) %collective-permute-start.6) | collective-permute-done | bytes 294944 | tf_op jit(solution)/shard_map/ppermute | solution.py:405
  38.0 0.0 collective-permute-done.7.refs_3_
  38.0 3.1 %shard_map.153 = (f32[6,96,128]{2,1,0:T(8,128)S(1)}, f32[6,96,128]{2,1,0:T(8,128)S(1)}, f32[768,128]{1,0:T(8,128)S(1)}, f32[768,128]{1,0:T(8,128)S(1)}, f32[768,128]{1,0:T(8,128)S(1)}) custom-call(s32[1]{0:T(128)S(6)} %copy.23.count_ref.refs_0_, s32[1]{0:T(128)S(6)} %select_n.7.parity_ref.refs_1_, f32[6,96,128]{2,1,0:T(8,128)S(1)} %collective-permute-done.6.refs_2_, ...), custom_call_target="tpu_custom_call" | custom-call | tf_op jit(solution)/shard_map/pallas_call | solution.py:433
  41.1 3.6 %collective-permute-start.8 = (f32[6,96,128]{2,1,0:T(8,128)S(1)}, f32[6,96,128]{2,1,0:T(8,128)S(1)}, u32[]{:S(2)}, u32[]{:S(2)}) collective-permute-start(f32[6,96,128]{2,1,0:T(8,128)S(1)} %get-tuple-element.75), channel_id=1, source_target_pairs={{1,2},{3,4},{5,6},{7,8},{9,10},{11,12},{13,14},{15,16},{17,18},{19... | collective-permute-start | bytes 884744 | tf_op jit(solution)/shard_map/ppermute | solution.py:405
  44.7 0.3 collective-permute-start.9
  45.0 4.1 %collective-permute-done.8.refs_3_ = f32[6,96,128]{2,1,0:T(8,128)S(1)} collective-permute-done((f32[6,96,128]{2,1,0:T(8,128)S(1)}, f32[6,96,128]{2,1,0:T(8,128)S(1)}, u32[]{:S(2)}, u32[]{:S(2)}) %collective-permute-start.8) | collective-permute-done | bytes 294944 | tf_op jit(solution)/shard_map/ppermute | solution.py:405
  49.1 3.2 %shard_map.154 = (f32[6,96,128]{2,1,0:T(8,128)}, f32[6,96,128]{2,1,0:T(8,128)S(1)}, f32[128,256]{1,0:T(8,128)S(1)}) custom-call(s32[1]{0:T(128)S(6)} %copy.23.count_ref.refs_0_, s32[1]{0:T(128)S(6)} %select_n.7.parity_ref.refs_1_, s32[1]{0:T(128)} %bitcast.refs_2_, f32[6,96,128]{2,1,0:T(8,128)S(1)} %collective-permute-done.8.refs_3_, ...), custom_call_target="tpu_custom_call" | custom-call | tf_op jit(solution)/shard_map/pallas_call | solution.py:433
  52.4 0.1 copy.16
  52.5 26.6 %all_to_all.11 = f32[128,1,256]{2,1,0:T(1,128)S(1)} all-to-all(f32[128,1,256]{2,1,0:T(1,128)S(1)} %copy.16), channel_id=1, replica_groups=mesh['grp'=4,'dom'=32] {'grp','dom'}, dimensions={0} | all-to-all | bytes 262144 | tf_op jit(solution)/shard_map/all_to_all | solution.py:440
  79.1 1.2 %shard_map.155 = f32[6,96,128]{2,1,0:T(8,128)} custom-call(f32[128,256]{1,0:T(8,128)S(1)} %bitcast.16, f32[16,2048]{1,0:T(8,128)S(1)} %copy-done.2, f32[16,2048]{1,0:T(8,128)S(1)} %collective-permute-done.2.inv_before, bf16[2,96,16]{2,1,0:T(8,128)(2,1)S(1)} %get-tuple-element.85.pick_t, f32[32,768]{1,0:T(8,128)S(1)} %get-tuple-element.86.change, ...), custom_call_target="tpu_custom_call" | custom-call | tf_op jit(solution)/shard_map/pallas_call | solution.py:441
  (11 shorter events, 0.0 us)
Async XLA Ops:
  1.3 7.6 %copy-start.2 = (f32[16,2048]{1,0:T(8,128)S(1)}, f32[16,2048]{1,0:T(8,128)}, u32[]{:S(2)}) copy-start(f32[16,2048]{1,0:T(8,128)} %inv_own.1) | copy-start | bytes 393220
  1.3 13.5 %copy-start = (f32[1,2,96,128]{3,2,1,0:T(8,128)S(1)}, f32[1,2,96,128]{3,2,1,0:T(8,128)}, u32[]{:S(2)}) copy-start(f32[1,2,96,128]{3,2,1,0:T(8,128)} %param.18) | copy-start | bytes 294916
  4.2 6.0 %copy-start.5 = (f32[1,3,16]{2,0,1:T(1,128)S(1)}, f32[1,3,16]{2,0,1:T(1,128)}, u32[]{:S(2)}) copy-start(f32[1,3,16]{2,0,1:T(1,128)} %param.23) | copy-start | bytes 580
  4.2 10.7 %collective-permute-start = (f32[8,96,128]{2,1,0:T(8,128)S(1)}, f32[8,96,128]{2,1,0:T(8,128)S(1)}, u32[]{:S(2)}, u32[]{:S(2)}) collective-permute-start(f32[8,96,128]{2,1,0:T(8,128)S(1)} %get-tuple-element.45), channel_id=1, source_target_pairs={{1,2},{3,4},{5,6},{7,8},{9,10},{11,12},{13,14},{15,16},{17,18},{19... | collective-permute-start | bytes 1179656 | tf_op jit(solution)/shard_map/ppermute | solution.py:405
  8.8 6.1 %collective-permute-start.1 = (f32[8,96,128]{2,1,0:T(8,128)S(1)}, f32[8,96,128]{2,1,0:T(8,128)S(1)}, u32[]{:S(2)}, u32[]{:S(2)}) collective-permute-start(f32[8,96,128]{2,1,0:T(8,128)S(1)} %get-tuple-element.46), channel_id=1, source_target_pairs={{0,1},{1,0},{2,3},{3,2},{4,5},{5,4},{6,7},{7,6},{8,9},{9,8},{10,11... | collective-permute-start | bytes 1179656 | tf_op jit(solution)/shard_map/ppermute | solution.py:406
  8.9 6.0 %collective-permute-start.2 = (f32[16,2048]{1,0:T(8,128)S(1)}, f32[16,2048]{1,0:T(8,128)S(1)}, u32[]{:S(2)}, u32[]{:S(2)}) collective-permute-start(f32[16,2048]{1,0:T(8,128)S(1)} %copy-done.2), channel_id=1, source_target_pairs={{0,32},{32,64},{64,96},{96,0},{1,33},{33,65},{65,97},{97,1},{2,34}... | collective-permute-start | bytes 393224 | tf_op jit(solution)/shard_map/ppermute | solution.py:408
  10.1 4.7 %collective-permute-start.3 = (f32[3,16]{1,0:T(4,128)S(1)}, f32[3,16]{1,0:T(4,128)S(1)}, u32[]{:S(2)}, u32[]{:S(2)}) collective-permute-start(f32[3,16]{1,0:T(4,128)S(1)} %bitcast.22), channel_id=1, source_target_pairs={{0,32},{32,64},{64,96},{96,0},{1,33},{33,65},{65,97},{97,1},{2,34}... | collective-permute-start | bytes 584 | tf_op jit(solution)/shard_map/ppermute | solution.py:409
  14.8 7.7 %copy-start.1 = (f32[1,2,96,128]{3,2,1,0:T(8,128)S(1)}, f32[1,2,96,128]{3,2,1,0:T(8,128)}, u32[]{:S(2)}) copy-start(f32[1,2,96,128]{3,2,1,0:T(8,128)} %param.17) | copy-start | bytes 294916
  18.0 4.5 %copy-start.3 = (s32[1,16]{1,0:T(1,128)S(1)}, s32[1,16]{1,0:T(1,128)}, u32[]{:S(2)}) copy-start(s32[1,16]{1,0:T(1,128)} %own.1) | copy-start | bytes 196
  18.1 4.5 %copy-start.4 = (s32[1,16]{1,0:T(1,128)S(1)}, s32[1,16]{1,0:T(1,128)}, u32[]{:S(2)}) copy-start(s32[1,16]{1,0:T(1,128)} %peer.1) | copy-start | bytes 196
  18.1 8.8 %collective-permute-start.4 = (f32[6,96,128]{2,1,0:T(8,128)S(1)}, f32[6,96,128]{2,1,0:T(8,128)S(1)}, u32[]{:S(2)}, u32[]{:S(2)}) collective-permute-start(f32[6,96,128]{2,1,0:T(8,128)S(1)} %get-tuple-element.56), channel_id=1, source_target_pairs={{1,2},{3,4},{5,6},{7,8},{9,10},{11,12},{13,14},{15,16},{17,18},{19... | collective-permute-start | bytes 884744 | tf_op jit(solution)/shard_map/ppermute | solution.py:405
  22.5 4.4 %collective-permute-start.5 = (f32[6,96,128]{2,1,0:T(8,128)S(1)}, f32[6,96,128]{2,1,0:T(8,128)S(1)}, u32[]{:S(2)}, u32[]{:S(2)}) collective-permute-start(f32[6,96,128]{2,1,0:T(8,128)S(1)} %get-tuple-element.57), channel_id=1, source_target_pairs={{0,1},{1,0},{2,3},{3,2},{4,5},{5,4},{6,7},{7,6},{8,9},{9,8},{10,11... | collective-permute-start | bytes 884744 | tf_op jit(solution)/shard_map/ppermute | solution.py:406
  30.0 8.0 %collective-permute-start.6 = (f32[6,96,128]{2,1,0:T(8,128)S(1)}, f32[6,96,128]{2,1,0:T(8,128)S(1)}, u32[]{:S(2)}, u32[]{:S(2)}) collective-permute-start(f32[6,96,128]{2,1,0:T(8,128)S(1)} %get-tuple-element.70), channel_id=1, source_target_pairs={{1,2},{3,4},{5,6},{7,8},{9,10},{11,12},{13,14},{15,16},{17,18},{19... | collective-permute-start | bytes 884744 | tf_op jit(solution)/shard_map/ppermute | solution.py:405
  33.6 4.4 %collective-permute-start.7 = (f32[6,96,128]{2,1,0:T(8,128)S(1)}, f32[6,96,128]{2,1,0:T(8,128)S(1)}, u32[]{:S(2)}, u32[]{:S(2)}) collective-permute-start(f32[6,96,128]{2,1,0:T(8,128)S(1)} %get-tuple-element.71), channel_id=1, source_target_pairs={{0,1},{1,0},{2,3},{3,2},{4,5},{5,4},{6,7},{7,6},{8,9},{9,8},{10,11... | collective-permute-start | bytes 884744 | tf_op jit(solution)/shard_map/ppermute | solution.py:406
  41.1 8.0 %collective-permute-start.8 = (f32[6,96,128]{2,1,0:T(8,128)S(1)}, f32[6,96,128]{2,1,0:T(8,128)S(1)}, u32[]{:S(2)}, u32[]{:S(2)}) collective-permute-start(f32[6,96,128]{2,1,0:T(8,128)S(1)} %get-tuple-element.75), channel_id=1, source_target_pairs={{1,2},{3,4},{5,6},{7,8},{9,10},{11,12},{13,14},{15,16},{17,18},{19... | collective-permute-start | bytes 884744 | tf_op jit(solution)/shard_map/ppermute | solution.py:405
  44.7 4.4 %collective-permute-start.9 = (f32[6,96,128]{2,1,0:T(8,128)S(1)}, f32[6,96,128]{2,1,0:T(8,128)S(1)}, u32[]{:S(2)}, u32[]{:S(2)}) collective-permute-start(f32[6,96,128]{2,1,0:T(8,128)S(1)} %get-tuple-element.76), channel_id=1, source_target_pairs={{0,1},{1,0},{2,3},{3,2},{4,5},{5,4},{6,7},{7,6},{8,9},{9,8},{10,11... | collective-permute-start | bytes 884744 | tf_op jit(solution)/shard_map/ppermute | solution.py:406

commit v5 on v4

--- a/solution.py
+++ b/solution.py
@@ -8,6 +8,8 @@
 
 MAXSUB = 8
 ROUNDS = MAXSUB // 2
+GROUPS = 4
+DOMS = 32
 COARSE = 0.4
 ROWS = 96
 HALF = ROWS // 2
@@ -107,21 +109,22 @@
 
 def inner_rows(own):
     def rows(r):
-        parts = split(jnp.concatenate([own[tile(r), :], own[tile((r + 1) % ROWS), :]], 0))
+        here, there = tile(r % ROWS), tile((r + 1) % ROWS)
+        parts = split(jnp.concatenate([own[here, :], own[there, :]], 0))
         pad = jnp.zeros((32, COLS), jnp.bfloat16)
         return jnp.concatenate(parts + parts[:2] + [pad], 0)
 
     return rows
 
 
-def sweep(rows, lhs, blocks, finish):
+def sweep(start, rows, lhs, blocks, finish):
     carry = {}
     first = {}
-    for i in range(HALF):
+    for i in range(start, start + HALF):
         rhs = jnp.concatenate([rows(i), rows(i + HALF)], 1)
         out = jnp.dot(lhs, rhs, preferred_element_type=F32)
         for h in range(2):
-            r = i + h * HALF
+            r = (i + h * HALF) % ROWS
             for n, terms in enumerate(blocks):
                 part = []
                 for b in range(2):
@@ -134,14 +137,14 @@
                             total = term if total is None else total + term
                         g.append(total)
                     part.append(g[0] + lane_down(g[1]))
-                if i == 0:
+                if i == start:
                     first[h, n] = part[0]
                 else:
                     finish(n, r, part[0] + carry[h, n])
                 carry[h, n] = part[1]
     for n in range(len(blocks)):
-        finish(n, 0, first[0, n] + carry[1, n])
-        finish(n, HALF, first[1, n] + carry[0, n])
+        finish(n, start, first[0, n] + carry[1, n])
+        finish(n, start + HALF, first[1, n] + carry[0, n])
 
 
 def inner_pass(a_ref, si, e, m, u, w, ei_out, h_out):
@@ -151,7 +154,7 @@
         ei_out[at, :] = rest
         h_out[at, :] = u[at, :] + (w[at, :] + rest)
 
-    sweep(inner_rows(u), a_ref[0:32, STEP_K:], [[(0, si)]], finish)
+    sweep(2, inner_rows(u), a_ref[0:32, STEP_K:], [[(0, si)]], finish)
 
 
 def send_edges(odd, u, h, x_msg, d_msg):
@@ -163,7 +166,7 @@
 
 
 def prep_body(
-    count_ref, parity_ref, kmat_h, row_h, col_h, keep_h, u_h, scale_h, v_h, mass_h, ext_h,
+    count_ref, place_ref, kmat_h, row_h, col_h, keep_h, u_h, scale_h, v_h, mass_h, ext_h,
     x_msg, d_msg, u_t, w_t, e_t, m_t, ei_t, si_t, a_out,
     kmat, row, col, keep, u_n, scale, v_n, mass, ext_n, h_t, sems,
 ):
@@ -176,7 +179,7 @@
         copy.start()
     for copy in copies:
         copy.wait()
-    odd = parity_ref[0] == 1
+    odd = place_ref[0] % 2 == 1
     dt = step_size(count_ref)[0:1]
     high = lax.Precision.HIGHEST
     rows = jnp.dot(row[...], kmat[...], precision=high, preferred_element_type=F32)
@@ -210,10 +213,8 @@
 def round_body(rnd, *refs):
     refs = list(refs)
     take = lambda n: [refs.pop(0) for _ in range(n)]
-    count_ref, parity_ref = take(2)
+    count_ref, place_ref = take(2)
     last = rnd == ROUNDS - 1
-    if last:
-        (place_ref,) = take(1)
     x_in, d_in, u_t, w_t, e_t, m_t, ei_t, si_t, a_ref = take(9)
     if rnd == 0:
         (scale,) = take(1)
@@ -229,13 +230,18 @@
     uh, hh, u1, u1h, w1, h_t = take(6)
     if last:
         u2, w2 = take(2)
-    odd = parity_ref[0] == 1
+    place = place_ref[0]
+    odd = place % 2 == 1
+    inside = (place > 0) & (place < DOMS - 1)
+
+    def across(k):
+        return jnp.where(inside, x_in[k], 0.0)
 
     def lower(k):
-        return jnp.where(odd, d_in[k], x_in[k])
+        return jnp.where(odd, d_in[k], across(k))
 
     def upper(k):
-        return jnp.where(odd, x_in[k], d_in[k])
+        return jnp.where(odd, across(k), d_in[k])
 
     blank = jnp.zeros((ROWS, COLS), F32)
     for q in (6, 7):
@@ -261,7 +267,7 @@
             before = uh[at, :]
             u1h[at, :] = before + act[0] * ((hh[at, :] - mh_t[at, :] * force) - before)
 
-    sweep(step_rows(u_t, uh), a_ref[32:96, 0:STEP_K], [[(0, sx_t)], [(32, sx_t)]], finish_first)
+    sweep(0, step_rows(u_t, uh), a_ref[32:96, 0:STEP_K], [[(0, sx_t)], [(32, sx_t)]], finish_first)
 
     def finish_second(n, r, force):
         at = tile(r)
@@ -269,7 +275,7 @@
         w2[at, :] = w
         u2[at, :] = u1[at, :] + act[1] * w
 
-    sweep(step_rows(u1, u1h), a_ref[0:64, 0:STEP_K], [[(0, si_t), (32, sx_t)]], finish_second)
+    sweep(1, step_rows(u1, u1h), a_ref[0:64, 0:STEP_K], [[(0, si_t), (32, sx_t)]], finish_second)
     if last:
         for q in range(6):
             u_out[q] = u2[every(q), :]
@@ -366,7 +372,17 @@
 TILE = (ROWS * 8, COLS)
 PLANES = (6, ROWS, COLS)
 WIDTH = STEP_K + INNER_K
-ACROSS = [(i, i + 1) for i in range(1, 31, 2)] + [(i + 1, i) for i in range(1, 31, 2)]
+
+
+def across_pairs():
+    pairs = [(g * DOMS + i, g * DOMS + i + 1) for g in range(GROUPS) for i in range(1, DOMS - 1, 2)]
+    for g in range(0, GROUPS, 2):
+        for i in (0, DOMS - 1):
+            pairs.append((g * DOMS + i, (g + 1) * DOMS + i))
+    return pairs + [(b, a) for a, b in pairs]
+
+
+ACROSS = across_pairs()
 WITHIN = [(i, i ^ 1) for i in range(32)]
 FROM_BEFORE = [(i, (i + 1) % 4) for i in range(4)]
 
@@ -385,7 +401,6 @@
     weight = mass[0]
     scale = elem_scale[0]
     place = lax.axis_index("dom").reshape(1)
-    parity = place % 2
     normal = normals[0]
 
     first = (8, ROWS, COLS)
@@ -399,10 +414,10 @@
             TILE, pltpu.SemaphoreType.DMA((9,)),
         ],
         [SM] * 2 + [HBM] * 9,
-    )(substeps, parity, *(far(v) for v in (stiffness[0], PICK_ROW, PICK_COL, KEEP, field, scale, speed, weight, loads)))
+    )(substeps, place, *(far(v) for v in (stiffness[0], PICK_ROW, PICK_COL, KEEP, field, scale, speed, weight, loads)))
     inv_before = before = None
     for rnd in range(ROUNDS):
-        x = lax.ppermute(x, "dom", ACROSS)
+        x = lax.ppermute(x, ("grp", "dom"), ACROSS)
         d = lax.ppermute(d, "dom", WITHIN)
         if rnd == 0:
             inv_before = lax.ppermute(schur_inverse, "grp", FROM_BEFORE)
@@ -416,9 +431,7 @@
             x, d, *nodes = lax.optimization_barrier((x, d, *nodes))
             pick, pick_t, share, change = nodes
         last = rnd == ROUNDS - 1
-        args = [substeps, parity]
-        if last:
-            args += [place]
+        args = [substeps, place]
         scalars = len(args)
         args += [x, d, u, w, e, m, ei, si, a]
         args += [scale] if rnd == 0 else [sx, mh]

time: 80.6 us -> 70.8 us (0.88)
  waiting for transfers between devices: 15.8 us -> 9.14 us
  Pallas kernels: 17 us -> 14.6 us
    ppermute x4, starting transfers between devices: 0.52 us -> 9.74 us  [on_device(): d = lax.ppermute(d, 'dom', WITHIN)]
    ppermute x4, starting transfers between devices: 16.2 us -> 7.56 us  [on_device(): x = lax.ppermute(x, ('grp', 'dom'), ACROSS)]
    ppermute x4, waiting for transfers between devices: 12.3 us -> 5.16 us  [on_device(): x = lax.ppermute(x, ('grp', 'dom'), ACROSS)]
    pallas_call x4, Pallas kernels: 12.6 us -> 10.2 us  [on_device(): call(body, outs, scratch, [SM] * scalars + [VM] * (len(args) - scalars))]
  transfers between devices with their start and end apart: 10 -> 10, of which waited for: 4 -> 4; matrix products, arithmetic and copies ran while one was open for 0% -> 0% of each run, Pallas kernels for 0% -> 1%
where the time goes in v5:
time: 70.8 us; the launch traced here: 70.7 us
  blocking collectives  25.9 us (37%)
  starting transfers between devices  19.4 us (27%)
  Pallas kernels  14.6 us (21%)
  waiting for transfers between devices  9.14 us (13%)
  between operations  1.39 us (2%)
    all_to_all x1, blocking collectives, on_device(): gathered = lax.all_to_all(gap, ('grp', 'dom'), 0, 0, tiled=True)  25.9 us
    pallas_call x4, Pallas kernels, on_device(): call(body, outs, scratch, [SM] * scalars + [VM] * (len(args) - scalars))  10.2 us
    ppermute x4, starting transfers between devices, on_device(): d = lax.ppermute(d, 'dom', WITHIN)  9.74 us
    ppermute x4, starting transfers between devices, on_device(): x = lax.ppermute(x, ('grp', 'dom'), ACROSS)  7.56 us
    ppermute x4, waiting for transfers between devices, on_device(): x = lax.ppermute(x, ('grp', 'dom'), ACROSS)  5.16 us
    ppermute x1, waiting for transfers between devices, on_device(): before = lax.ppermute(normal, 'grp', FROM_BEFORE)  3.97 us
    pallas_call x1, Pallas kernels, on_device(): call(prep_body, [first, first, TILE, TILE, TILE, TILE, TILE, TILE, weight...  2.83 us
  transfers between devices with their start and end apart: 10, of which 4 were waited for; matrix products, arithmetic and copies ran while one was open for 0% of the time, Pallas kernels for 1%

profile of v5, /device:TPU:1, one launch (start us, length us, event | category | flops | bytes accessed | tf_op | source)
XLA Modules:
  0.0 70.7 jit_solution(13401626023740232715)
XLA Ops:
  1.3 2.8 %shard_map.149 = (f32[8,96,128]{2,1,0:T(8,128)S(1)}, f32[8,96,128]{2,1,0:T(8,128)S(1)}, f32[768,128]{1,0:T(8,128)S(1)}, f32[768,128]{1,0:T(8,128)S(1)}, f32[768,...) custom-call(s32[1]{0:T(128)S(6)} %copy.23.count_ref.refs_0_, ...), custom_call_target="tpu_custom_call" | custom-call | tf_op jit(solution)/shard_map/pallas_call | solution.py:409
  4.1 0.0 copy-start.5
  4.2 2.8 %collective-permute-start = (f32[8,96,128]{2,1,0:T(8,128)S(1)}, f32[8,96,128]{2,1,0:T(8,128)S(1)}, u32[]{:S(2)}, u32[]{:S(2)}) collective-permute-start(f32[8,96,128]{2,1,0:T(8,128)S(1)} %get-tuple-element.45), channel_id=1, source_target_pairs={{1,2},{3,4},{5,6},{7,8},{9,10},{11,12},{13,14},{15,16},{17,18},{19... | collective-permute-start | bytes 1179656 | tf_op jit(solution)/shard_map/ppermute | solution.py:420
  6.9 0.3 collective-permute-start.1
  7.2 0.9 %collective-permute-start.2 = (f32[16,2048]{1,0:T(8,128)S(1)}, f32[16,2048]{1,0:T(8,128)S(1)}, u32[]{:S(2)}, u32[]{:S(2)}) collective-permute-start(f32[16,2048]{1,0:T(8,128)S(1)} %copy-done.2), channel_id=1, source_target_pairs={{0,32},{32,64},{64,96},{96,0},{1,33},{33,65},{65,97},{97,1},{2,34}... | collective-permute-start | bytes 393224 | tf_op jit(solution)/shard_map/ppermute | solution.py:423
  8.1 1.2 %collective-permute-start.3 = (f32[3,16]{1,0:T(4,128)S(1)}, f32[3,16]{1,0:T(4,128)S(1)}, u32[]{:S(2)}, u32[]{:S(2)}) collective-permute-start(f32[3,16]{1,0:T(4,128)S(1)} %bitcast.22), channel_id=1, source_target_pairs={{0,32},{32,64},{64,96},{96,0},{1,33},{33,65},{65,97},{97,1},{2,34}... | collective-permute-start | bytes 584 | tf_op jit(solution)/shard_map/ppermute | solution.py:424
  9.4 4.0 %collective-permute-done.3.before = f32[3,16]{1,0:T(4,128)S(1)} collective-permute-done((f32[3,16]{1,0:T(4,128)S(1)}, f32[3,16]{1,0:T(4,128)S(1)}, u32[]{:S(2)}, u32[]{:S(2)}) %collective-permute-start.3) | collective-permute-done | bytes 224 | tf_op jit(solution)/shard_map/ppermute | solution.py:424
  13.3 0.0 collective-permute-done.2.inv_before
  13.3 0.0 collective-permute-done.refs_2_
  13.3 0.0 collective-permute-done.1.refs_3_
  13.4 0.0 copy-start.1
  13.4 2.6 %shard_map.150 = (f32[6,96,128]{2,1,0:T(8,128)S(1)}, f32[6,96,128]{2,1,0:T(8,128)S(1)}, f32[768,128]{1,0:T(8,128)S(1)}, f32[768,128]{1,0:T(8,128)S(1)}, f32[768,...) custom-call(s32[1]{0:T(128)S(6)} %copy.23.count_ref.refs_0_, s32[1]{0:T(128)} %bitcast.place_ref.refs_1_, ...), custom_call_target="tpu_custom_call" | custom-call | tf_op jit(solution)/shard_map/pallas_call | solution.py:446
  15.9 0.0 copy-start.3
  16.0 0.0 copy-start.4
  16.0 2.0 %collective-permute-start.4 = (f32[6,96,128]{2,1,0:T(8,128)S(1)}, f32[6,96,128]{2,1,0:T(8,128)S(1)}, u32[]{:S(2)}, u32[]{:S(2)}) collective-permute-start(f32[6,96,128]{2,1,0:T(8,128)S(1)} %get-tuple-element.56), channel_id=1, source_target_pairs={{1,2},{3,4},{5,6},{7,8},{9,10},{11,12},{13,14},{15,16},{17,18},{19... | collective-permute-start | bytes 884744 | tf_op jit(solution)/shard_map/ppermute | solution.py:420
  18.0 2.6 %collective-permute-start.5 = (f32[6,96,128]{2,1,0:T(8,128)S(1)}, f32[6,96,128]{2,1,0:T(8,128)S(1)}, u32[]{:S(2)}, u32[]{:S(2)}) collective-permute-start(f32[6,96,128]{2,1,0:T(8,128)S(1)} %get-tuple-element.57), channel_id=1, source_target_pairs={{0,1},{1,0},{2,3},{3,2},{4,5},{5,4},{6,7},{7,6},{8,9},{9,8},{10,11... | collective-permute-start | bytes 884744 | tf_op jit(solution)/shard_map/ppermute | solution.py:421
  20.6 0.4 shard_map.151
  20.9 1.8 %collective-permute-done.4.refs_2_ = f32[6,96,128]{2,1,0:T(8,128)S(1)} collective-permute-done((f32[6,96,128]{2,1,0:T(8,128)S(1)}, f32[6,96,128]{2,1,0:T(8,128)S(1)}, u32[]{:S(2)}, u32[]{:S(2)}) %collective-permute-start.4) | collective-permute-done | bytes 294944 | tf_op jit(solution)/shard_map/ppermute | solution.py:420
  22.7 0.0 collective-permute-done.5.refs_3_
  22.7 2.5 %shard_map.152 = (f32[6,96,128]{2,1,0:T(8,128)S(1)}, f32[6,96,128]{2,1,0:T(8,128)S(1)}, f32[768,128]{1,0:T(8,128)S(1)}, f32[768,128]{1,0:T(8,128)S(1)}, f32[768,128]{1,0:T(8,128)S(1)}) custom-call(s32[1]{0:T(128)S(6)} %copy.23.count_ref.refs_0_, s32[1]{0:T(128)} %bitcast.place_ref.refs_1_, f32[6,96,128]{2,1,0:T(8,128)S(1)} %collective-permute-done.4.refs_2_, ...), custom_call_target="tpu_custom_call" | custom-call | tf_op jit(solution)/shard_map/pallas_call | solution.py:446
  25.2 1.5 %collective-permute-start.6 = (f32[6,96,128]{2,1,0:T(8,128)S(1)}, f32[6,96,128]{2,1,0:T(8,128)S(1)}, u32[]{:S(2)}, u32[]{:S(2)}) collective-permute-start(f32[6,96,128]{2,1,0:T(8,128)S(1)} %get-tuple-element.70), channel_id=1, source_target_pairs={{1,2},{3,4},{5,6},{7,8},{9,10},{11,12},{13,14},{15,16},{17,18},{19... | collective-permute-start | bytes 884744 | tf_op jit(solution)/shard_map/ppermute | solution.py:420
  26.7 3.1 %collective-permute-start.7 = (f32[6,96,128]{2,1,0:T(8,128)S(1)}, f32[6,96,128]{2,1,0:T(8,128)S(1)}, u32[]{:S(2)}, u32[]{:S(2)}) collective-permute-start(f32[6,96,128]{2,1,0:T(8,128)S(1)} %get-tuple-element.71), channel_id=1, source_target_pairs={{0,1},{1,0},{2,3},{3,2},{4,5},{5,4},{6,7},{7,6},{8,9},{9,8},{10,11... | collective-permute-start | bytes 884744 | tf_op jit(solution)/shard_map/ppermute | solution.py:421
  29.9 1.8 %collective-permute-done.6.refs_2_ = f32[6,96,128]{2,1,0:T(8,128)S(1)} collective-permute-done((f32[6,96,128]{2,1,0:T(8,128)S(1)}, f32[6,96,128]{2,1,0:T(8,128)S(1)}, u32[]{:S(2)}, u32[]{:S(2)}) %collective-permute-start.6) | collective-permute-done | bytes 294944 | tf_op jit(solution)/shard_map/ppermute | solution.py:420
  31.7 0.0 collective-permute-done.7.refs_3_
  31.7 2.5 %shard_map.153 = (f32[6,96,128]{2,1,0:T(8,128)S(1)}, f32[6,96,128]{2,1,0:T(8,128)S(1)}, f32[768,128]{1,0:T(8,128)S(1)}, f32[768,128]{1,0:T(8,128)S(1)}, f32[768,128]{1,0:T(8,128)S(1)}) custom-call(s32[1]{0:T(128)S(6)} %copy.23.count_ref.refs_0_, s32[1]{0:T(128)} %bitcast.place_ref.refs_1_, f32[6,96,128]{2,1,0:T(8,128)S(1)} %collective-permute-done.6.refs_2_, ...), custom_call_target="tpu_custom_call" | custom-call | tf_op jit(solution)/shard_map/pallas_call | solution.py:446
  34.2 1.2 %collective-permute-start.8 = (f32[6,96,128]{2,1,0:T(8,128)S(1)}, f32[6,96,128]{2,1,0:T(8,128)S(1)}, u32[]{:S(2)}, u32[]{:S(2)}) collective-permute-start(f32[6,96,128]{2,1,0:T(8,128)S(1)} %get-tuple-element.75), channel_id=1, source_target_pairs={{1,2},{3,4},{5,6},{7,8},{9,10},{11,12},{13,14},{15,16},{17,18},{19... | collective-permute-start | bytes 884744 | tf_op jit(solution)/shard_map/ppermute | solution.py:420
  35.5 3.7 %collective-permute-start.9 = (f32[6,96,128]{2,1,0:T(8,128)S(1)}, f32[6,96,128]{2,1,0:T(8,128)S(1)}, u32[]{:S(2)}, u32[]{:S(2)}) collective-permute-start(f32[6,96,128]{2,1,0:T(8,128)S(1)} %get-tuple-element.76), channel_id=1, source_target_pairs={{0,1},{1,0},{2,3},{3,2},{4,5},{5,4},{6,7},{7,6},{8,9},{9,8},{10,11... | collective-permute-start | bytes 884744 | tf_op jit(solution)/shard_map/ppermute | solution.py:421
  39.2 1.6 %collective-permute-done.8.refs_2_ = f32[6,96,128]{2,1,0:T(8,128)S(1)} collective-permute-done((f32[6,96,128]{2,1,0:T(8,128)S(1)}, f32[6,96,128]{2,1,0:T(8,128)S(1)}, u32[]{:S(2)}, u32[]{:S(2)}) %collective-permute-start.8) | collective-permute-done | bytes 294944 | tf_op jit(solution)/shard_map/ppermute | solution.py:420
  40.7 2.7 %shard_map.154 = (f32[6,96,128]{2,1,0:T(8,128)}, f32[6,96,128]{2,1,0:T(8,128)S(1)}, f32[128,256]{1,0:T(8,128)S(1)}) custom-call(s32[1]{0:T(128)S(6)} %copy.23.count_ref.refs_0_, s32[1]{0:T(128)} %bitcast.place_ref.refs_1_, f32[6,96,128]{2,1,0:T(8,128)S(1)} %collective-permute-done.8.refs_2_, f32[6,96,128]{2,1,0:T(8,128)S(1)} %collective-permute-done.9.refs_3_, ...), custom_call_target="tpu_custom_call" | custom-call | tf_op jit(solution)/shard_map/pallas_call | solution.py:446
  43.4 0.1 copy.16
  43.5 25.9 %all_to_all.11 = f32[128,1,256]{2,1,0:T(1,128)S(1)} all-to-all(f32[128,1,256]{2,1,0:T(1,128)S(1)} %copy.16), channel_id=1, replica_groups=mesh['grp'=4,'dom'=32] {'grp','dom'}, dimensions={0} | all-to-all | bytes 262144 | tf_op jit(solution)/shard_map/all_to_all | solution.py:453
  69.5 1.2 %shard_map.155 = f32[6,96,128]{2,1,0:T(8,128)} custom-call(f32[128,256]{1,0:T(8,128)S(1)} %bitcast.16, f32[16,2048]{1,0:T(8,128)S(1)} %copy-done.2, f32[16,2048]{1,0:T(8,128)S(1)} %collective-permute-done.2.inv_before, bf16[2,96,16]{2,1,0:T(8,128)(2,1)S(1)} %get-tuple-element.85.pick_t, f32[32,768]{1,0:T(8,128)S(1)} %get-tuple-element.86.change, ...), custom_call_target="tpu_custom_call" | custom-call | tf_op jit(solution)/shard_map/pallas_call | solution.py:454
  (11 shorter events, 0.0 us)
Async XLA Ops:
  1.3 5.9 %copy-start.2 = (f32[16,2048]{1,0:T(8,128)S(1)}, f32[16,2048]{1,0:T(8,128)}, u32[]{:S(2)}) copy-start(f32[16,2048]{1,0:T(8,128)} %inv_own.1) | copy-start | bytes 393220
  1.3 12.1 %copy-start = (f32[1,2,96,128]{3,2,1,0:T(8,128)S(1)}, f32[1,2,96,128]{3,2,1,0:T(8,128)}, u32[]{:S(2)}) copy-start(f32[1,2,96,128]{3,2,1,0:T(8,128)} %param.18) | copy-start | bytes 294916
  4.1 4.0 %copy-start.5 = (f32[1,3,16]{2,0,1:T(1,128)S(1)}, f32[1,3,16]{2,0,1:T(1,128)}, u32[]{:S(2)}) copy-start(f32[1,3,16]{2,0,1:T(1,128)} %param.23) | copy-start | bytes 580
  4.2 9.2 %collective-permute-start = (f32[8,96,128]{2,1,0:T(8,128)S(1)}, f32[8,96,128]{2,1,0:T(8,128)S(1)}, u32[]{:S(2)}, u32[]{:S(2)}) collective-permute-start(f32[8,96,128]{2,1,0:T(8,128)S(1)} %get-tuple-element.45), channel_id=1, source_target_pairs={{1,2},{3,4},{5,6},{7,8},{9,10},{11,12},{13,14},{15,16},{17,18},{19... | collective-permute-start | bytes 1179656 | tf_op jit(solution)/shard_map/ppermute | solution.py:420
  6.9 6.4 %collective-permute-start.1 = (f32[8,96,128]{2,1,0:T(8,128)S(1)}, f32[8,96,128]{2,1,0:T(8,128)S(1)}, u32[]{:S(2)}, u32[]{:S(2)}) collective-permute-start(f32[8,96,128]{2,1,0:T(8,128)S(1)} %get-tuple-element.46), channel_id=1, source_target_pairs={{0,1},{1,0},{2,3},{3,2},{4,5},{5,4},{6,7},{7,6},{8,9},{9,8},{10,11... | collective-permute-start | bytes 1179656 | tf_op jit(solution)/shard_map/ppermute | solution.py:421
  7.2 6.1 %collective-permute-start.2 = (f32[16,2048]{1,0:T(8,128)S(1)}, f32[16,2048]{1,0:T(8,128)S(1)}, u32[]{:S(2)}, u32[]{:S(2)}) collective-permute-start(f32[16,2048]{1,0:T(8,128)S(1)} %copy-done.2), channel_id=1, source_target_pairs={{0,32},{32,64},{64,96},{96,0},{1,33},{33,65},{65,97},{97,1},{2,34}... | collective-permute-start | bytes 393224 | tf_op jit(solution)/shard_map/ppermute | solution.py:423
  8.1 5.2 %collective-permute-start.3 = (f32[3,16]{1,0:T(4,128)S(1)}, f32[3,16]{1,0:T(4,128)S(1)}, u32[]{:S(2)}, u32[]{:S(2)}) collective-permute-start(f32[3,16]{1,0:T(4,128)S(1)} %bitcast.22), channel_id=1, source_target_pairs={{0,32},{32,64},{64,96},{96,0},{1,33},{33,65},{65,97},{97,1},{2,34}... | collective-permute-start | bytes 584 | tf_op jit(solution)/shard_map/ppermute | solution.py:424
  13.4 7.2 %copy-start.1 = (f32[1,2,96,128]{3,2,1,0:T(8,128)S(1)}, f32[1,2,96,128]{3,2,1,0:T(8,128)}, u32[]{:S(2)}) copy-start(f32[1,2,96,128]{3,2,1,0:T(8,128)} %param.17) | copy-start | bytes 294916
  15.9 4.6 %copy-start.3 = (s32[1,16]{1,0:T(1,128)S(1)}, s32[1,16]{1,0:T(1,128)}, u32[]{:S(2)}) copy-start(s32[1,16]{1,0:T(1,128)} %own.1) | copy-start | bytes 196
  16.0 4.6 %copy-start.4 = (s32[1,16]{1,0:T(1,128)S(1)}, s32[1,16]{1,0:T(1,128)}, u32[]{:S(2)}) copy-start(s32[1,16]{1,0:T(1,128)} %peer.1) | copy-start | bytes 196
  16.0 6.7 %collective-permute-start.4 = (f32[6,96,128]{2,1,0:T(8,128)S(1)}, f32[6,96,128]{2,1,0:T(8,128)S(1)}, u32[]{:S(2)}, u32[]{:S(2)}) collective-permute-start(f32[6,96,128]{2,1,0:T(8,128)S(1)} %get-tuple-element.56), channel_id=1, source_target_pairs={{1,2},{3,4},{5,6},{7,8},{9,10},{11,12},{13,14},{15,16},{17,18},{19... | collective-permute-start | bytes 884744 | tf_op jit(solution)/shard_map/ppermute | solution.py:420
  18.0 4.7 %collective-permute-start.5 = (f32[6,96,128]{2,1,0:T(8,128)S(1)}, f32[6,96,128]{2,1,0:T(8,128)S(1)}, u32[]{:S(2)}, u32[]{:S(2)}) collective-permute-start(f32[6,96,128]{2,1,0:T(8,128)S(1)} %get-tuple-element.57), channel_id=1, source_target_pairs={{0,1},{1,0},{2,3},{3,2},{4,5},{5,4},{6,7},{7,6},{8,9},{9,8},{10,11... | collective-permute-start | bytes 884744 | tf_op jit(solution)/shard_map/ppermute | solution.py:421
  25.2 6.5 %collective-permute-start.6 = (f32[6,96,128]{2,1,0:T(8,128)S(1)}, f32[6,96,128]{2,1,0:T(8,128)S(1)}, u32[]{:S(2)}, u32[]{:S(2)}) collective-permute-start(f32[6,96,128]{2,1,0:T(8,128)S(1)} %get-tuple-element.70), channel_id=1, source_target_pairs={{1,2},{3,4},{5,6},{7,8},{9,10},{11,12},{13,14},{15,16},{17,18},{19... | collective-permute-start | bytes 884744 | tf_op jit(solution)/shard_map/ppermute | solution.py:420
  26.7 5.0 %collective-permute-start.7 = (f32[6,96,128]{2,1,0:T(8,128)S(1)}, f32[6,96,128]{2,1,0:T(8,128)S(1)}, u32[]{:S(2)}, u32[]{:S(2)}) collective-permute-start(f32[6,96,128]{2,1,0:T(8,128)S(1)} %get-tuple-element.71), channel_id=1, source_target_pairs={{0,1},{1,0},{2,3},{3,2},{4,5},{5,4},{6,7},{7,6},{8,9},{9,8},{10,11... | collective-permute-start | bytes 884744 | tf_op jit(solution)/shard_map/ppermute | solution.py:421
  34.2 6.5 %collective-permute-start.8 = (f32[6,96,128]{2,1,0:T(8,128)S(1)}, f32[6,96,128]{2,1,0:T(8,128)S(1)}, u32[]{:S(2)}, u32[]{:S(2)}) collective-permute-start(f32[6,96,128]{2,1,0:T(8,128)S(1)} %get-tuple-element.75), channel_id=1, source_target_pairs={{1,2},{3,4},{5,6},{7,8},{9,10},{11,12},{13,14},{15,16},{17,18},{19... | collective-permute-start | bytes 884744 | tf_op jit(solution)/shard_map/ppermute | solution.py:420
  35.5 5.3 %collective-permute-start.9 = (f32[6,96,128]{2,1,0:T(8,128)S(1)}, f32[6,96,128]{2,1,0:T(8,128)S(1)}, u32[]{:S(2)}, u32[]{:S(2)}) collective-permute-start(f32[6,96,128]{2,1,0:T(8,128)S(1)} %get-tuple-element.76), channel_id=1, source_target_pairs={{0,1},{1,0},{2,3},{3,2},{4,5},{5,4},{6,7},{7,6},{8,9},{9,8},{10,11... | collective-permute-start | bytes 884744 | tf_op jit(solution)/shard_map/ppermute | solution.py:421

commit v6 on v5

v6 whole, which is shorter than its diff:
```python
import jax
import jax.numpy as jnp
import numpy as np
from jax import lax
from jax.experimental import pallas as pl
from jax.experimental.pallas import tpu as pltpu
from jax.sharding import PartitionSpec as P

MAXSUB = 8
ROUNDS = MAXSUB // 2
GROUPS = 4
DOMS = 32
COARSE = 0.4
ROWS = 96
HALF = ROWS // 2
COLS = 128
WIDTH = 256
F32 = jnp.float32
BF16 = jnp.bfloat16
VM = pl.BlockSpec(memory_space=pltpu.VMEM)
SM = pl.BlockSpec(memory_space=pltpu.SMEM)
HBM = pl.BlockSpec(memory_space=pltpu.HBM)


def describe():
    cols = []
    for low, kinds in ((0, 4), (1, 2)):
        for kind in range(kinds):
            for q in range(16):
                cols.append((q // 8, kind % 2, q % 8, low))
    for low in (0, 0, 1):
        for q in range(16):
            cols.append((2, q // 8, q % 8, low))
    return cols


def selectors():
    pick_row = np.zeros((2, 32, 24), np.float32)
    pick_col = np.zeros((2, 2, 24, WIDTH), np.float32)
    for w in range(2):
        for be in range(4):
            for q in range(6):
                pick_row[w, be * 8 + q, (4 * (q % 2 ^ w) + be) * 3 + q // 2] = 1.0
        for t in range(2):
            for k, (at, e, q, _) in enumerate(describe()):
                if q < 6 and at - t in (0, 1):
                    pick_col[w, t, (4 * (q % 2 ^ w) + 2 * (at - t) + e) * 3 + q // 2, k] = 1.0
    return pick_row, pick_col


PICK_ROW, PICK_COL = selectors()


def step_size(count_ref):
    count = jnp.full((8, COLS), count_ref[0], jnp.int32).astype(F32)
    return COARSE / count


def lane_up(x):
    return pltpu.roll(x, COLS - 1, 1)


def lane_down(x):
    return pltpu.roll(x, 1, 1)


def every(i, stride=8):
    return pl.ds(i, ROWS, stride=stride)


def tile(r):
    return slice(8 * (r % ROWS), 8 * (r % ROWS) + 8)


def halves(u):
    hi = u.astype(BF16)
    return hi, (u - hi.astype(F32)).astype(BF16)


def tile_rows(get):
    def rows(r):
        hi, lo = halves(jnp.concatenate([get(r), get(r + 1)], 0))
        parts = [hi, lane_up(hi), lo, lane_up(lo)]
        third = get(r + 2)
        hi, lo = halves(jnp.concatenate([third, lane_up(third)], 0))
        pad = jnp.zeros((WIDTH - 144, COLS), BF16)
        return jnp.concatenate(parts + parts[:2] + [hi, lo, hi, pad], 0)

    return rows


def sweep(start, terms, finish):
    carry = {}
    first = {}
    for i in range(start, start + HALF, 2):
        outs = []
        for rows, lhs, _ in terms:
            rhs = jnp.concatenate([rows(i), rows(i + HALF)], 1)
            outs.append(jnp.dot(lhs, rhs, preferred_element_type=F32))
        for h in range(2):
            for t in range(2):
                r = i + t + h * HALF
                part = []
                for b in range(2):
                    g = []
                    for e in range(2):
                        j = 32 * t + 16 * b + 8 * e
                        block = [
                            scale[tile(r), :] * out[j : j + 8, h * COLS : (h + 1) * COLS]
                            for (_, _, scale), out in zip(terms, outs)
                        ]
                        g.append(sum(block[1:], block[0]))
                    part.append(g[0] + lane_down(g[1]))
                if i + t == start:
                    first[h] = part[0]
                else:
                    finish(r, part[0] + carry[h])
                carry[h] = part[1]
    finish(start, first[0] + carry[1])
    finish(start + HALF, first[1] + carry[0])


def weights_of(a_ref, n):
    return a_ref[64 * n : 64 * n + 64, :]


def inner_pass(a_ref, si, e, m, u, w, ei_out, h_out):
    def finish(r, force):
        at = tile(r)
        rest = e[at, :] - m[at, :] * force
        ei_out[at, :] = rest
        h_out[at, :] = u[at, :] + (w[at, :] + rest)

    sweep(2, [(tile_rows(lambda r: u[tile(r), :]), weights_of(a_ref, 0), si)], finish)


def send_edges(u, h, x_msg, d_msg):
    for base, src in ((0, u), (3, h)):
        for c in range(3):
            x_msg[base + c] = src[every(2 * c), :]
            d_msg[base + c] = src[every(2 * c + 1), :]


def blank_pads(*refs):
    zero = jnp.zeros((ROWS, COLS), F32)
    for q in (6, 7):
        for ref in refs:
            ref[every(q), :] = zero


def prep_body(
    count_ref, place_ref, kmat_h, row_h, col_h, u_h, scale_h, v_h, mass_h, ext_h,
    x_msg, d_msg, u_t, w_t, e_t, m_t, ei_t, h_t, si_t, a_out,
    kmat, row, col, u_n, scale, v_n, mass, ext_n, sems,
):
    pairs = [
        (kmat_h, kmat), (row_h, row), (col_h, col), (u_h, u_n),
        (scale_h, scale), (v_h, v_n), (mass_h, mass), (ext_h, ext_n),
    ]
    copies = [pltpu.make_async_copy(a, b, sems.at[n]) for n, (a, b) in enumerate(pairs)]
    for copy in copies:
        copy.start()
    blank_pads(u_t, w_t, e_t, m_t, si_t)
    odd = place_ref[0] % 2 == 1
    dt = step_size(count_ref)[0:1]
    high = lax.Precision.HIGHEST
    for copy in copies[:3]:
        copy.wait()
    slot = lax.broadcasted_iota(jnp.int32, (64, WIDTH), 1)
    low = ((slot >= 64) & (slot < 96)) | (slot >= 128)
    full = []
    for layer in range(2):
        flip = odd if layer == 0 else jnp.logical_not(odd)
        rows = jnp.dot(
            jnp.where(flip, row[1], row[0]), kmat[...], precision=high, preferred_element_type=F32
        )
        cols = [jnp.where(flip, col[1, t], col[0, t]) for t in range(2)]
        blocks = [jnp.dot(rows, c, precision=high, preferred_element_type=F32) for c in cols]
        block = jnp.concatenate(blocks, 0)
        big = block.astype(BF16).astype(F32)
        full.append(jnp.where(low, block - big, big).astype(BF16))
    across = (lax.broadcasted_iota(jnp.int32, (64, WIDTH), 0) % 2) == 0
    a_out[0:64, :] = full[0]
    a_out[64:128, :] = full[1]
    a_out[128:192, :] = jnp.where(across, full[1].astype(F32), 0.0).astype(BF16)
    a_out[192:256, :] = jnp.where(across, 0.0, full[1].astype(F32)).astype(BF16)

    def sides(ref, k=None):
        low_plane, top_plane = (ref[0], ref[1]) if k is None else (ref[2 * k], ref[2 * k + 1])
        return jnp.where(odd, top_plane, low_plane), jnp.where(odd, low_plane, top_plane)

    for copy in copies[3:]:
        copy.wait()
    inv = [(dt * dt) / part for part in sides(mass)]
    for c in range(3):
        us, vs, es = sides(u_n, c), sides(v_n, c), sides(ext_n, c)
        for x in range(2):
            at = every(2 * c + x)
            u_t[at, :] = us[x]
            w_t[at, :] = dt * vs[x]
            e_t[at, :] = inv[x] * es[x]
            m_t[at, :] = inv[x]
            si_t[at, :] = scale[0]
    inner_pass(a_out, si_t, e_t, m_t, u_t, w_t, ei_t, h_t)
    send_edges(u_t, h_t, x_msg, d_msg)
    x_msg[6] = inv[0]
    d_msg[6] = inv[1]
    x_msg[7] = scale[1]
    d_msg[7] = scale[1]


def taken(rnd, x):
    sub = lax.broadcasted_iota(jnp.int32, (8, COLS), 0)
    return (sub % 2 == x) & (sub < 6)


def outer_step(rnd, x, planes, scale, count_ref, refs):
    u_t, w_t, m_t, ei_t, h_t, a_ref, s_t, mm_t, ur, hr, u1, w1 = refs
    act = jnp.where(count_ref[0] > 2 * rnd, 1.0, 0.0).astype(F32)
    mask = taken(rnd, 1 - x)
    for c in range(3):
        at = every(2 * c + 1 - x)
        ur[at, :] = planes(c)
        hr[at, :] = planes(3 + c)
        if rnd == 0:
            mm_t[at, :] = planes(6)
    if rnd == 0:
        blank_pads(s_t)
        for q in range(6):
            s_t[every(q), :] = scale
        for r in range(ROWS):
            mm_t[tile(r), :] = jnp.where(mask, mm_t[tile(r), :], m_t[tile(r), :])

    def get(r):
        return jnp.where(mask, ur[tile(r), :], u_t[tile(r), :])

    def finish(r, force):
        at = tile(r)
        pull = mm_t[at, :] * force
        u = get(r)
        goal = jnp.where(mask, hr[at, :], h_t[at, :])
        u1[at, :] = u + act * ((goal - pull) - u)
        w1[at, :] = w_t[at, :] + act * (ei_t[at, :] - pull)

    sweep(0, [(tile_rows(get), weights_of(a_ref, 1), s_t)], finish)


def within_body(rnd, *refs):
    refs = list(refs)
    take = lambda n: [refs.pop(0) for _ in range(n)]
    count_ref, place_ref, d_in, u_t, w_t, m_t, ei_t, h_t, a_ref = take(9)
    (scale,) = take(1) if rnd == 0 else (None,)
    if rnd > 0:
        sd_t, md_t = take(2)
    u1, w1, fd = take(3)
    if rnd == 0:
        sd_t, md_t = take(2)
    ur, hr = take(2)
    odd = place_ref[0] % 2 == 1
    layer = jnp.where(odd, d_in[7], scale[1]) if rnd == 0 else None
    outer_step(
        rnd, 1, lambda k: d_in[k], layer, count_ref,
        (u_t, w_t, m_t, ei_t, h_t, a_ref, sd_t, md_t, ur, hr, u1, w1),
    )

    def finish(r, force):
        fd[tile(r), :] = force

    sweep(1, [(tile_rows(lambda r: u1[tile(r), :]), weights_of(a_ref, 3), sd_t)], finish)


def across_body(rnd, *refs):
    refs = list(refs)
    take = lambda n: [refs.pop(0) for _ in range(n)]
    last = rnd == ROUNDS - 1
    count_ref, place_ref, x_in, u_t, w_t, e_t, m_t, ei_t, h_t, si_t, a_ref, u1d, w1d, fd = take(14)
    (scale,) = take(1) if rnd == 0 else (None,)
    if rnd > 0:
        sx_t, mx_t = take(2)
    if last:
        pick, share = take(2)
        u_out, v_out, g_out = take(3)
    else:
        x_msg, d_msg, u2, w2, ei_out, h_out = take(6)
    if rnd == 0:
        sx_t, mx_t = take(2)
    ur, hr, u1x, w1x, u1 = take(5)
    if last:
        u2, w2, u_nat, sem = take(4)
    place = place_ref[0]
    odd = place % 2 == 1
    inside = (place > 0) & (place < DOMS - 1)

    def planes(k):
        return jnp.where(inside, x_in[k], 0.0)

    layer = jnp.where(odd, scale[1], planes(7)) if rnd == 0 else None
    outer_step(
        rnd, 0, planes, layer, count_ref,
        (u_t, w_t, m_t, ei_t, h_t, a_ref, sx_t, mx_t, ur, hr, u1x, w1x),
    )
    act = jnp.where(count_ref[0] > 2 * rnd + 1, 1.0, 0.0).astype(F32)
    within = lax.broadcasted_iota(jnp.int32, (8, COLS), 0) % 2 == 1

    def middle(r):
        return jnp.where(within, u1d[tile(r), :], u1x[tile(r), :])

    def finish(r, force):
        at = tile(r)
        w = jnp.where(within, w1d[at, :], w1x[at, :])
        w = w + act * (e_t[at, :] - m_t[at, :] * (force + fd[at, :]))
        w2[at, :] = w
        u2[at, :] = middle(r) + act * w

    sweep(
        1,
        [
            (tile_rows(middle), weights_of(a_ref, 0), si_t),
            (tile_rows(lambda r: u1x[tile(r), :]), weights_of(a_ref, 2), sx_t),
        ],
        finish,
    )
    if last:
        back = step_size(count_ref)[0:1]
        for c in range(3):
            for src, out, scaled in ((u2, u_nat, False), (w2, v_out, True)):
                here, there = src[every(2 * c), :], src[every(2 * c + 1), :]
                if scaled:
                    here, there = here / back, there / back
                out[2 * c] = jnp.where(odd, there, here)
                out[2 * c + 1] = jnp.where(odd, here, there)
        copy = pltpu.make_async_copy(u_nat, u_out, sem)
        copy.start()
        partial_gaps(place_ref, pick, share, v_out, g_out)
        copy.wait()
        return
    inner_pass(a_ref, si_t, e_t, m_t, u2, w2, ei_out, h_out)
    send_edges(u2, h_out, x_msg, d_msg)


def thirds(x):
    parts = []
    for _ in range(3):
        part = x.astype(jnp.bfloat16)
        parts.append(part)
        x = x - part.astype(F32)
    return parts


def chosen(onehot, values):
    return sum(jnp.dot(onehot, part, preferred_element_type=F32) for part in thirds(values))


def node_body(own, peer, normal, before, mass, pick, pick_t, share, change):
    sub = lax.broadcasted_iota(jnp.int32, (16, 16), 0)
    eye = sub == lax.broadcasted_iota(jnp.int32, (16, 16), 1)
    lane = lax.broadcasted_iota(jnp.int32, (16, COLS), 1)
    weights = jnp.concatenate([mass[0], mass[1]], 1)

    def column(line):
        return jnp.sum(jnp.where(eye, jnp.broadcast_to(line, (16, 16)), 0.0), axis=1, keepdims=True)

    for side, nodes, vec, sign in ((0, own, normal, 1.0), (1, peer, before, -1.0)):
        at = slice(16 * side, 16 * side + 16)
        index = column(nodes[...].astype(F32)).astype(jnp.int32)
        plane = jnp.where(index >= ROWS * COLS, 1, 0)
        rest = index - plane * (ROWS * COLS)
        row = rest // COLS
        col = rest - row * COLS
        onehot = jnp.where(lane == row, 1.0, 0.0)
        pick[at, :] = onehot[:, 0:ROWS].astype(jnp.bfloat16)
        heavy = chosen(onehot[:, 0:ROWS].astype(jnp.bfloat16), weights)
        hits = [(lane == col) & (plane == p) for p in range(2)]
        total = jnp.where(hits[0], heavy[:, 0:COLS], 0.0) + jnp.where(hits[1], heavy[:, COLS:], 0.0)
        total = jnp.sum(total, axis=1, keepdims=True)
        for c in range(3):
            value = sign * column(vec[c : c + 1, :])
            for p in range(2):
                q = 2 * c + p
                part = jnp.where(hits[p], value, 0.0)
                share[at, q * COLS : (q + 1) * COLS] = part
                change[at, q * COLS : (q + 1) * COLS] = -part / total
        pick_t[side] = jnp.transpose(onehot)[0:ROWS].astype(jnp.bfloat16)


def partial_gaps(place_ref, pick, share, v, g_out):
    values = jnp.concatenate([v[q] for q in range(6)], 1)
    total = jnp.sum(chosen(pick[...], values) * share[...], axis=1, keepdims=True)
    lane = lax.broadcasted_iota(jnp.int32, (32, COLS), 1)
    sub = lax.broadcasted_iota(jnp.int32, (32, COLS), 0)
    line = jnp.where(lane == sub % 16 + 16 * (place_ref[0] % 8), jnp.broadcast_to(total, (32, COLS)), 0.0)
    for side in range(2):
        part = jnp.sum(line[16 * side : 16 * side + 16], axis=0, keepdims=True)
        g_out[:, side * COLS : (side + 1) * COLS] = jnp.broadcast_to(part, (128, COLS))


def final_body(gathered, inv_own, inv_before, pick_t, change, v_in, v_out):
    mine = jnp.sum(gathered[:, 0:COLS].reshape(16, 8, COLS), axis=1)
    other = jnp.sum(gathered[:, COLS : 2 * COLS].reshape(16, 8, COLS), axis=1)
    gap = mine + jnp.concatenate([other[4:16], other[0:4]], 0)
    total = None
    for side, rows in ((0, inv_own), (1, inv_before)):
        acc = jnp.zeros((16, COLS), F32)
        for k in range(16):
            acc = acc + rows[:, k * COLS : (k + 1) * COLS] * gap[k : k + 1, :]
        lam = jnp.sum(acc, axis=1, keepdims=True)
        part = chosen(pick_t[side], change[16 * side : 16 * side + 16, :] * lam)
        total = part if total is None else total + part
    for q in range(6):
        v_out[q] = v_in[q] + total[:, q * COLS : (q + 1) * COLS]


def call(body, outs, scratch, ins, limit=24 * 1024 * 1024, far_outs=()):
    return pl.pallas_call(
        body,
        out_shape=[s if isinstance(s, jax.ShapeDtypeStruct) else jax.ShapeDtypeStruct(s, F32) for s in outs],
        in_specs=ins,
        out_specs=[HBM if n in far_outs else VM for n in range(len(outs))],
        scratch_shapes=[pltpu.VMEM(s, F32) if isinstance(s, tuple) else s for s in scratch],
        compiler_params=pltpu.CompilerParams(vmem_limit_bytes=limit),
    )


TILE = (ROWS * 8, COLS)
PLANES = (6, ROWS, COLS)


def across_pairs():
    pairs = [(g * DOMS + i, g * DOMS + i + 1) for g in range(GROUPS) for i in range(1, DOMS - 1, 2)]
    for g in range(0, GROUPS, 2):
        for i in (0, DOMS - 1):
            pairs.append((g * DOMS + i, (g + 1) * DOMS + i))
    return pairs + [(b, a) for a, b in pairs]


ACROSS = across_pairs()
WITHIN = [(i, i ^ 1) for i in range(DOMS)]
FROM_BEFORE = [(i, (i + 1) % GROUPS) for i in range(GROUPS)]


def far(x):
    return pltpu.with_memory_space_constraint(jnp.asarray(x), pltpu.HBM)


def on_device(
    displacement, velocity, external, mass, elem_scale, stiffness, substeps,
    own_nodes, peer_nodes, normals, schur_inverse,
):
    field = displacement[0].reshape(PLANES)
    speed = velocity[0].reshape(PLANES)
    loads = external[0].reshape(PLANES)
    weight = mass[0]
    scale = elem_scale[0]
    place = lax.axis_index("dom").reshape(1)
    normal = normals[0]
    scalars = (substeps, place)
    b16 = lambda *shape: jax.ShapeDtypeStruct(shape, BF16)

    first = (8, ROWS, COLS)
    pair = (2, ROWS, COLS)
    x, d, u, w, e, m, ei, h, si, a = call(
        prep_body,
        [first, first] + [TILE] * 7 + [b16(256, WIDTH)],
        [
            (24, 24), (2, 32, 24), (2, 2, 24, WIDTH), PLANES, pair, PLANES, pair, PLANES,
            pltpu.SemaphoreType.DMA((8,)),
        ],
        [SM] * 2 + [HBM] * 8,
    )(*scalars, *(far(v) for v in (stiffness[0], PICK_ROW, PICK_COL, field, scale, speed, weight, loads)))
    for rnd in range(ROUNDS):
        last = rnd == ROUNDS - 1
        x = lax.ppermute(x, ("grp", "dom"), ACROSS)
        d = lax.ppermute(d, "dom", WITHIN)
        if rnd == 0:
            inv_before = lax.ppermute(schur_inverse, "grp", FROM_BEFORE)
            before = lax.ppermute(normal, "grp", FROM_BEFORE)

        def within(*refs, rnd=rnd):
            return within_body(rnd, *refs)

        args = [d, u, w, m, ei, h, a] + ([scale] if rnd == 0 else [sd, md])
        got = call(
            within, [TILE] * (5 if rnd == 0 else 3), [TILE] * 2, [SM] * 2 + [VM] * len(args)
        )(*scalars, *args)
        u1d, w1d, fd = got[:3]
        if rnd == 0:
            sd, md = got[3:]
            x, inv_before, before = lax.optimization_barrier((x, inv_before, before))
        if rnd == 1:
            nodes = call(
                node_body, [b16(32, ROWS), b16(2, ROWS, 16), (32, 6 * COLS), (32, 6 * COLS)], [], [VM] * 5
            )(own_nodes, peer_nodes, normal, before, weight)
            x, *nodes = lax.optimization_barrier((x, *nodes))
            pick, pick_t, share, change = nodes

        def across(*refs, rnd=rnd):
            return across_body(rnd, *refs)

        args = [x, u, w, e, m, ei, h, si, a, u1d, w1d, fd] + ([scale] if rnd == 0 else [sx, mx])
        args += [pick, share] if last else []
        outs = [PLANES, PLANES, (128, 2 * COLS)] if last else [PLANES, PLANES] + [TILE] * 4
        outs += [TILE, TILE] if rnd == 0 else []
        scratch = [TILE] * 5 + ([TILE, TILE, PLANES, pltpu.SemaphoreType.DMA] if last else [])
        got = call(
            across, outs, scratch, [SM] * 2 + [VM] * len(args), far_outs=(0,) if last else ()
        )(*scalars, *args)
        if last:
            u, v, gap = got
        else:
            x, d, u, w, ei, h = got[:6]
        if rnd == 0:
            sx, mx = got[6:]
    gathered = lax.all_to_all(gap, ("grp", "dom"), 0, 0, tiled=True)
    (v,) = call(final_body, [PLANES], [], [VM] * 6)(
        gathered, schur_inverse, inv_before, pick_t, change, v
    )
    shape = displacement.shape
    return u.reshape(shape), v.reshape(shape)


def solution(mesh):
    return jax.shard_map(
        on_device,
        mesh=mesh,
        in_specs=(
            P("grp", None, "dom", None, None),
            P("grp", None, "dom", None, None),
            P("grp", None, "dom", None, None),
            P("grp", "dom", None, None),
            P("grp", "dom", None, None),
            P("grp", None, None),
            P("grp"),
            P("grp", "dom"),
            P("grp", "dom"),
            P("grp", None, "dom"),
            P(("grp", "dom"), None),
        ),
        out_specs=(P("grp", None, "dom", None, None), P("grp", None, "dom", None, None)),
        check_vma=False,
    )
```

time: 70.8 us -> 71.7 us (1.013)
  waiting for transfers between devices: 9.14 us -> 16.4 us
  starting transfers between devices: 19.4 us -> 13.1 us
  Pallas kernels: 14.6 us -> 17.3 us
  blocking collectives: 25.9 us -> 23.2 us
    ppermute x4, waiting for transfers between devices: 5.16 us -> 9.97 us  [on_device(): x = lax.ppermute(x, ('grp', 'dom'), ACROSS)]
    ppermute x4, starting transfers between devices: 9.74 us -> 6.16 us  [on_device(): d = lax.ppermute(d, 'dom', WITHIN)]
    ppermute x4, starting transfers between devices: 7.56 us -> 4.78 us  [on_device(): x = lax.ppermute(x, ('grp', 'dom'), ACROSS)]
    all_to_all x1, blocking collectives: 25.9 us -> 23.2 us  [on_device(): gathered = lax.all_to_all(gap, ('grp', 'dom'), 0, 0, tiled=True)]
    pallas_call x5 -> x9, Pallas kernels: 13.1 us -> 15.8 us  [the longest x4 8.74 us: on_device(): call(across, outs, scratch, [SM] * 2 + [VM] * len(args), far_outs=(0,) if...]
    ppermute x4, waiting for transfers between devices: 0.01 us -> 2.42 us  [on_device(): d = lax.ppermute(d, 'dom', WITHIN)]
  transfers between devices with their start and end apart: 10 -> 10, of which waited for: 4 -> 6; matrix products, arithmetic and copies ran while one was open for 0% -> 0% of each run, Pallas kernels for 1% -> 4%
where the time goes in v6:
time: 71.7 us; the launch traced here: 71.5 us
  blocking collectives  23.2 us (32%)
  Pallas kernels  17.3 us (24%)
  waiting for transfers between devices  16.4 us (23%)
  starting transfers between devices  13.1 us (18%)
  between operations  1.43 us (2%)
    all_to_all x1, blocking collectives, on_device(): gathered = lax.all_to_all(gap, ('grp', 'dom'), 0, 0, tiled=True)  23.2 us
    ppermute x4, waiting for transfers between devices, on_device(): x = lax.ppermute(x, ('grp', 'dom'), ACROSS)  9.97 us
    pallas_call x4, Pallas kernels, on_device(): call(across, outs, scratch, [SM] * 2 + [VM] * len(args), far_outs=(0,) if...  8.74 us
    ppermute x4, starting transfers between devices, on_device(): d = lax.ppermute(d, 'dom', WITHIN)  6.16 us
    ppermute x4, starting transfers between devices, on_device(): x = lax.ppermute(x, ('grp', 'dom'), ACROSS)  4.78 us
    pallas_call x4, Pallas kernels, on_device(): call(within, [TILE] * (5 if rnd == 0 else 3), [TILE] * 2, [SM] * 2 + [VM]...  4.56 us
    ppermute x1, waiting for transfers between devices, on_device(): before = lax.ppermute(normal, 'grp', FROM_BEFORE)  3.98 us
    pallas_call x1, Pallas kernels, on_device(): call(prep_body, [first, first] + [TILE] * 7 + [b16(256, WIDTH)], [(24, 24...  2.45 us
  transfers between devices with their start and end apart: 10, of which 6 were waited for; matrix products, arithmetic and copies ran while one was open for 0% of the time, Pallas kernels for 4%

profile of v6, /device:TPU:1, one launch (start us, length us, event | category | flops | bytes accessed | tf_op | source)
XLA Modules:
  0.0 71.5 jit_solution(4246956682545535150)
XLA Ops:
  1.3 2.5 %shard_map.140 = (f32[8,96,128]{2,1,0:T(8,128)S(1)}, f32[8,96,128]{2,1,0:T(8,128)S(1)}, f32[768,128]{1,0:T(8,128)S(1)}, f32[768,128]{1,0:T(8,128)S(1)}, f32[768,...) custom-call(s32[1]{0:T(128)S(6)} %copy.22.count_ref.refs_0_, ...), custom_call_target="tpu_custom_call" | custom-call | tf_op jit(solution)/shard_map/pallas_call | solution.py:461
  3.8 0.0 copy-start.5
  3.8 2.8 %collective-permute-start = (f32[8,96,128]{2,1,0:T(8,128)S(1)}, f32[8,96,128]{2,1,0:T(8,128)S(1)}, u32[]{:S(2)}, u32[]{:S(2)}) collective-permute-start(f32[8,96,128]{2,1,0:T(8,128)S(1)} %get-tuple-element.61), channel_id=1, source_target_pairs={{1,2},{3,4},{5,6},{7,8},{9,10},{11,12},{13,14},{15,16},{17,18},{19... | collective-permute-start | bytes 1179656 | tf_op jit(solution)/shard_map/ppermute | solution.py:472
  6.5 0.3 collective-permute-start.3
  6.8 0.9 %collective-permute-start.1 = (f32[16,2048]{1,0:T(8,128)S(1)}, f32[16,2048]{1,0:T(8,128)S(1)}, u32[]{:S(2)}, u32[]{:S(2)}) collective-permute-start(f32[16,2048]{1,0:T(8,128)S(1)} %copy-done.2), channel_id=1, source_target_pairs={{0,32},{32,64},{64,96},{96,0},{1,33},{33,65},{65,97},{97,1},{2,34}... | collective-permute-start | bytes 393224 | tf_op jit(solution)/shard_map/ppermute | solution.py:475
  7.8 1.2 %collective-permute-start.2 = (f32[3,16]{1,0:T(4,128)S(1)}, f32[3,16]{1,0:T(4,128)S(1)}, u32[]{:S(2)}, u32[]{:S(2)}) collective-permute-start(f32[3,16]{1,0:T(4,128)S(1)} %bitcast.23), channel_id=1, source_target_pairs={{0,32},{32,64},{64,96},{96,0},{1,33},{33,65},{65,97},{97,1},{2,34}... | collective-permute-start | bytes 584 | tf_op jit(solution)/shard_map/ppermute | solution.py:476
  9.0 4.0 %collective-permute-done.2.before = f32[3,16]{1,0:T(4,128)S(1)} collective-permute-done((f32[3,16]{1,0:T(4,128)S(1)}, f32[3,16]{1,0:T(4,128)S(1)}, u32[]{:S(2)}, u32[]{:S(2)}) %collective-permute-start.2) | collective-permute-done | bytes 224 | tf_op jit(solution)/shard_map/ppermute | solution.py:476
  13.0 1.2 %shard_map.141 = (f32[768,128]{1,0:T(8,128)S(1)}, f32[768,128]{1,0:T(8,128)S(1)}, f32[768,128]{1,0:T(8,128)S(1)}, f32[768,128]{1,0:T(8,128)S(1)}, f32[768,128]{1,0:T(8,128)S(1)}) custom-call(s32[1]{0:T(128)S(6)} %copy.22.count_ref.refs_0_, s32[1]{0:T(128)} %bitcast.place_ref.refs_1_, f32[8,96,128]{2,1,0:T(8,128)S(1)} %collective-permute-done.3.refs_2_, ...), custom_call_target="tpu_custom_call" | custom-call | tf_op jit(solution)/shard_map/pallas_call | solution.py:482
  14.2 0.0 copy-start.1
  14.2 2.2 %shard_map.142 = (f32[6,96,128]{2,1,0:T(8,128)S(1)}, f32[6,96,128]{2,1,0:T(8,128)S(1)}, f32[768,128]{1,0:T(8,128)S(1)}, f32[768,128]{1,0:T(8,128)S(1)}, f32[768,...) custom-call(s32[1]{0:T(128)S(6)} %copy.22.count_ref.refs_0_, ...), custom_call_target="tpu_custom_call" | custom-call | tf_op jit(solution)/shard_map/pallas_call | solution.py:504
  16.4 0.0 copy-start.3
  16.4 0.0 copy-start.4
  16.5 2.0 %collective-permute-start.4 = (f32[6,96,128]{2,1,0:T(8,128)S(1)}, f32[6,96,128]{2,1,0:T(8,128)S(1)}, u32[]{:S(2)}, u32[]{:S(2)}) collective-permute-start(f32[6,96,128]{2,1,0:T(8,128)S(1)} %get-tuple-element.75), channel_id=1, source_target_pairs={{1,2},{3,4},{5,6},{7,8},{9,10},{11,12},{13,14},{15,16},{17,18},{19... | collective-permute-start | bytes 884744 | tf_op jit(solution)/shard_map/ppermute | solution.py:472
  18.5 2.6 %collective-permute-start.5 = (f32[6,96,128]{2,1,0:T(8,128)S(1)}, f32[6,96,128]{2,1,0:T(8,128)S(1)}, u32[]{:S(2)}, u32[]{:S(2)}) collective-permute-start(f32[6,96,128]{2,1,0:T(8,128)S(1)} %get-tuple-element.86), channel_id=1, source_target_pairs={{0,1},{1,0},{2,3},{3,2},{4,5},{5,4},{6,7},{7,6},{8,9},{9,8},{10,11... | collective-permute-start | bytes 884744 | tf_op jit(solution)/shard_map/ppermute | solution.py:473
  21.1 0.4 shard_map.143
  21.4 1.8 %collective-permute-done.4.refs_2_ = f32[6,96,128]{2,1,0:T(8,128)S(1)} collective-permute-done((f32[6,96,128]{2,1,0:T(8,128)S(1)}, f32[6,96,128]{2,1,0:T(8,128)S(1)}, u32[]{:S(2)}, u32[]{:S(2)}) %collective-permute-start.4) | collective-permute-done | bytes 294944 | tf_op jit(solution)/shard_map/ppermute | solution.py:472
  23.2 1.1 %shard_map.144 = (f32[768,128]{1,0:T(8,128)S(1)}, f32[768,128]{1,0:T(8,128)S(1)}, f32[768,128]{1,0:T(8,128)S(1)}) custom-call(s32[1]{0:T(128)S(6)} %copy.22.count_ref.refs_0_, s32[1]{0:T(128)} %bitcast.place_ref.refs_1_, f32[6,96,128]{2,1,0:T(8,128)S(1)} %collective-permute-done.5.refs_2_, f32[768,128]{1,0:T(8,128)S(1)} %get-tuple-element.82.refs_3_, ...), custom_call_target="tpu_custom_call" | custom-call | tf_op jit(solution)/shard_map/pallas_call | solution.py:482
  24.3 2.1 %shard_map.145 = (f32[6,96,128]{2,1,0:T(8,128)S(1)}, f32[6,96,128]{2,1,0:T(8,128)S(1)}, f32[768,128]{1,0:T(8,128)S(1)}, f32[768,128]{1,0:T(8,128)S(1)}, f32[768,128]{1,0:T(8,128)S(1)}, /*index=5*/f32[768,128]{1,0:T(8,128)S(1)}) custom-call(s32[1]{0:T(128)S(6)} %copy.22.count_ref.refs_0_, s32[1]{0:T(128)} %bitcast.place_ref.refs_1_, ...), custom_call_target="tpu_custom_call" | custom-call | tf_op jit(solution)/shard_map/pallas_call | solution.py:504
  26.4 2.7 %collective-permute-start.7 = (f32[6,96,128]{2,1,0:T(8,128)S(1)}, f32[6,96,128]{2,1,0:T(8,128)S(1)}, u32[]{:S(2)}, u32[]{:S(2)}) collective-permute-start(f32[6,96,128]{2,1,0:T(8,128)S(1)} %get-tuple-element.99), channel_id=1, source_target_pairs={{0,1},{1,0},{2,3},{3,2},{4,5},{5,4},{6,7},{7,6},{8,9},{9,8},{10,11... | collective-permute-start | bytes 884744 | tf_op jit(solution)/shard_map/ppermute | solution.py:473
  29.0 0.0 collective-permute-start.6
  29.0 1.2 %collective-permute-done.7.refs_2_ = f32[6,96,128]{2,1,0:T(8,128)S(1)} collective-permute-done((f32[6,96,128]{2,1,0:T(8,128)S(1)}, f32[6,96,128]{2,1,0:T(8,128)S(1)}, u32[]{:S(2)}, u32[]{:S(2)}) %collective-permute-start.7) | collective-permute-done | bytes 294944 | tf_op jit(solution)/shard_map/ppermute | solution.py:473
  30.2 1.1 %shard_map.146 = (f32[768,128]{1,0:T(8,128)S(1)}, f32[768,128]{1,0:T(8,128)S(1)}, f32[768,128]{1,0:T(8,128)S(1)}) custom-call(s32[1]{0:T(128)S(6)} %copy.22.count_ref.refs_0_, s32[1]{0:T(128)} %bitcast.place_ref.refs_1_, f32[6,96,128]{2,1,0:T(8,128)S(1)} %collective-permute-done.7.refs_2_, f32[768,128]{1,0:T(8,128)S(1)} %get-tuple-element.95.refs_3_, ...), custom_call_target="tpu_custom_call" | custom-call | tf_op jit(solution)/shard_map/pallas_call | solution.py:482
  31.4 4.1 %collective-permute-done.6.refs_2_ = f32[6,96,128]{2,1,0:T(8,128)S(1)} collective-permute-done((f32[6,96,128]{2,1,0:T(8,128)S(1)}, f32[6,96,128]{2,1,0:T(8,128)S(1)}, u32[]{:S(2)}, u32[]{:S(2)}) %collective-permute-start.6) | collective-permute-done | bytes 294944 | tf_op jit(solution)/shard_map/ppermute | solution.py:472
  35.5 2.1 %shard_map.147 = (f32[6,96,128]{2,1,0:T(8,128)S(1)}, f32[6,96,128]{2,1,0:T(8,128)S(1)}, f32[768,128]{1,0:T(8,128)S(1)}, f32[768,128]{1,0:T(8,128)S(1)}, f32[768,128]{1,0:T(8,128)S(1)}, /*index=5*/f32[768,128]{1,0:T(8,128)S(1)}) custom-call(s32[1]{0:T(128)S(6)} %copy.22.count_ref.refs_0_, s32[1]{0:T(128)} %bitcast.place_ref.refs_1_, ...), custom_call_target="tpu_custom_call" | custom-call | tf_op jit(solution)/shard_map/pallas_call | solution.py:504
  37.5 0.6 collective-permute-start.9
  38.2 1.2 %collective-permute-done.9.refs_2_ = f32[6,96,128]{2,1,0:T(8,128)S(1)} collective-permute-done((f32[6,96,128]{2,1,0:T(8,128)S(1)}, f32[6,96,128]{2,1,0:T(8,128)S(1)}, u32[]{:S(2)}, u32[]{:S(2)}) %collective-permute-start.9) | collective-permute-done | bytes 294944 | tf_op jit(solution)/shard_map/ppermute | solution.py:473
  39.4 1.1 %shard_map.148 = (f32[768,128]{1,0:T(8,128)S(1)}, f32[768,128]{1,0:T(8,128)S(1)}, f32[768,128]{1,0:T(8,128)S(1)}) custom-call(s32[1]{0:T(128)S(6)} %copy.22.count_ref.refs_0_, s32[1]{0:T(128)} %bitcast.place_ref.refs_1_, f32[6,96,128]{2,1,0:T(8,128)S(1)} %collective-permute-done.9.refs_2_, f32[768,128]{1,0:T(8,128)S(1)} %get-tuple-element.104.refs_3_, ...), custom_call_target="tpu_custom_call" | custom-call | tf_op jit(solution)/shard_map/pallas_call | solution.py:482
  40.5 4.1 %collective-permute-done.8.refs_2_ = f32[6,96,128]{2,1,0:T(8,128)S(1)} collective-permute-done((f32[6,96,128]{2,1,0:T(8,128)S(1)}, f32[6,96,128]{2,1,0:T(8,128)S(1)}, u32[]{:S(2)}, u32[]{:S(2)}) %collective-permute-start.8) | collective-permute-done | bytes 294944 | tf_op jit(solution)/shard_map/ppermute | solution.py:472
  44.6 2.4 %shard_map.149 = (f32[6,96,128]{2,1,0:T(8,128)}, f32[6,96,128]{2,1,0:T(8,128)S(1)}, f32[128,256]{1,0:T(8,128)S(1)}) custom-call(s32[1]{0:T(128)S(6)} %copy.22.count_ref.refs_0_, s32[1]{0:T(128)} %bitcast.place_ref.refs_1_, f32[6,96,128]{2,1,0:T(8,128)S(1)} %collective-permute-done.8.refs_2_, f32[768,128]{1,0:T(8,128)S(1)} %get-tuple-element.104.refs_3_, ...), custom_call_target="tpu_custom_call" | custom-call | tf_op jit(solution)/shard_map/pallas_call | solution.py:504
  47.0 0.1 copy.15
  47.1 23.2 %all_to_all.11 = f32[128,1,256]{2,1,0:T(1,128)S(1)} all-to-all(f32[128,1,256]{2,1,0:T(1,128)S(1)} %copy.15), channel_id=1, replica_groups=mesh['grp'=4,'dom'=32] {'grp','dom'}, dimensions={0} | all-to-all | bytes 262144 | tf_op jit(solution)/shard_map/all_to_all | solution.py:513
  70.3 1.2 %shard_map.150 = f32[6,96,128]{2,1,0:T(8,128)} custom-call(f32[128,256]{1,0:T(8,128)S(1)} %bitcast.19, f32[16,2048]{1,0:T(8,128)S(1)} %copy-done.2, f32[16,2048]{1,0:T(8,128)S(1)} %collective-permute-done.1.inv_before, bf16[2,96,16]{2,1,0:T(8,128)(2,1)S(1)} %get-tuple-element.117.pick_t, f32[32,768]{1,0:T(8,128)S(1)} %get-tuple-element.118.change, ...), custom_call_target="tpu_custom_call" | custom-call | tf_op jit(solution)/shard_map/pallas_call | solution.py:514
  (15 shorter events, 0.0 us)
Async XLA Ops:
  1.3 5.6 %copy-start.2 = (f32[16,2048]{1,0:T(8,128)S(1)}, f32[16,2048]{1,0:T(8,128)}, u32[]{:S(2)}) copy-start(f32[16,2048]{1,0:T(8,128)} %inv_own.1) | copy-start | bytes 393220
  1.3 11.7 %copy-start = (f32[1,2,96,128]{3,2,1,0:T(8,128)S(1)}, f32[1,2,96,128]{3,2,1,0:T(8,128)}, u32[]{:S(2)}) copy-start(f32[1,2,96,128]{3,2,1,0:T(8,128)} %param.17) | copy-start | bytes 294916
  3.8 4.0 %copy-start.5 = (f32[1,3,16]{2,0,1:T(1,128)S(1)}, f32[1,3,16]{2,0,1:T(1,128)}, u32[]{:S(2)}) copy-start(f32[1,3,16]{2,0,1:T(1,128)} %param.22) | copy-start | bytes 580
  3.8 9.2 %collective-permute-start = (f32[8,96,128]{2,1,0:T(8,128)S(1)}, f32[8,96,128]{2,1,0:T(8,128)S(1)}, u32[]{:S(2)}, u32[]{:S(2)}) collective-permute-start(f32[8,96,128]{2,1,0:T(8,128)S(1)} %get-tuple-element.61), channel_id=1, source_target_pairs={{1,2},{3,4},{5,6},{7,8},{9,10},{11,12},{13,14},{15,16},{17,18},{19... | collective-permute-start | bytes 1179656 | tf_op jit(solution)/shard_map/ppermute | solution.py:472
  6.5 6.4 %collective-permute-start.3 = (f32[8,96,128]{2,1,0:T(8,128)S(1)}, f32[8,96,128]{2,1,0:T(8,128)S(1)}, u32[]{:S(2)}, u32[]{:S(2)}) collective-permute-start(f32[8,96,128]{2,1,0:T(8,128)S(1)} %get-tuple-element.71), channel_id=1, source_target_pairs={{0,1},{1,0},{2,3},{3,2},{4,5},{5,4},{6,7},{7,6},{8,9},{9,8},{10,11... | collective-permute-start | bytes 1179656 | tf_op jit(solution)/shard_map/ppermute | solution.py:473
  6.8 6.1 %collective-permute-start.1 = (f32[16,2048]{1,0:T(8,128)S(1)}, f32[16,2048]{1,0:T(8,128)S(1)}, u32[]{:S(2)}, u32[]{:S(2)}) collective-permute-start(f32[16,2048]{1,0:T(8,128)S(1)} %copy-done.2), channel_id=1, source_target_pairs={{0,32},{32,64},{64,96},{96,0},{1,33},{33,65},{65,97},{97,1},{2,34}... | collective-permute-start | bytes 393224 | tf_op jit(solution)/shard_map/ppermute | solution.py:475
  7.8 5.2 %collective-permute-start.2 = (f32[3,16]{1,0:T(4,128)S(1)}, f32[3,16]{1,0:T(4,128)S(1)}, u32[]{:S(2)}, u32[]{:S(2)}) collective-permute-start(f32[3,16]{1,0:T(4,128)S(1)} %bitcast.23), channel_id=1, source_target_pairs={{0,32},{32,64},{64,96},{96,0},{1,33},{33,65},{65,97},{97,1},{2,34}... | collective-permute-start | bytes 584 | tf_op jit(solution)/shard_map/ppermute | solution.py:476
  14.2 6.8 %copy-start.1 = (f32[1,2,96,128]{3,2,1,0:T(8,128)S(1)}, f32[1,2,96,128]{3,2,1,0:T(8,128)}, u32[]{:S(2)}) copy-start(f32[1,2,96,128]{3,2,1,0:T(8,128)} %param.16) | copy-start | bytes 294916
  16.4 4.6 %copy-start.3 = (s32[1,16]{1,0:T(1,128)S(1)}, s32[1,16]{1,0:T(1,128)}, u32[]{:S(2)}) copy-start(s32[1,16]{1,0:T(1,128)} %own.1) | copy-start | bytes 196
  16.4 4.6 %copy-start.4 = (s32[1,16]{1,0:T(1,128)S(1)}, s32[1,16]{1,0:T(1,128)}, u32[]{:S(2)}) copy-start(s32[1,16]{1,0:T(1,128)} %peer.1) | copy-start | bytes 196
  16.5 6.7 %collective-permute-start.4 = (f32[6,96,128]{2,1,0:T(8,128)S(1)}, f32[6,96,128]{2,1,0:T(8,128)S(1)}, u32[]{:S(2)}, u32[]{:S(2)}) collective-permute-start(f32[6,96,128]{2,1,0:T(8,128)S(1)} %get-tuple-element.75), channel_id=1, source_target_pairs={{1,2},{3,4},{5,6},{7,8},{9,10},{11,12},{13,14},{15,16},{17,18},{19... | collective-permute-start | bytes 884744 | tf_op jit(solution)/shard_map/ppermute | solution.py:472
  18.5 4.7 %collective-permute-start.5 = (f32[6,96,128]{2,1,0:T(8,128)S(1)}, f32[6,96,128]{2,1,0:T(8,128)S(1)}, u32[]{:S(2)}, u32[]{:S(2)}) collective-permute-start(f32[6,96,128]{2,1,0:T(8,128)S(1)} %get-tuple-element.86), channel_id=1, source_target_pairs={{0,1},{1,0},{2,3},{3,2},{4,5},{5,4},{6,7},{7,6},{8,9},{9,8},{10,11... | collective-permute-start | bytes 884744 | tf_op jit(solution)/shard_map/ppermute | solution.py:473
  26.4 3.9 %collective-permute-start.7 = (f32[6,96,128]{2,1,0:T(8,128)S(1)}, f32[6,96,128]{2,1,0:T(8,128)S(1)}, u32[]{:S(2)}, u32[]{:S(2)}) collective-permute-start(f32[6,96,128]{2,1,0:T(8,128)S(1)} %get-tuple-element.99), channel_id=1, source_target_pairs={{0,1},{1,0},{2,3},{3,2},{4,5},{5,4},{6,7},{7,6},{8,9},{9,8},{10,11... | collective-permute-start | bytes 884744 | tf_op jit(solution)/shard_map/ppermute | solution.py:473
  29.0 6.4 %collective-permute-start.6 = (f32[6,96,128]{2,1,0:T(8,128)S(1)}, f32[6,96,128]{2,1,0:T(8,128)S(1)}, u32[]{:S(2)}, u32[]{:S(2)}) collective-permute-start(f32[6,96,128]{2,1,0:T(8,128)S(1)} %get-tuple-element.94), channel_id=1, source_target_pairs={{1,2},{3,4},{5,6},{7,8},{9,10},{11,12},{13,14},{15,16},{17,18},{19... | collective-permute-start | bytes 884744 | tf_op jit(solution)/shard_map/ppermute | solution.py:472
  37.5 1.8 %collective-permute-start.9 = (f32[6,96,128]{2,1,0:T(8,128)S(1)}, f32[6,96,128]{2,1,0:T(8,128)S(1)}, u32[]{:S(2)}, u32[]{:S(2)}) collective-permute-start(f32[6,96,128]{2,1,0:T(8,128)S(1)} %get-tuple-element.108), channel_id=1, source_target_pairs={{0,1},{1,0},{2,3},{3,2},{4,5},{5,4},{6,7},{7,6},{8,9},{9,8},{10,11... | collective-permute-start | bytes 884744 | tf_op jit(solution)/shard_map/ppermute | solution.py:473
  38.2 6.4 %collective-permute-start.8 = (f32[6,96,128]{2,1,0:T(8,128)S(1)}, f32[6,96,128]{2,1,0:T(8,128)S(1)}, u32[]{:S(2)}, u32[]{:S(2)}) collective-permute-start(f32[6,96,128]{2,1,0:T(8,128)S(1)} %get-tuple-element.103), channel_id=1, source_target_pairs={{1,2},{3,4},{5,6},{7,8},{9,10},{11,12},{13,14},{15,16},{17,18},{19... | collective-permute-start | bytes 884744 | tf_op jit(solution)/shard_map/ppermute | solution.py:472

commit v7 on v6

--- a/solution.py
+++ b/solution.py
@@ -23,15 +23,9 @@
 
 
 def describe():
-    cols = []
-    for low, kinds in ((0, 4), (1, 2)):
-        for kind in range(kinds):
-            for q in range(16):
-                cols.append((q // 8, kind % 2, q % 8, low))
-    for low in (0, 0, 1):
-        for q in range(16):
-            cols.append((2, q // 8, q % 8, low))
-    return cols
+    return [
+        (at, q // 8, q % 8, part == 2) for at in range(3) for part in range(3) for q in range(16)
+    ]
 
 
 def selectors():
@@ -77,14 +71,21 @@
     return hi, (u - hi.astype(F32)).astype(BF16)
 
 
-def tile_rows(get):
+def tile_rows(get, rotated=None):
+    done = {}
+
+    def one(r):
+        r %= ROWS
+        if r not in done:
+            here = get(r)
+            shifted = lane_up(here) if rotated is None else rotated(r)
+            done[r] = halves(jnp.concatenate([here, shifted], 0))
+        hi, lo = done[r]
+        return [hi, lo, hi]
+
     def rows(r):
-        hi, lo = halves(jnp.concatenate([get(r), get(r + 1)], 0))
-        parts = [hi, lane_up(hi), lo, lane_up(lo)]
-        third = get(r + 2)
-        hi, lo = halves(jnp.concatenate([third, lane_up(third)], 0))
         pad = jnp.zeros((WIDTH - 144, COLS), BF16)
-        return jnp.concatenate(parts + parts[:2] + [hi, lo, hi, pad], 0)
+        return jnp.concatenate(one(r) + one(r + 1) + one(r + 2) + [pad], 0)
 
     return rows
 
@@ -92,6 +93,10 @@
 def sweep(start, terms, finish):
     carry = {}
     first = {}
+
+    def close(r, a, b):
+        finish(r, (a[0] + b[0]) + lane_down(a[1] + b[1]))
+
     for i in range(start, start + HALF, 2):
         outs = []
         for rows, lhs, _ in terms:
@@ -101,23 +106,20 @@
             for t in range(2):
                 r = i + t + h * HALF
                 part = []
-                for b in range(2):
-                    g = []
-                    for e in range(2):
-                        j = 32 * t + 16 * b + 8 * e
-                        block = [
-                            scale[tile(r), :] * out[j : j + 8, h * COLS : (h + 1) * COLS]
-                            for (_, _, scale), out in zip(terms, outs)
-                        ]
-                        g.append(sum(block[1:], block[0]))
-                    part.append(g[0] + lane_down(g[1]))
+                for be in range(4):
+                    j = 32 * t + 8 * be
+                    block = [
+                        scale[tile(r), :] * out[j : j + 8, h * COLS : (h + 1) * COLS]
+                        for (_, _, scale), out in zip(terms, outs)
+                    ]
+                    part.append(sum(block[1:], block[0]))
                 if i + t == start:
-                    first[h] = part[0]
+                    first[h] = part[:2]
                 else:
-                    finish(r, part[0] + carry[h])
-                carry[h] = part[1]
-    finish(start, first[0] + carry[1])
-    finish(start + HALF, first[1] + carry[0])
+                    close(r, part[:2], carry[h])
+                carry[h] = part[2:]
+    close(start, first[0], carry[1])
+    close(start + HALF, first[1], carry[0])
 
 
 def weights_of(a_ref, n):
@@ -167,7 +169,7 @@
     for copy in copies[:3]:
         copy.wait()
     slot = lax.broadcasted_iota(jnp.int32, (64, WIDTH), 1)
-    low = ((slot >= 64) & (slot < 96)) | (slot >= 128)
+    low = slot % 48 >= 32
     full = []
     for layer in range(2):
         flip = odd if layer == 0 else jnp.logical_not(odd)
@@ -252,7 +254,7 @@
     (scale,) = take(1) if rnd == 0 else (None,)
     if rnd > 0:
         sd_t, md_t = take(2)
-    u1, w1, fd = take(3)
+    u1, w1, fd, u1_shift = take(4)
     if rnd == 0:
         sd_t, md_t = take(2)
     ur, hr = take(2)
@@ -266,14 +268,19 @@
     def finish(r, force):
         fd[tile(r), :] = force
 
-    sweep(1, [(tile_rows(lambda r: u1[tile(r), :]), weights_of(a_ref, 3), sd_t)], finish)
+    def rotated(r):
+        u1_shift[tile(r), :] = lane_up(u1[tile(r), :])
+        return u1_shift[tile(r), :]
+
+    rows = tile_rows(lambda r: u1[tile(r), :], rotated)
+    sweep(1, [(rows, weights_of(a_ref, 3), sd_t)], finish)
 
 
 def across_body(rnd, *refs):
     refs = list(refs)
     take = lambda n: [refs.pop(0) for _ in range(n)]
     last = rnd == ROUNDS - 1
-    count_ref, place_ref, x_in, u_t, w_t, e_t, m_t, ei_t, h_t, si_t, a_ref, u1d, w1d, fd = take(14)
+    count_ref, place_ref, x_in, u_t, w_t, e_t, m_t, ei_t, h_t, si_t, a_ref, u1d, w1d, fd, u1d_shift = take(15)
     (scale,) = take(1) if rnd == 0 else (None,)
     if rnd > 0:
         sx_t, mx_t = take(2)
@@ -312,11 +319,21 @@
         w2[at, :] = w
         u2[at, :] = middle(r) + act * w
 
+    shifts = {}
+
+    def shift_x(r):
+        if r not in shifts:
+            shifts[r] = lane_up(u1x[tile(r), :])
+        return shifts[r]
+
+    def shift_middle(r):
+        return jnp.where(within, u1d_shift[tile(r), :], shift_x(r))
+
     sweep(
         1,
         [
-            (tile_rows(middle), weights_of(a_ref, 0), si_t),
-            (tile_rows(lambda r: u1x[tile(r), :]), weights_of(a_ref, 2), sx_t),
+            (tile_rows(middle, shift_middle), weights_of(a_ref, 0), si_t),
+            (tile_rows(lambda r: u1x[tile(r), :], shift_x), weights_of(a_ref, 2), sx_t),
         ],
         finish,
     )
@@ -474,29 +491,30 @@
         if rnd == 0:
             inv_before = lax.ppermute(schur_inverse, "grp", FROM_BEFORE)
             before = lax.ppermute(normal, "grp", FROM_BEFORE)
-
-        def within(*refs, rnd=rnd):
-            return within_body(rnd, *refs)
-
-        args = [d, u, w, m, ei, h, a] + ([scale] if rnd == 0 else [sd, md])
-        got = call(
-            within, [TILE] * (5 if rnd == 0 else 3), [TILE] * 2, [SM] * 2 + [VM] * len(args)
-        )(*scalars, *args)
-        u1d, w1d, fd = got[:3]
-        if rnd == 0:
-            sd, md = got[3:]
-            x, inv_before, before = lax.optimization_barrier((x, inv_before, before))
+            d, inv_before, before = lax.optimization_barrier((d, inv_before, before))
+
         if rnd == 1:
             nodes = call(
                 node_body, [b16(32, ROWS), b16(2, ROWS, 16), (32, 6 * COLS), (32, 6 * COLS)], [], [VM] * 5
             )(own_nodes, peer_nodes, normal, before, weight)
-            x, *nodes = lax.optimization_barrier((x, *nodes))
+            d, *nodes = lax.optimization_barrier((d, *nodes))
             pick, pick_t, share, change = nodes
+
+        def within(*refs, rnd=rnd):
+            return within_body(rnd, *refs)
+
+        args = [d, u, w, m, ei, h, a] + ([scale] if rnd == 0 else [sd, md])
+        got = call(
+            within, [TILE] * (6 if rnd == 0 else 4), [TILE] * 2, [SM] * 2 + [VM] * len(args)
+        )(*scalars, *args)
+        u1d, w1d, fd, u1d_shift = got[:4]
+        if rnd == 0:
+            sd, md = got[4:]
 
         def across(*refs, rnd=rnd):
             return across_body(rnd, *refs)
 
-        args = [x, u, w, e, m, ei, h, si, a, u1d, w1d, fd] + ([scale] if rnd == 0 else [sx, mx])
+        args = [x, u, w, e, m, ei, h, si, a, u1d, w1d, fd, u1d_shift] + ([scale] if rnd == 0 else [sx, mx])
         args += [pick, share] if last else []
         outs = [PLANES, PLANES, (128, 2 * COLS)] if last else [PLANES, PLANES] + [TILE] * 4
         outs += [TILE, TILE] if rnd == 0 else []

time: 71.7 us -> 70.5 us (0.983)
  starting transfers between devices: 13.1 us -> 9.37 us
  waiting for transfers between devices: 16.4 us -> 19.2 us
    ppermute x4, starting transfers between devices: 4.78 us -> 1.39 us  [on_device(): x = lax.ppermute(x, ('grp', 'dom'), ACROSS)]
    ppermute x4, waiting for transfers between devices: 9.97 us -> 12.4 us  [on_device(): x = lax.ppermute(x, ('grp', 'dom'), ACROSS)]
    ppermute x4, waiting for transfers between devices: 2.42 us -> 3.24 us  [on_device(): d = lax.ppermute(d, 'dom', WITHIN)]
  transfers between devices with their start and end apart: 10 -> 10, of which waited for: 6 -> 7; matrix products, arithmetic and copies ran while one was open for 0% -> 0% of each run, Pallas kernels for 4% -> 7%
where the time goes in v7:
time: 70.5 us; the launch traced here: 70.3 us
  blocking collectives  22.5 us (32%)
  waiting for transfers between devices  19.2 us (27%)
  Pallas kernels  17.7 us (25%)
  starting transfers between devices  9.37 us (13%)
  between operations  1.42 us (2%)
    all_to_all x1, blocking collectives, on_device(): gathered = lax.all_to_all(gap, ('grp', 'dom'), 0, 0, tiled=True)  22.5 us
    ppermute x4, waiting for transfers between devices, on_device(): x = lax.ppermute(x, ('grp', 'dom'), ACROSS)  12.4 us
    pallas_call x4, Pallas kernels, on_device(): call(across, outs, scratch, [SM] * 2 + [VM] * len(args), far_outs=(0,) if...  9.15 us
    ppermute x4, starting transfers between devices, on_device(): d = lax.ppermute(d, 'dom', WITHIN)  5.55 us
    pallas_call x4, Pallas kernels, on_device(): call(within, [TILE] * (6 if rnd == 0 else 4), [TILE] * 2, [SM] * 2 + [VM]...  4.51 us
    ppermute x1, waiting for transfers between devices, on_device(): before = lax.ppermute(normal, 'grp', FROM_BEFORE)  3.57 us
    ppermute x4, waiting for transfers between devices, on_device(): d = lax.ppermute(d, 'dom', WITHIN)  3.24 us
    pallas_call x1, Pallas kernels, on_device(): call(prep_body, [first, first] + [TILE] * 7 + [b16(256, WIDTH)], [(24, 24...  2.44 us
  transfers between devices with their start and end apart: 10, of which 7 were waited for; matrix products, arithmetic and copies ran while one was open for 0% of the time, Pallas kernels for 7%

profile of v7, /device:TPU:1, one launch (start us, length us, event | category | flops | bytes accessed | tf_op | source)
XLA Modules:
  0.0 70.3 jit_solution(10403983886954943075)
XLA Ops:
  1.3 2.4 %shard_map.140 = (f32[8,96,128]{2,1,0:T(8,128)S(1)}, f32[8,96,128]{2,1,0:T(8,128)S(1)}, f32[768,128]{1,0:T(8,128)S(1)}, f32[768,128]{1,0:T(8,128)S(1)}, f32[768,...) custom-call(s32[1]{0:T(128)S(6)} %copy.22.count_ref.refs_0_, ...), custom_call_target="tpu_custom_call" | custom-call | tf_op jit(solution)/shard_map/pallas_call | solution.py:478
  3.7 0.0 copy-start.5
  3.8 1.5 %collective-permute-start.1 = (f32[8,96,128]{2,1,0:T(8,128)S(1)}, f32[8,96,128]{2,1,0:T(8,128)S(1)}, u32[]{:S(2)}, u32[]{:S(2)}) collective-permute-start(f32[8,96,128]{2,1,0:T(8,128)S(1)} %get-tuple-element.74), channel_id=1, source_target_pairs={{0,1},{1,0},{2,3},{3,2},{4,5},{5,4},{6,7},{7,6},{8,9},{9,8},{10,11... | collective-permute-start | bytes 1179656 | tf_op jit(solution)/shard_map/ppermute | solution.py:490
  5.2 1.4 %collective-permute-start = (f32[8,96,128]{2,1,0:T(8,128)S(1)}, f32[8,96,128]{2,1,0:T(8,128)S(1)}, u32[]{:S(2)}, u32[]{:S(2)}) collective-permute-start(f32[8,96,128]{2,1,0:T(8,128)S(1)} %get-tuple-element.65), channel_id=1, source_target_pairs={{1,2},{3,4},{5,6},{7,8},{9,10},{11,12},{13,14},{15,16},{17,18},{19... | collective-permute-start | bytes 1179656 | tf_op jit(solution)/shard_map/ppermute | solution.py:489
  6.6 1.2 %collective-permute-start.2 = (f32[16,2048]{1,0:T(8,128)S(1)}, f32[16,2048]{1,0:T(8,128)S(1)}, u32[]{:S(2)}, u32[]{:S(2)}) collective-permute-start(f32[16,2048]{1,0:T(8,128)S(1)} %copy-done.2), channel_id=1, source_target_pairs={{0,32},{32,64},{64,96},{96,0},{1,33},{33,65},{65,97},{97,1},{2,34}... | collective-permute-start | bytes 393224 | tf_op jit(solution)/shard_map/ppermute | solution.py:492
  7.8 1.2 %collective-permute-start.3 = (f32[3,16]{1,0:T(4,128)S(1)}, f32[3,16]{1,0:T(4,128)S(1)}, u32[]{:S(2)}, u32[]{:S(2)}) collective-permute-start(f32[3,16]{1,0:T(4,128)S(1)} %bitcast.23), channel_id=1, source_target_pairs={{0,32},{32,64},{64,96},{96,0},{1,33},{33,65},{65,97},{97,1},{2,34}... | collective-permute-start | bytes 584 | tf_op jit(solution)/shard_map/ppermute | solution.py:493
  9.0 3.6 %collective-permute-done.3.before = f32[3,16]{1,0:T(4,128)S(1)} collective-permute-done((f32[3,16]{1,0:T(4,128)S(1)}, f32[3,16]{1,0:T(4,128)S(1)}, u32[]{:S(2)}, u32[]{:S(2)}) %collective-permute-start.3) | collective-permute-done | bytes 224 | tf_op jit(solution)/shard_map/ppermute | solution.py:493
  12.6 0.0 collective-permute-done.2.inv_before
  12.6 1.2 %shard_map.141 = (f32[768,128]{1,0:T(8,128)S(1)}, f32[768,128]{1,0:T(8,128)S(1)}, f32[768,128]{1,0:T(8,128)S(1)}, f32[768,128]{1,0:T(8,128)S(1)}, f32[768,128]{1,0:T(8,128)S(1)}, /*index=5*/f32[768,128]{1,0:T(8,128)S(1)}) custom-call(s32[1]{0:T(128)S(6)} %copy.22.count_ref.refs_0_, s32[1]{0:T(128)} %bitcast.place_ref.refs_1_, ...), custom_call_target="tpu_custom_call" | custom-call | tf_op jit(solution)/shard_map/pallas_call | solution.py:507
  13.8 0.0 copy-start.1
  13.8 2.3 %shard_map.142 = (f32[6,96,128]{2,1,0:T(8,128)S(1)}, f32[6,96,128]{2,1,0:T(8,128)S(1)}, f32[768,128]{1,0:T(8,128)S(1)}, f32[768,128]{1,0:T(8,128)S(1)}, f32[768,...) custom-call(s32[1]{0:T(128)S(6)} %copy.22.count_ref.refs_0_, ...), custom_call_target="tpu_custom_call" | custom-call | tf_op jit(solution)/shard_map/pallas_call | solution.py:522
  16.1 0.0 copy-start.3
  16.1 0.0 copy-start.4
  16.1 2.5 %collective-permute-start.5 = (f32[6,96,128]{2,1,0:T(8,128)S(1)}, f32[6,96,128]{2,1,0:T(8,128)S(1)}, u32[]{:S(2)}, u32[]{:S(2)}) collective-permute-start(f32[6,96,128]{2,1,0:T(8,128)S(1)} %get-tuple-element.85), channel_id=1, source_target_pairs={{0,1},{1,0},{2,3},{3,2},{4,5},{5,4},{6,7},{7,6},{8,9},{9,8},{10,11... | collective-permute-start | bytes 884744 | tf_op jit(solution)/shard_map/ppermute | solution.py:490
  18.7 0.4 shard_map.143
  19.0 0.8 %collective-permute-done.5.refs_2_ = f32[6,96,128]{2,1,0:T(8,128)S(1)} collective-permute-done((f32[6,96,128]{2,1,0:T(8,128)S(1)}, f32[6,96,128]{2,1,0:T(8,128)S(1)}, u32[]{:S(2)}, u32[]{:S(2)}) %collective-permute-start.5) | collective-permute-done | bytes 294944 | tf_op jit(solution)/shard_map/ppermute | solution.py:490
  19.9 1.1 %shard_map.144 = (f32[768,128]{1,0:T(8,128)S(1)}, f32[768,128]{1,0:T(8,128)S(1)}, f32[768,128]{1,0:T(8,128)S(1)}, f32[768,128]{1,0:T(8,128)S(1)}) custom-call(s32[1]{0:T(128)S(6)} %copy.22.count_ref.refs_0_, s32[1]{0:T(128)} %bitcast.place_ref.refs_1_, f32[6,96,128]{2,1,0:T(8,128)S(1)} %collective-permute-done.5.refs_2_, ...), custom_call_target="tpu_custom_call" | custom-call | tf_op jit(solution)/shard_map/pallas_call | solution.py:507
  21.0 4.1 %collective-permute-done.4.refs_2_ = f32[6,96,128]{2,1,0:T(8,128)S(1)} collective-permute-done((f32[6,96,128]{2,1,0:T(8,128)S(1)}, f32[6,96,128]{2,1,0:T(8,128)S(1)}, u32[]{:S(2)}, u32[]{:S(2)}) %collective-permute-start.4) | collective-permute-done | bytes 294944 | tf_op jit(solution)/shard_map/ppermute | solution.py:489
  25.1 2.2 %shard_map.145 = (f32[6,96,128]{2,1,0:T(8,128)S(1)}, f32[6,96,128]{2,1,0:T(8,128)S(1)}, f32[768,128]{1,0:T(8,128)S(1)}, f32[768,128]{1,0:T(8,128)S(1)}, f32[768,128]{1,0:T(8,128)S(1)}, /*index=5*/f32[768,128]{1,0:T(8,128)S(1)}) custom-call(s32[1]{0:T(128)S(6)} %copy.22.count_ref.refs_0_, s32[1]{0:T(128)} %bitcast.place_ref.refs_1_, ...), custom_call_target="tpu_custom_call" | custom-call | tf_op jit(solution)/shard_map/pallas_call | solution.py:522
  27.3 0.9 %collective-permute-start.7 = (f32[6,96,128]{2,1,0:T(8,128)S(1)}, f32[6,96,128]{2,1,0:T(8,128)S(1)}, u32[]{:S(2)}, u32[]{:S(2)}) collective-permute-start(f32[6,96,128]{2,1,0:T(8,128)S(1)} %get-tuple-element.105), channel_id=1, source_target_pairs={{0,1},{1,0},{2,3},{3,2},{4,5},{5,4},{6,7},{7,6},{8,9},{9,8},{10,11... | collective-permute-start | bytes 884744 | tf_op jit(solution)/shard_map/ppermute | solution.py:490
  28.2 1.2 %collective-permute-done.7.refs_2_ = f32[6,96,128]{2,1,0:T(8,128)S(1)} collective-permute-done((f32[6,96,128]{2,1,0:T(8,128)S(1)}, f32[6,96,128]{2,1,0:T(8,128)S(1)}, u32[]{:S(2)}, u32[]{:S(2)}) %collective-permute-start.7) | collective-permute-done | bytes 294944 | tf_op jit(solution)/shard_map/ppermute | solution.py:490
  29.4 1.1 %shard_map.146 = (f32[768,128]{1,0:T(8,128)S(1)}, f32[768,128]{1,0:T(8,128)S(1)}, f32[768,128]{1,0:T(8,128)S(1)}, f32[768,128]{1,0:T(8,128)S(1)}) custom-call(s32[1]{0:T(128)S(6)} %copy.22.count_ref.refs_0_, s32[1]{0:T(128)} %bitcast.place_ref.refs_1_, f32[6,96,128]{2,1,0:T(8,128)S(1)} %collective-permute-done.7.refs_2_, ...), custom_call_target="tpu_custom_call" | custom-call | tf_op jit(solution)/shard_map/pallas_call | solution.py:507
  30.5 4.1 %collective-permute-done.6.refs_2_ = f32[6,96,128]{2,1,0:T(8,128)S(1)} collective-permute-done((f32[6,96,128]{2,1,0:T(8,128)S(1)}, f32[6,96,128]{2,1,0:T(8,128)S(1)}, u32[]{:S(2)}, u32[]{:S(2)}) %collective-permute-start.6) | collective-permute-done | bytes 294944 | tf_op jit(solution)/shard_map/ppermute | solution.py:489
  34.6 2.2 %shard_map.147 = (f32[6,96,128]{2,1,0:T(8,128)S(1)}, f32[6,96,128]{2,1,0:T(8,128)S(1)}, f32[768,128]{1,0:T(8,128)S(1)}, f32[768,128]{1,0:T(8,128)S(1)}, f32[768,128]{1,0:T(8,128)S(1)}, /*index=5*/f32[768,128]{1,0:T(8,128)S(1)}) custom-call(s32[1]{0:T(128)S(6)} %copy.22.count_ref.refs_0_, s32[1]{0:T(128)} %bitcast.place_ref.refs_1_, ...), custom_call_target="tpu_custom_call" | custom-call | tf_op jit(solution)/shard_map/pallas_call | solution.py:522
  36.8 0.7 collective-permute-start.9
  37.5 1.2 %collective-permute-done.9.refs_2_ = f32[6,96,128]{2,1,0:T(8,128)S(1)} collective-permute-done((f32[6,96,128]{2,1,0:T(8,128)S(1)}, f32[6,96,128]{2,1,0:T(8,128)S(1)}, u32[]{:S(2)}, u32[]{:S(2)}) %collective-permute-start.9) | collective-permute-done | bytes 294944 | tf_op jit(solution)/shard_map/ppermute | solution.py:490
  38.7 1.1 %shard_map.148 = (f32[768,128]{1,0:T(8,128)S(1)}, f32[768,128]{1,0:T(8,128)S(1)}, f32[768,128]{1,0:T(8,128)S(1)}, f32[768,128]{1,0:T(8,128)S(1)}) custom-call(s32[1]{0:T(128)S(6)} %copy.22.count_ref.refs_0_, s32[1]{0:T(128)} %bitcast.place_ref.refs_1_, f32[6,96,128]{2,1,0:T(8,128)S(1)} %collective-permute-done.9.refs_2_, ...), custom_call_target="tpu_custom_call" | custom-call | tf_op jit(solution)/shard_map/pallas_call | solution.py:507
  39.8 4.1 %collective-permute-done.8.refs_2_ = f32[6,96,128]{2,1,0:T(8,128)S(1)} collective-permute-done((f32[6,96,128]{2,1,0:T(8,128)S(1)}, f32[6,96,128]{2,1,0:T(8,128)S(1)}, u32[]{:S(2)}, u32[]{:S(2)}) %collective-permute-start.8) | collective-permute-done | bytes 294944 | tf_op jit(solution)/shard_map/ppermute | solution.py:489
  43.9 2.5 %shard_map.149 = (f32[6,96,128]{2,1,0:T(8,128)}, f32[6,96,128]{2,1,0:T(8,128)S(1)}, f32[128,256]{1,0:T(8,128)S(1)}) custom-call(s32[1]{0:T(128)S(6)} %copy.22.count_ref.refs_0_, s32[1]{0:T(128)} %bitcast.place_ref.refs_1_, f32[6,96,128]{2,1,0:T(8,128)S(1)} %collective-permute-done.8.refs_2_, f32[768,128]{1,0:T(8,128)S(1)} %get-tuple-element.111.refs_3_, ...), custom_call_target="tpu_custom_call" | custom-call | tf_op jit(solution)/shard_map/pallas_call | solution.py:522
  46.5 0.1 copy.15
  46.6 22.5 %all_to_all.11 = f32[128,1,256]{2,1,0:T(1,128)S(1)} all-to-all(f32[128,1,256]{2,1,0:T(1,128)S(1)} %copy.15), channel_id=1, replica_groups=mesh['grp'=4,'dom'=32] {'grp','dom'}, dimensions={0} | all-to-all | bytes 262144 | tf_op jit(solution)/shard_map/all_to_all | solution.py:531
  69.1 1.2 %shard_map.150 = f32[6,96,128]{2,1,0:T(8,128)} custom-call(f32[128,256]{1,0:T(8,128)S(1)} %bitcast.19, f32[16,2048]{1,0:T(8,128)S(1)} %copy-done.2, f32[16,2048]{1,0:T(8,128)S(1)} %collective-permute-done.2.inv_before, bf16[2,96,16]{2,1,0:T(8,128)(2,1)S(1)} %get-tuple-element.125.pick_t, f32[32,768]{1,0:T(8,128)S(1)} %get-tuple-element.126.change, ...), custom_call_target="tpu_custom_call" | custom-call | tf_op jit(solution)/shard_map/pallas_call | solution.py:532
  (15 shorter events, 0.0 us)
Async XLA Ops:
  1.3 5.3 %copy-start.2 = (f32[16,2048]{1,0:T(8,128)S(1)}, f32[16,2048]{1,0:T(8,128)}, u32[]{:S(2)}) copy-start(f32[16,2048]{1,0:T(8,128)} %inv_own.1) | copy-start | bytes 393220
  1.3 11.3 %copy-start = (f32[1,2,96,128]{3,2,1,0:T(8,128)S(1)}, f32[1,2,96,128]{3,2,1,0:T(8,128)}, u32[]{:S(2)}) copy-start(f32[1,2,96,128]{3,2,1,0:T(8,128)} %param.17) | copy-start | bytes 294916
  3.7 4.1 %copy-start.5 = (f32[1,3,16]{2,0,1:T(1,128)S(1)}, f32[1,3,16]{2,0,1:T(1,128)}, u32[]{:S(2)}) copy-start(f32[1,3,16]{2,0,1:T(1,128)} %param.22) | copy-start | bytes 580
  3.8 8.8 %collective-permute-start.1 = (f32[8,96,128]{2,1,0:T(8,128)S(1)}, f32[8,96,128]{2,1,0:T(8,128)S(1)}, u32[]{:S(2)}, u32[]{:S(2)}) collective-permute-start(f32[8,96,128]{2,1,0:T(8,128)S(1)} %get-tuple-element.74), channel_id=1, source_target_pairs={{0,1},{1,0},{2,3},{3,2},{4,5},{5,4},{6,7},{7,6},{8,9},{9,8},{10,11... | collective-permute-start | bytes 1179656 | tf_op jit(solution)/shard_map/ppermute | solution.py:490
  5.2 8.6 %collective-permute-start = (f32[8,96,128]{2,1,0:T(8,128)S(1)}, f32[8,96,128]{2,1,0:T(8,128)S(1)}, u32[]{:S(2)}, u32[]{:S(2)}) collective-permute-start(f32[8,96,128]{2,1,0:T(8,128)S(1)} %get-tuple-element.65), channel_id=1, source_target_pairs={{1,2},{3,4},{5,6},{7,8},{9,10},{11,12},{13,14},{15,16},{17,18},{19... | collective-permute-start | bytes 1179656 | tf_op jit(solution)/shard_map/ppermute | solution.py:489
  6.6 6.0 %collective-permute-start.2 = (f32[16,2048]{1,0:T(8,128)S(1)}, f32[16,2048]{1,0:T(8,128)S(1)}, u32[]{:S(2)}, u32[]{:S(2)}) collective-permute-start(f32[16,2048]{1,0:T(8,128)S(1)} %copy-done.2), channel_id=1, source_target_pairs={{0,32},{32,64},{64,96},{96,0},{1,33},{33,65},{65,97},{97,1},{2,34}... | collective-permute-start | bytes 393224 | tf_op jit(solution)/shard_map/ppermute | solution.py:492
  7.8 4.8 %collective-permute-start.3 = (f32[3,16]{1,0:T(4,128)S(1)}, f32[3,16]{1,0:T(4,128)S(1)}, u32[]{:S(2)}, u32[]{:S(2)}) collective-permute-start(f32[3,16]{1,0:T(4,128)S(1)} %bitcast.23), channel_id=1, source_target_pairs={{0,32},{32,64},{64,96},{96,0},{1,33},{33,65},{65,97},{97,1},{2,34}... | collective-permute-start | bytes 584 | tf_op jit(solution)/shard_map/ppermute | solution.py:493
  13.8 4.8 %copy-start.1 = (f32[1,2,96,128]{3,2,1,0:T(8,128)S(1)}, f32[1,2,96,128]{3,2,1,0:T(8,128)}, u32[]{:S(2)}) copy-start(f32[1,2,96,128]{3,2,1,0:T(8,128)} %param.16) | copy-start | bytes 294916
  16.1 2.6 %copy-start.3 = (s32[1,16]{1,0:T(1,128)S(1)}, s32[1,16]{1,0:T(1,128)}, u32[]{:S(2)}) copy-start(s32[1,16]{1,0:T(1,128)} %own.1) | copy-start | bytes 196
  16.1 2.5 %copy-start.4 = (s32[1,16]{1,0:T(1,128)S(1)}, s32[1,16]{1,0:T(1,128)}, u32[]{:S(2)}) copy-start(s32[1,16]{1,0:T(1,128)} %peer.1) | copy-start | bytes 196
  16.1 3.7 %collective-permute-start.5 = (f32[6,96,128]{2,1,0:T(8,128)S(1)}, f32[6,96,128]{2,1,0:T(8,128)S(1)}, u32[]{:S(2)}, u32[]{:S(2)}) collective-permute-start(f32[6,96,128]{2,1,0:T(8,128)S(1)} %get-tuple-element.85), channel_id=1, source_target_pairs={{0,1},{1,0},{2,3},{3,2},{4,5},{5,4},{6,7},{7,6},{8,9},{9,8},{10,11... | collective-permute-start | bytes 884744 | tf_op jit(solution)/shard_map/ppermute | solution.py:490
  18.6 6.4 %collective-permute-start.4 = (f32[6,96,128]{2,1,0:T(8,128)S(1)}, f32[6,96,128]{2,1,0:T(8,128)S(1)}, u32[]{:S(2)}, u32[]{:S(2)}) collective-permute-start(f32[6,96,128]{2,1,0:T(8,128)S(1)} %get-tuple-element.80), channel_id=1, source_target_pairs={{1,2},{3,4},{5,6},{7,8},{9,10},{11,12},{13,14},{15,16},{17,18},{19... | collective-permute-start | bytes 884744 | tf_op jit(solution)/shard_map/ppermute | solution.py:489
  27.3 2.1 %collective-permute-start.7 = (f32[6,96,128]{2,1,0:T(8,128)S(1)}, f32[6,96,128]{2,1,0:T(8,128)S(1)}, u32[]{:S(2)}, u32[]{:S(2)}) collective-permute-start(f32[6,96,128]{2,1,0:T(8,128)S(1)} %get-tuple-element.105), channel_id=1, source_target_pairs={{0,1},{1,0},{2,3},{3,2},{4,5},{5,4},{6,7},{7,6},{8,9},{9,8},{10,11... | collective-permute-start | bytes 884744 | tf_op jit(solution)/shard_map/ppermute | solution.py:490
  28.2 6.4 %collective-permute-start.6 = (f32[6,96,128]{2,1,0:T(8,128)S(1)}, f32[6,96,128]{2,1,0:T(8,128)S(1)}, u32[]{:S(2)}, u32[]{:S(2)}) collective-permute-start(f32[6,96,128]{2,1,0:T(8,128)S(1)} %get-tuple-element.100), channel_id=1, source_target_pairs={{1,2},{3,4},{5,6},{7,8},{9,10},{11,12},{13,14},{15,16},{17,18},{19... | collective-permute-start | bytes 884744 | tf_op jit(solution)/shard_map/ppermute | solution.py:489
  36.8 1.9 %collective-permute-start.9 = (f32[6,96,128]{2,1,0:T(8,128)S(1)}, f32[6,96,128]{2,1,0:T(8,128)S(1)}, u32[]{:S(2)}, u32[]{:S(2)}) collective-permute-start(f32[6,96,128]{2,1,0:T(8,128)S(1)} %get-tuple-element.115), channel_id=1, source_target_pairs={{0,1},{1,0},{2,3},{3,2},{4,5},{5,4},{6,7},{7,6},{8,9},{9,8},{10,11... | collective-permute-start | bytes 884744 | tf_op jit(solution)/shard_map/ppermute | solution.py:490
  37.5 6.4 %collective-permute-start.8 = (f32[6,96,128]{2,1,0:T(8,128)S(1)}, f32[6,96,128]{2,1,0:T(8,128)S(1)}, u32[]{:S(2)}, u32[]{:S(2)}) collective-permute-start(f32[6,96,128]{2,1,0:T(8,128)S(1)} %get-tuple-element.110), channel_id=1, source_target_pairs={{1,2},{3,4},{5,6},{7,8},{9,10},{11,12},{13,14},{15,16},{17,18},{19... | collective-permute-start | bytes 884744 | tf_op jit(solution)/shard_map/ppermute | solution.py:489

commit v8 on v7

--- a/solution.py
+++ b/solution.py
@@ -5,6 +5,7 @@
 from jax.experimental import pallas as pl
 from jax.experimental.pallas import tpu as pltpu
 from jax.sharding import PartitionSpec as P
+
 
 MAXSUB = 8
 ROUNDS = MAXSUB // 2
@@ -211,7 +212,7 @@
     d_msg[7] = scale[1]
 
 
-def taken(rnd, x):
+def taken(x):
     sub = lax.broadcasted_iota(jnp.int32, (8, COLS), 0)
     return (sub % 2 == x) & (sub < 6)
 
@@ -219,7 +220,7 @@
 def outer_step(rnd, x, planes, scale, count_ref, refs):
     u_t, w_t, m_t, ei_t, h_t, a_ref, s_t, mm_t, ur, hr, u1, w1 = refs
     act = jnp.where(count_ref[0] > 2 * rnd, 1.0, 0.0).astype(F32)
-    mask = taken(rnd, 1 - x)
+    mask = taken(1 - x)
     for c in range(3):
         at = every(2 * c + 1 - x)
         ur[at, :] = planes(c)
@@ -291,7 +292,7 @@
         x_msg, d_msg, u2, w2, ei_out, h_out = take(6)
     if rnd == 0:
         sx_t, mx_t = take(2)
-    ur, hr, u1x, w1x, u1 = take(5)
+    ur, hr, u1x, w1x, _ = take(5)
     if last:
         u2, w2, u_nat, sem = take(4)
     place = place_ref[0]
@@ -491,7 +492,6 @@
         if rnd == 0:
             inv_before = lax.ppermute(schur_inverse, "grp", FROM_BEFORE)
             before = lax.ppermute(normal, "grp", FROM_BEFORE)
-            d, inv_before, before = lax.optimization_barrier((d, inv_before, before))
 
         if rnd == 1:
             nodes = call(
@@ -510,6 +510,7 @@
         u1d, w1d, fd, u1d_shift = got[:4]
         if rnd == 0:
             sd, md = got[4:]
+            u1d, inv_before, before = lax.optimization_barrier((u1d, inv_before, before))
 
         def across(*refs, rnd=rnd):
             return across_body(rnd, *refs)

time: 70.5 us -> 70.5 us (level)
  blocking collectives: 22.5 us -> 23.7 us
  waiting for transfers between devices: 19.2 us -> 18.1 us
    all_to_all x1, blocking collectives: 22.5 us -> 23.7 us  [on_device(): gathered = lax.all_to_all(gap, ('grp', 'dom'), 0, 0, tiled=True)]
    ppermute x1, waiting for transfers between devices: 3.57 us -> 2.37 us  [on_device(): before = lax.ppermute(normal, 'grp', FROM_BEFORE)]
  transfers between devices with their start and end apart: 10 -> 10, of which waited for: 7 -> 8; matrix products, arithmetic and copies ran while one was open for 0% -> 0% of each run, Pallas kernels for 7% -> 7%
where the time goes in v8:
time: 70.5 us; the launch traced here: 70.3 us
  blocking collectives  23.7 us (34%)
  waiting for transfers between devices  18.1 us (26%)
  Pallas kernels  17.7 us (25%)
  starting transfers between devices  9.28 us (13%)
  between operations  1.4 us (2%)
    all_to_all x1, blocking collectives, on_device(): gathered = lax.all_to_all(gap, ('grp', 'dom'), 0, 0, tiled=True)  23.7 us
    ppermute x4, waiting for transfers between devices, on_device(): x = lax.ppermute(x, ('grp', 'dom'), ACROSS)  12.5 us
    pallas_call x4, Pallas kernels, on_device(): call(across, outs, scratch, [SM] * 2 + [VM] * len(args), far_outs=(0,) if...  9.15 us
    ppermute x4, starting transfers between devices, on_device(): d = lax.ppermute(d, 'dom', WITHIN)  5.46 us
    pallas_call x4, Pallas kernels, on_device(): call(within, [TILE] * (6 if rnd == 0 else 4), [TILE] * 2, [SM] * 2 + [VM]...  4.5 us
    ppermute x4, waiting for transfers between devices, on_device(): d = lax.ppermute(d, 'dom', WITHIN)  3.24 us
    pallas_call x1, Pallas kernels, on_device(): call(prep_body, [first, first] + [TILE] * 7 + [b16(256, WIDTH)], [(24, 24...  2.44 us
    ppermute x1, waiting for transfers between devices, on_device(): before = lax.ppermute(normal, 'grp', FROM_BEFORE)  2.37 us
  transfers between devices with their start and end apart: 10, of which 8 were waited for; matrix products, arithmetic and copies ran while one was open for 0% of the time, Pallas kernels for 7%

profile of v8, /device:TPU:1, one launch (start us, length us, event | category | flops | bytes accessed | tf_op | source)
XLA Modules:
  0.0 70.3 jit_solution(14551529486023353929)
XLA Ops:
  1.3 2.4 %shard_map.140 = (f32[8,96,128]{2,1,0:T(8,128)S(1)}, f32[8,96,128]{2,1,0:T(8,128)S(1)}, f32[768,128]{1,0:T(8,128)S(1)}, f32[768,128]{1,0:T(8,128)S(1)}, f32[768,...) custom-call(s32[1]{0:T(128)S(6)} %copy.22.count_ref.refs_0_, ...), custom_call_target="tpu_custom_call" | custom-call | tf_op jit(solution)/shard_map/pallas_call | solution.py:479
  3.7 0.0 copy-start.5
  3.8 1.5 %collective-permute-start.1 = (f32[8,96,128]{2,1,0:T(8,128)S(1)}, f32[8,96,128]{2,1,0:T(8,128)S(1)}, u32[]{:S(2)}, u32[]{:S(2)}) collective-permute-start(f32[8,96,128]{2,1,0:T(8,128)S(1)} %get-tuple-element.74), channel_id=1, source_target_pairs={{0,1},{1,0},{2,3},{3,2},{4,5},{5,4},{6,7},{7,6},{8,9},{9,8},{10,11... | collective-permute-start | bytes 1179656 | tf_op jit(solution)/shard_map/ppermute | solution.py:491
  5.2 1.4 %collective-permute-start = (f32[8,96,128]{2,1,0:T(8,128)S(1)}, f32[8,96,128]{2,1,0:T(8,128)S(1)}, u32[]{:S(2)}, u32[]{:S(2)}) collective-permute-start(f32[8,96,128]{2,1,0:T(8,128)S(1)} %get-tuple-element.65), channel_id=1, source_target_pairs={{1,2},{3,4},{5,6},{7,8},{9,10},{11,12},{13,14},{15,16},{17,18},{19... | collective-permute-start | bytes 1179656 | tf_op jit(solution)/shard_map/ppermute | solution.py:490
  6.6 1.2 %collective-permute-start.2 = (f32[16,2048]{1,0:T(8,128)S(1)}, f32[16,2048]{1,0:T(8,128)S(1)}, u32[]{:S(2)}, u32[]{:S(2)}) collective-permute-start(f32[16,2048]{1,0:T(8,128)S(1)} %copy-done.2), channel_id=1, source_target_pairs={{0,32},{32,64},{64,96},{96,0},{1,33},{33,65},{65,97},{97,1},{2,34}... | collective-permute-start | bytes 393224 | tf_op jit(solution)/shard_map/ppermute | solution.py:493
  7.8 1.2 %collective-permute-start.3 = (f32[3,16]{1,0:T(4,128)S(1)}, f32[3,16]{1,0:T(4,128)S(1)}, u32[]{:S(2)}, u32[]{:S(2)}) collective-permute-start(f32[3,16]{1,0:T(4,128)S(1)} %bitcast.23), channel_id=1, source_target_pairs={{0,32},{32,64},{64,96},{96,0},{1,33},{33,65},{65,97},{97,1},{2,34}... | collective-permute-start | bytes 584 | tf_op jit(solution)/shard_map/ppermute | solution.py:494
  9.0 1.2 %shard_map.141 = (f32[768,128]{1,0:T(8,128)S(1)}, f32[768,128]{1,0:T(8,128)S(1)}, f32[768,128]{1,0:T(8,128)S(1)}, f32[768,128]{1,0:T(8,128)S(1)}, f32[768,128]{1,0:T(8,128)S(1)}, /*index=5*/f32[768,128]{1,0:T(8,128)S(1)}) custom-call(s32[1]{0:T(128)S(6)} %copy.22.count_ref.refs_0_, s32[1]{0:T(128)} %bitcast.place_ref.refs_1_, ...), custom_call_target="tpu_custom_call" | custom-call | tf_op jit(solution)/shard_map/pallas_call | solution.py:507
  10.2 2.4 %collective-permute-done.3.before = f32[3,16]{1,0:T(4,128)S(1)} collective-permute-done((f32[3,16]{1,0:T(4,128)S(1)}, f32[3,16]{1,0:T(4,128)S(1)}, u32[]{:S(2)}, u32[]{:S(2)}) %collective-permute-start.3) | collective-permute-done | bytes 224 | tf_op jit(solution)/shard_map/ppermute | solution.py:494
  12.6 0.1 collective-permute-done.refs_2_
  12.7 2.2 %shard_map.142 = (f32[6,96,128]{2,1,0:T(8,128)S(1)}, f32[6,96,128]{2,1,0:T(8,128)S(1)}, f32[768,128]{1,0:T(8,128)S(1)}, f32[768,128]{1,0:T(8,128)S(1)}, f32[768,...) custom-call(s32[1]{0:T(128)S(6)} %copy.22.count_ref.refs_0_, ...), custom_call_target="tpu_custom_call" | custom-call | tf_op jit(solution)/shard_map/pallas_call | solution.py:523
  15.0 0.0 copy-start.3
  15.0 0.0 copy-start.4
  15.0 2.4 %collective-permute-start.5 = (f32[6,96,128]{2,1,0:T(8,128)S(1)}, f32[6,96,128]{2,1,0:T(8,128)S(1)}, u32[]{:S(2)}, u32[]{:S(2)}) collective-permute-start(f32[6,96,128]{2,1,0:T(8,128)S(1)} %get-tuple-element.85), channel_id=1, source_target_pairs={{0,1},{1,0},{2,3},{3,2},{4,5},{5,4},{6,7},{7,6},{8,9},{9,8},{10,11... | collective-permute-start | bytes 884744 | tf_op jit(solution)/shard_map/ppermute | solution.py:491
  17.4 0.0 collective-permute-start.4
  17.4 0.4 shard_map.143
  17.8 0.8 %collective-permute-done.5.refs_2_ = f32[6,96,128]{2,1,0:T(8,128)S(1)} collective-permute-done((f32[6,96,128]{2,1,0:T(8,128)S(1)}, f32[6,96,128]{2,1,0:T(8,128)S(1)}, u32[]{:S(2)}, u32[]{:S(2)}) %collective-permute-start.5) | collective-permute-done | bytes 294944 | tf_op jit(solution)/shard_map/ppermute | solution.py:491
  18.6 1.1 %shard_map.144 = (f32[768,128]{1,0:T(8,128)S(1)}, f32[768,128]{1,0:T(8,128)S(1)}, f32[768,128]{1,0:T(8,128)S(1)}, f32[768,128]{1,0:T(8,128)S(1)}) custom-call(s32[1]{0:T(128)S(6)} %copy.22.count_ref.refs_0_, s32[1]{0:T(128)} %bitcast.place_ref.refs_1_, f32[6,96,128]{2,1,0:T(8,128)S(1)} %collective-permute-done.5.refs_2_, ...), custom_call_target="tpu_custom_call" | custom-call | tf_op jit(solution)/shard_map/pallas_call | solution.py:507
  19.7 4.1 %collective-permute-done.4.refs_2_ = f32[6,96,128]{2,1,0:T(8,128)S(1)} collective-permute-done((f32[6,96,128]{2,1,0:T(8,128)S(1)}, f32[6,96,128]{2,1,0:T(8,128)S(1)}, u32[]{:S(2)}, u32[]{:S(2)}) %collective-permute-start.4) | collective-permute-done | bytes 294944 | tf_op jit(solution)/shard_map/ppermute | solution.py:490
  23.9 2.2 %shard_map.145 = (f32[6,96,128]{2,1,0:T(8,128)S(1)}, f32[6,96,128]{2,1,0:T(8,128)S(1)}, f32[768,128]{1,0:T(8,128)S(1)}, f32[768,128]{1,0:T(8,128)S(1)}, f32[768,128]{1,0:T(8,128)S(1)}, /*index=5*/f32[768,128]{1,0:T(8,128)S(1)}) custom-call(s32[1]{0:T(128)S(6)} %copy.22.count_ref.refs_0_, s32[1]{0:T(128)} %bitcast.place_ref.refs_1_, ...), custom_call_target="tpu_custom_call" | custom-call | tf_op jit(solution)/shard_map/pallas_call | solution.py:523
  26.0 0.9 %collective-permute-start.7 = (f32[6,96,128]{2,1,0:T(8,128)S(1)}, f32[6,96,128]{2,1,0:T(8,128)S(1)}, u32[]{:S(2)}, u32[]{:S(2)}) collective-permute-start(f32[6,96,128]{2,1,0:T(8,128)S(1)} %get-tuple-element.105), channel_id=1, source_target_pairs={{0,1},{1,0},{2,3},{3,2},{4,5},{5,4},{6,7},{7,6},{8,9},{9,8},{10,11... | collective-permute-start | bytes 884744 | tf_op jit(solution)/shard_map/ppermute | solution.py:491
  27.0 1.2 %collective-permute-done.7.refs_2_ = f32[6,96,128]{2,1,0:T(8,128)S(1)} collective-permute-done((f32[6,96,128]{2,1,0:T(8,128)S(1)}, f32[6,96,128]{2,1,0:T(8,128)S(1)}, u32[]{:S(2)}, u32[]{:S(2)}) %collective-permute-start.7) | collective-permute-done | bytes 294944 | tf_op jit(solution)/shard_map/ppermute | solution.py:491
  28.2 1.1 %shard_map.146 = (f32[768,128]{1,0:T(8,128)S(1)}, f32[768,128]{1,0:T(8,128)S(1)}, f32[768,128]{1,0:T(8,128)S(1)}, f32[768,128]{1,0:T(8,128)S(1)}) custom-call(s32[1]{0:T(128)S(6)} %copy.22.count_ref.refs_0_, s32[1]{0:T(128)} %bitcast.place_ref.refs_1_, f32[6,96,128]{2,1,0:T(8,128)S(1)} %collective-permute-done.7.refs_2_, ...), custom_call_target="tpu_custom_call" | custom-call | tf_op jit(solution)/shard_map/pallas_call | solution.py:507
  29.3 4.1 %collective-permute-done.6.refs_2_ = f32[6,96,128]{2,1,0:T(8,128)S(1)} collective-permute-done((f32[6,96,128]{2,1,0:T(8,128)S(1)}, f32[6,96,128]{2,1,0:T(8,128)S(1)}, u32[]{:S(2)}, u32[]{:S(2)}) %collective-permute-start.6) | collective-permute-done | bytes 294944 | tf_op jit(solution)/shard_map/ppermute | solution.py:490
  33.4 2.2 %shard_map.147 = (f32[6,96,128]{2,1,0:T(8,128)S(1)}, f32[6,96,128]{2,1,0:T(8,128)S(1)}, f32[768,128]{1,0:T(8,128)S(1)}, f32[768,128]{1,0:T(8,128)S(1)}, f32[768,128]{1,0:T(8,128)S(1)}, /*index=5*/f32[768,128]{1,0:T(8,128)S(1)}) custom-call(s32[1]{0:T(128)S(6)} %copy.22.count_ref.refs_0_, s32[1]{0:T(128)} %bitcast.place_ref.refs_1_, ...), custom_call_target="tpu_custom_call" | custom-call | tf_op jit(solution)/shard_map/pallas_call | solution.py:523
  35.6 0.6 collective-permute-start.9
  36.3 1.2 %collective-permute-done.9.refs_2_ = f32[6,96,128]{2,1,0:T(8,128)S(1)} collective-permute-done((f32[6,96,128]{2,1,0:T(8,128)S(1)}, f32[6,96,128]{2,1,0:T(8,128)S(1)}, u32[]{:S(2)}, u32[]{:S(2)}) %collective-permute-start.9) | collective-permute-done | bytes 294944 | tf_op jit(solution)/shard_map/ppermute | solution.py:491
  37.5 1.1 %shard_map.148 = (f32[768,128]{1,0:T(8,128)S(1)}, f32[768,128]{1,0:T(8,128)S(1)}, f32[768,128]{1,0:T(8,128)S(1)}, f32[768,128]{1,0:T(8,128)S(1)}) custom-call(s32[1]{0:T(128)S(6)} %copy.22.count_ref.refs_0_, s32[1]{0:T(128)} %bitcast.place_ref.refs_1_, f32[6,96,128]{2,1,0:T(8,128)S(1)} %collective-permute-done.9.refs_2_, ...), custom_call_target="tpu_custom_call" | custom-call | tf_op jit(solution)/shard_map/pallas_call | solution.py:507
  38.6 4.1 %collective-permute-done.8.refs_2_ = f32[6,96,128]{2,1,0:T(8,128)S(1)} collective-permute-done((f32[6,96,128]{2,1,0:T(8,128)S(1)}, f32[6,96,128]{2,1,0:T(8,128)S(1)}, u32[]{:S(2)}, u32[]{:S(2)}) %collective-permute-start.8) | collective-permute-done | bytes 294944 | tf_op jit(solution)/shard_map/ppermute | solution.py:490
  42.7 2.5 %shard_map.149 = (f32[6,96,128]{2,1,0:T(8,128)}, f32[6,96,128]{2,1,0:T(8,128)S(1)}, f32[128,256]{1,0:T(8,128)S(1)}) custom-call(s32[1]{0:T(128)S(6)} %copy.22.count_ref.refs_0_, s32[1]{0:T(128)} %bitcast.place_ref.refs_1_, f32[6,96,128]{2,1,0:T(8,128)S(1)} %collective-permute-done.8.refs_2_, f32[768,128]{1,0:T(8,128)S(1)} %get-tuple-element.111.refs_3_, ...), custom_call_target="tpu_custom_call" | custom-call | tf_op jit(solution)/shard_map/pallas_call | solution.py:523
  45.3 0.1 copy.15
  45.4 23.7 %all_to_all.11 = f32[128,1,256]{2,1,0:T(1,128)S(1)} all-to-all(f32[128,1,256]{2,1,0:T(1,128)S(1)} %copy.15), channel_id=1, replica_groups=mesh['grp'=4,'dom'=32] {'grp','dom'}, dimensions={0} | all-to-all | bytes 262144 | tf_op jit(solution)/shard_map/all_to_all | solution.py:532
  69.1 1.2 %shard_map.150 = f32[6,96,128]{2,1,0:T(8,128)} custom-call(f32[128,256]{1,0:T(8,128)S(1)} %bitcast.19, f32[16,2048]{1,0:T(8,128)S(1)} %copy-done.2, f32[16,2048]{1,0:T(8,128)S(1)} %collective-permute-done.2.inv_before, bf16[2,96,16]{2,1,0:T(8,128)(2,1)S(1)} %get-tuple-element.125.pick_t, f32[32,768]{1,0:T(8,128)S(1)} %get-tuple-element.126.change, ...), custom_call_target="tpu_custom_call" | custom-call | tf_op jit(solution)/shard_map/pallas_call | solution.py:533
  (15 shorter events, 0.0 us)
Async XLA Ops:
  1.3 5.3 %copy-start.2 = (f32[16,2048]{1,0:T(8,128)S(1)}, f32[16,2048]{1,0:T(8,128)}, u32[]{:S(2)}) copy-start(f32[16,2048]{1,0:T(8,128)} %inv_own.1) | copy-start | bytes 393220
  1.3 7.7 %copy-start = (f32[1,2,96,128]{3,2,1,0:T(8,128)S(1)}, f32[1,2,96,128]{3,2,1,0:T(8,128)}, u32[]{:S(2)}) copy-start(f32[1,2,96,128]{3,2,1,0:T(8,128)} %param.17) | copy-start | bytes 294916
  3.7 4.1 %copy-start.5 = (f32[1,3,16]{2,0,1:T(1,128)S(1)}, f32[1,3,16]{2,0,1:T(1,128)}, u32[]{:S(2)}) copy-start(f32[1,3,16]{2,0,1:T(1,128)} %param.22) | copy-start | bytes 580
  3.8 5.3 %collective-permute-start.1 = (f32[8,96,128]{2,1,0:T(8,128)S(1)}, f32[8,96,128]{2,1,0:T(8,128)S(1)}, u32[]{:S(2)}, u32[]{:S(2)}) collective-permute-start(f32[8,96,128]{2,1,0:T(8,128)S(1)} %get-tuple-element.74), channel_id=1, source_target_pairs={{0,1},{1,0},{2,3},{3,2},{4,5},{5,4},{6,7},{7,6},{8,9},{9,8},{10,11... | collective-permute-start | bytes 1179656 | tf_op jit(solution)/shard_map/ppermute | solution.py:491
  5.2 7.5 %collective-permute-start = (f32[8,96,128]{2,1,0:T(8,128)S(1)}, f32[8,96,128]{2,1,0:T(8,128)S(1)}, u32[]{:S(2)}, u32[]{:S(2)}) collective-permute-start(f32[8,96,128]{2,1,0:T(8,128)S(1)} %get-tuple-element.65), channel_id=1, source_target_pairs={{1,2},{3,4},{5,6},{7,8},{9,10},{11,12},{13,14},{15,16},{17,18},{19... | collective-permute-start | bytes 1179656 | tf_op jit(solution)/shard_map/ppermute | solution.py:490
  6.6 6.0 %collective-permute-start.2 = (f32[16,2048]{1,0:T(8,128)S(1)}, f32[16,2048]{1,0:T(8,128)S(1)}, u32[]{:S(2)}, u32[]{:S(2)}) collective-permute-start(f32[16,2048]{1,0:T(8,128)S(1)} %copy-done.2), channel_id=1, source_target_pairs={{0,32},{32,64},{64,96},{96,0},{1,33},{33,65},{65,97},{97,1},{2,34}... | collective-permute-start | bytes 393224 | tf_op jit(solution)/shard_map/ppermute | solution.py:493
  7.8 4.8 %collective-permute-start.3 = (f32[3,16]{1,0:T(4,128)S(1)}, f32[3,16]{1,0:T(4,128)S(1)}, u32[]{:S(2)}, u32[]{:S(2)}) collective-permute-start(f32[3,16]{1,0:T(4,128)S(1)} %bitcast.23), channel_id=1, source_target_pairs={{0,32},{32,64},{64,96},{96,0},{1,33},{33,65},{65,97},{97,1},{2,34}... | collective-permute-start | bytes 584 | tf_op jit(solution)/shard_map/ppermute | solution.py:494
  12.7 4.7 %copy-start.1 = (f32[1,2,96,128]{3,2,1,0:T(8,128)S(1)}, f32[1,2,96,128]{3,2,1,0:T(8,128)}, u32[]{:S(2)}) copy-start(f32[1,2,96,128]{3,2,1,0:T(8,128)} %param.16) | copy-start | bytes 294916
  15.0 2.5 %copy-start.3 = (s32[1,16]{1,0:T(1,128)S(1)}, s32[1,16]{1,0:T(1,128)}, u32[]{:S(2)}) copy-start(s32[1,16]{1,0:T(1,128)} %own.1) | copy-start | bytes 196
  15.0 2.5 %copy-start.4 = (s32[1,16]{1,0:T(1,128)S(1)}, s32[1,16]{1,0:T(1,128)}, u32[]{:S(2)}) copy-start(s32[1,16]{1,0:T(1,128)} %peer.1) | copy-start | bytes 196
  15.0 3.6 %collective-permute-start.5 = (f32[6,96,128]{2,1,0:T(8,128)S(1)}, f32[6,96,128]{2,1,0:T(8,128)S(1)}, u32[]{:S(2)}, u32[]{:S(2)}) collective-permute-start(f32[6,96,128]{2,1,0:T(8,128)S(1)} %get-tuple-element.85), channel_id=1, source_target_pairs={{0,1},{1,0},{2,3},{3,2},{4,5},{5,4},{6,7},{7,6},{8,9},{9,8},{10,11... | collective-permute-start | bytes 884744 | tf_op jit(solution)/shard_map/ppermute | solution.py:491
  17.4 6.4 %collective-permute-start.4 = (f32[6,96,128]{2,1,0:T(8,128)S(1)}, f32[6,96,128]{2,1,0:T(8,128)S(1)}, u32[]{:S(2)}, u32[]{:S(2)}) collective-permute-start(f32[6,96,128]{2,1,0:T(8,128)S(1)} %get-tuple-element.80), channel_id=1, source_target_pairs={{1,2},{3,4},{5,6},{7,8},{9,10},{11,12},{13,14},{15,16},{17,18},{19... | collective-permute-start | bytes 884744 | tf_op jit(solution)/shard_map/ppermute | solution.py:490
  26.0 2.1 %collective-permute-start.7 = (f32[6,96,128]{2,1,0:T(8,128)S(1)}, f32[6,96,128]{2,1,0:T(8,128)S(1)}, u32[]{:S(2)}, u32[]{:S(2)}) collective-permute-start(f32[6,96,128]{2,1,0:T(8,128)S(1)} %get-tuple-element.105), channel_id=1, source_target_pairs={{0,1},{1,0},{2,3},{3,2},{4,5},{5,4},{6,7},{7,6},{8,9},{9,8},{10,11... | collective-permute-start | bytes 884744 | tf_op jit(solution)/shard_map/ppermute | solution.py:491
  27.0 6.4 %collective-permute-start.6 = (f32[6,96,128]{2,1,0:T(8,128)S(1)}, f32[6,96,128]{2,1,0:T(8,128)S(1)}, u32[]{:S(2)}, u32[]{:S(2)}) collective-permute-start(f32[6,96,128]{2,1,0:T(8,128)S(1)} %get-tuple-element.100), channel_id=1, source_target_pairs={{1,2},{3,4},{5,6},{7,8},{9,10},{11,12},{13,14},{15,16},{17,18},{19... | collective-permute-start | bytes 884744 | tf_op jit(solution)/shard_map/ppermute | solution.py:490
  35.6 1.9 %collective-permute-start.9 = (f32[6,96,128]{2,1,0:T(8,128)S(1)}, f32[6,96,128]{2,1,0:T(8,128)S(1)}, u32[]{:S(2)}, u32[]{:S(2)}) collective-permute-start(f32[6,96,128]{2,1,0:T(8,128)S(1)} %get-tuple-element.115), channel_id=1, source_target_pairs={{0,1},{1,0},{2,3},{3,2},{4,5},{5,4},{6,7},{7,6},{8,9},{9,8},{10,11... | collective-permute-start | bytes 884744 | tf_op jit(solution)/shard_map/ppermute | solution.py:491
  36.3 6.4 %collective-permute-start.8 = (f32[6,96,128]{2,1,0:T(8,128)S(1)}, f32[6,96,128]{2,1,0:T(8,128)S(1)}, u32[]{:S(2)}, u32[]{:S(2)}) collective-permute-start(f32[6,96,128]{2,1,0:T(8,128)S(1)} %get-tuple-element.110), channel_id=1, source_target_pairs={{1,2},{3,4},{5,6},{7,8},{9,10},{11,12},{13,14},{15,16},{17,18},{19... | collective-permute-start | bytes 884744 | tf_op jit(solution)/shard_map/ppermute | solution.py:490

commit v9 on v8

--- a/solution.py
+++ b/solution.py
@@ -294,7 +294,7 @@
         sx_t, mx_t = take(2)
     ur, hr, u1x, w1x, _ = take(5)
     if last:
-        u2, w2, u_nat, sem = take(4)
+        u2, w2 = take(2)
     place = place_ref[0]
     odd = place % 2 == 1
     inside = (place > 0) & (place < DOMS - 1)
@@ -339,18 +339,15 @@
         finish,
     )
     if last:
-        back = step_size(count_ref)[0:1]
-        for c in range(3):
-            for src, out, scaled in ((u2, u_nat, False), (w2, v_out, True)):
+        back = 1.0 / step_size(count_ref)[0:1]
+        for src, out, scaled in ((w2, v_out, True), (u2, u_out, False)):
+            for c in range(3):
                 here, there = src[every(2 * c), :], src[every(2 * c + 1), :]
                 if scaled:
-                    here, there = here / back, there / back
+                    here, there = here * back, there * back
                 out[2 * c] = jnp.where(odd, there, here)
                 out[2 * c + 1] = jnp.where(odd, here, there)
-        copy = pltpu.make_async_copy(u_nat, u_out, sem)
-        copy.start()
         partial_gaps(place_ref, pick, share, v_out, g_out)
-        copy.wait()
         return
     inner_pass(a_ref, si_t, e_t, m_t, u2, w2, ei_out, h_out)
     send_edges(u2, h_out, x_msg, d_msg)
@@ -412,7 +409,9 @@
         g_out[:, side * COLS : (side + 1) * COLS] = jnp.broadcast_to(part, (128, COLS))
 
 
-def final_body(gathered, inv_own, inv_before, pick_t, change, v_in, v_out):
+def final_body(gathered, inv_own, inv_before, pick_t, change, u_in, v_in, u_out, v_out, plane, sems):
+    copies = [pltpu.make_async_copy(u_in, u_out, sems.at[6])]
+    copies[0].start()
     mine = jnp.sum(gathered[:, 0:COLS].reshape(16, 8, COLS), axis=1)
     other = jnp.sum(gathered[:, COLS : 2 * COLS].reshape(16, 8, COLS), axis=1)
     gap = mine + jnp.concatenate([other[4:16], other[0:4]], 0)
@@ -425,7 +424,11 @@
         part = chosen(pick_t[side], change[16 * side : 16 * side + 16, :] * lam)
         total = part if total is None else total + part
     for q in range(6):
-        v_out[q] = v_in[q] + total[:, q * COLS : (q + 1) * COLS]
+        plane[q] = v_in[q] + total[:, q * COLS : (q + 1) * COLS]
+        copies.append(pltpu.make_async_copy(plane.at[q], v_out.at[q], sems.at[q]))
+        copies[-1].start()
+    for copy in copies:
+        copy.wait()
 
 
 def call(body, outs, scratch, ins, limit=24 * 1024 * 1024, far_outs=()):
@@ -519,10 +522,8 @@
         args += [pick, share] if last else []
         outs = [PLANES, PLANES, (128, 2 * COLS)] if last else [PLANES, PLANES] + [TILE] * 4
         outs += [TILE, TILE] if rnd == 0 else []
-        scratch = [TILE] * 5 + ([TILE, TILE, PLANES, pltpu.SemaphoreType.DMA] if last else [])
-        got = call(
-            across, outs, scratch, [SM] * 2 + [VM] * len(args), far_outs=(0,) if last else ()
-        )(*scalars, *args)
+        scratch = [TILE] * 5 + ([TILE, TILE] if last else [])
+        got = call(across, outs, scratch, [SM] * 2 + [VM] * len(args))(*scalars, *args)
         if last:
             u, v, gap = got
         else:
@@ -530,9 +531,9 @@
         if rnd == 0:
             sx, mx = got[6:]
     gathered = lax.all_to_all(gap, ("grp", "dom"), 0, 0, tiled=True)
-    (v,) = call(final_body, [PLANES], [], [VM] * 6)(
-        gathered, schur_inverse, inv_before, pick_t, change, v
-    )
+    u, v = call(
+        final_body, [PLANES, PLANES], [PLANES, pltpu.SemaphoreType.DMA((7,))], [VM] * 7, far_outs=(0, 1)
+    )(gathered, schur_inverse, inv_before, pick_t, change, u, v)
     shape = displacement.shape
     return u.reshape(shape), v.reshape(shape)
 

time: 70.5 us -> 70.2 us (level)
  no operation moved by 1% of the time
where the time goes in v9:
time: 70.2 us; the launch traced here: 70.1 us
  blocking collectives  23.7 us (34%)
  waiting for transfers between devices  18.1 us (26%)
  Pallas kernels  17.3 us (25%)
  starting transfers between devices  9.28 us (13%)
  between operations  1.56 us (2%)
    all_to_all x1, blocking collectives, on_device(): gathered = lax.all_to_all(gap, ('grp', 'dom'), 0, 0, tiled=True)  23.7 us
    ppermute x4, waiting for transfers between devices, on_device(): x = lax.ppermute(x, ('grp', 'dom'), ACROSS)  12.5 us
    pallas_call x4, Pallas kernels, on_device(): call(across, outs, scratch, [SM] * 2 + [VM] * len(args))(*scalars, *args)  8.75 us
    ppermute x4, starting transfers between devices, on_device(): d = lax.ppermute(d, 'dom', WITHIN)  5.47 us
    pallas_call x4, Pallas kernels, on_device(): call(within, [TILE] * (6 if rnd == 0 else 4), [TILE] * 2, [SM] * 2 + [VM]...  4.53 us
    ppermute x4, waiting for transfers between devices, on_device(): d = lax.ppermute(d, 'dom', WITHIN)  3.24 us
    pallas_call x1, Pallas kernels, on_device(): call(prep_body, [first, first] + [TILE] * 7 + [b16(256, WIDTH)], [(24, 24...  2.44 us
    ppermute x1, waiting for transfers between devices, on_device(): before = lax.ppermute(normal, 'grp', FROM_BEFORE)  2.37 us
  transfers between devices with their start and end apart: 10, of which 8 were waited for; matrix products, arithmetic and copies ran while one was open for 0% of the time, Pallas kernels for 7%

profile of v9, /device:TPU:1, one launch (start us, length us, event | category | flops | bytes accessed | tf_op | source)
XLA Modules:
  0.0 70.1 jit_solution(891495417318659920)
XLA Ops:
  1.3 2.4 %shard_map.140 = (f32[8,96,128]{2,1,0:T(8,128)S(1)}, f32[8,96,128]{2,1,0:T(8,128)S(1)}, f32[768,128]{1,0:T(8,128)S(1)}, f32[768,128]{1,0:T(8,128)S(1)}, f32[768,...) custom-call(s32[1]{0:T(128)S(6)} %copy.22.count_ref.refs_0_, ...), custom_call_target="tpu_custom_call" | custom-call | tf_op jit(solution)/shard_map/pallas_call | solution.py:482
  3.7 0.0 copy-start.5
  3.8 1.5 %collective-permute-start.1 = (f32[8,96,128]{2,1,0:T(8,128)S(1)}, f32[8,96,128]{2,1,0:T(8,128)S(1)}, u32[]{:S(2)}, u32[]{:S(2)}) collective-permute-start(f32[8,96,128]{2,1,0:T(8,128)S(1)} %get-tuple-element.76), channel_id=1, source_target_pairs={{0,1},{1,0},{2,3},{3,2},{4,5},{5,4},{6,7},{7,6},{8,9},{9,8},{10,11... | collective-permute-start | bytes 1179656 | tf_op jit(solution)/shard_map/ppermute | solution.py:494
  5.2 1.4 %collective-permute-start = (f32[8,96,128]{2,1,0:T(8,128)S(1)}, f32[8,96,128]{2,1,0:T(8,128)S(1)}, u32[]{:S(2)}, u32[]{:S(2)}) collective-permute-start(f32[8,96,128]{2,1,0:T(8,128)S(1)} %get-tuple-element.67), channel_id=1, source_target_pairs={{1,2},{3,4},{5,6},{7,8},{9,10},{11,12},{13,14},{15,16},{17,18},{19... | collective-permute-start | bytes 1179656 | tf_op jit(solution)/shard_map/ppermute | solution.py:493
  6.6 1.2 %collective-permute-start.2 = (f32[16,2048]{1,0:T(8,128)S(1)}, f32[16,2048]{1,0:T(8,128)S(1)}, u32[]{:S(2)}, u32[]{:S(2)}) collective-permute-start(f32[16,2048]{1,0:T(8,128)S(1)} %copy-done.2), channel_id=1, source_target_pairs={{0,32},{32,64},{64,96},{96,0},{1,33},{33,65},{65,97},{97,1},{2,34}... | collective-permute-start | bytes 393224 | tf_op jit(solution)/shard_map/ppermute | solution.py:496
  7.8 1.2 %collective-permute-start.3 = (f32[3,16]{1,0:T(4,128)S(1)}, f32[3,16]{1,0:T(4,128)S(1)}, u32[]{:S(2)}, u32[]{:S(2)}) collective-permute-start(f32[3,16]{1,0:T(4,128)S(1)} %bitcast.23), channel_id=1, source_target_pairs={{0,32},{32,64},{64,96},{96,0},{1,33},{33,65},{65,97},{97,1},{2,34}... | collective-permute-start | bytes 584 | tf_op jit(solution)/shard_map/ppermute | solution.py:497
  9.0 1.2 %shard_map.141 = (f32[768,128]{1,0:T(8,128)S(1)}, f32[768,128]{1,0:T(8,128)S(1)}, f32[768,128]{1,0:T(8,128)S(1)}, f32[768,128]{1,0:T(8,128)S(1)}, f32[768,128]{1,0:T(8,128)S(1)}, /*index=5*/f32[768,128]{1,0:T(8,128)S(1)}) custom-call(s32[1]{0:T(128)S(6)} %copy.22.count_ref.refs_0_, s32[1]{0:T(128)} %bitcast.place_ref.refs_1_, ...), custom_call_target="tpu_custom_call" | custom-call | tf_op jit(solution)/shard_map/pallas_call | solution.py:510
  10.2 2.4 %collective-permute-done.3.before = f32[3,16]{1,0:T(4,128)S(1)} collective-permute-done((f32[3,16]{1,0:T(4,128)S(1)}, f32[3,16]{1,0:T(4,128)S(1)}, u32[]{:S(2)}, u32[]{:S(2)}) %collective-permute-start.3) | collective-permute-done | bytes 224 | tf_op jit(solution)/shard_map/ppermute | solution.py:497
  12.6 0.1 collective-permute-done.refs_2_
  12.7 2.2 %shard_map.142 = (f32[6,96,128]{2,1,0:T(8,128)S(1)}, f32[6,96,128]{2,1,0:T(8,128)S(1)}, f32[768,128]{1,0:T(8,128)S(1)}, f32[768,128]{1,0:T(8,128)S(1)}, f32[768,...) custom-call(s32[1]{0:T(128)S(6)} %copy.22.count_ref.refs_0_, ...), custom_call_target="tpu_custom_call" | custom-call | tf_op jit(solution)/shard_map/pallas_call | solution.py:526
  15.0 0.0 copy-start.3
  15.0 0.0 copy-start.4
  15.0 2.4 %collective-permute-start.5 = (f32[6,96,128]{2,1,0:T(8,128)S(1)}, f32[6,96,128]{2,1,0:T(8,128)S(1)}, u32[]{:S(2)}, u32[]{:S(2)}) collective-permute-start(f32[6,96,128]{2,1,0:T(8,128)S(1)} %get-tuple-element.87), channel_id=1, source_target_pairs={{0,1},{1,0},{2,3},{3,2},{4,5},{5,4},{6,7},{7,6},{8,9},{9,8},{10,11... | collective-permute-start | bytes 884744 | tf_op jit(solution)/shard_map/ppermute | solution.py:494
  17.4 0.0 collective-permute-start.4
  17.4 0.4 shard_map.143
  17.8 0.8 %collective-permute-done.5.refs_2_ = f32[6,96,128]{2,1,0:T(8,128)S(1)} collective-permute-done((f32[6,96,128]{2,1,0:T(8,128)S(1)}, f32[6,96,128]{2,1,0:T(8,128)S(1)}, u32[]{:S(2)}, u32[]{:S(2)}) %collective-permute-start.5) | collective-permute-done | bytes 294944 | tf_op jit(solution)/shard_map/ppermute | solution.py:494
  18.6 1.1 %shard_map.144 = (f32[768,128]{1,0:T(8,128)S(1)}, f32[768,128]{1,0:T(8,128)S(1)}, f32[768,128]{1,0:T(8,128)S(1)}, f32[768,128]{1,0:T(8,128)S(1)}) custom-call(s32[1]{0:T(128)S(6)} %copy.22.count_ref.refs_0_, s32[1]{0:T(128)} %bitcast.place_ref.refs_1_, f32[6,96,128]{2,1,0:T(8,128)S(1)} %collective-permute-done.5.refs_2_, ...), custom_call_target="tpu_custom_call" | custom-call | tf_op jit(solution)/shard_map/pallas_call | solution.py:510
  19.7 4.1 %collective-permute-done.4.refs_2_ = f32[6,96,128]{2,1,0:T(8,128)S(1)} collective-permute-done((f32[6,96,128]{2,1,0:T(8,128)S(1)}, f32[6,96,128]{2,1,0:T(8,128)S(1)}, u32[]{:S(2)}, u32[]{:S(2)}) %collective-permute-start.4) | collective-permute-done | bytes 294944 | tf_op jit(solution)/shard_map/ppermute | solution.py:493
  23.9 2.2 %shard_map.145 = (f32[6,96,128]{2,1,0:T(8,128)S(1)}, f32[6,96,128]{2,1,0:T(8,128)S(1)}, f32[768,128]{1,0:T(8,128)S(1)}, f32[768,128]{1,0:T(8,128)S(1)}, f32[768,128]{1,0:T(8,128)S(1)}, /*index=5*/f32[768,128]{1,0:T(8,128)S(1)}) custom-call(s32[1]{0:T(128)S(6)} %copy.22.count_ref.refs_0_, s32[1]{0:T(128)} %bitcast.place_ref.refs_1_, ...), custom_call_target="tpu_custom_call" | custom-call | tf_op jit(solution)/shard_map/pallas_call | solution.py:526
  26.0 0.9 %collective-permute-start.7 = (f32[6,96,128]{2,1,0:T(8,128)S(1)}, f32[6,96,128]{2,1,0:T(8,128)S(1)}, u32[]{:S(2)}, u32[]{:S(2)}) collective-permute-start(f32[6,96,128]{2,1,0:T(8,128)S(1)} %get-tuple-element.107), channel_id=1, source_target_pairs={{0,1},{1,0},{2,3},{3,2},{4,5},{5,4},{6,7},{7,6},{8,9},{9,8},{10,11... | collective-permute-start | bytes 884744 | tf_op jit(solution)/shard_map/ppermute | solution.py:494
  27.0 1.2 %collective-permute-done.7.refs_2_ = f32[6,96,128]{2,1,0:T(8,128)S(1)} collective-permute-done((f32[6,96,128]{2,1,0:T(8,128)S(1)}, f32[6,96,128]{2,1,0:T(8,128)S(1)}, u32[]{:S(2)}, u32[]{:S(2)}) %collective-permute-start.7) | collective-permute-done | bytes 294944 | tf_op jit(solution)/shard_map/ppermute | solution.py:494
  28.2 1.1 %shard_map.146 = (f32[768,128]{1,0:T(8,128)S(1)}, f32[768,128]{1,0:T(8,128)S(1)}, f32[768,128]{1,0:T(8,128)S(1)}, f32[768,128]{1,0:T(8,128)S(1)}) custom-call(s32[1]{0:T(128)S(6)} %copy.22.count_ref.refs_0_, s32[1]{0:T(128)} %bitcast.place_ref.refs_1_, f32[6,96,128]{2,1,0:T(8,128)S(1)} %collective-permute-done.7.refs_2_, ...), custom_call_target="tpu_custom_call" | custom-call | tf_op jit(solution)/shard_map/pallas_call | solution.py:510
  29.3 4.1 %collective-permute-done.6.refs_2_ = f32[6,96,128]{2,1,0:T(8,128)S(1)} collective-permute-done((f32[6,96,128]{2,1,0:T(8,128)S(1)}, f32[6,96,128]{2,1,0:T(8,128)S(1)}, u32[]{:S(2)}, u32[]{:S(2)}) %collective-permute-start.6) | collective-permute-done | bytes 294944 | tf_op jit(solution)/shard_map/ppermute | solution.py:493
  33.4 2.2 %shard_map.147 = (f32[6,96,128]{2,1,0:T(8,128)S(1)}, f32[6,96,128]{2,1,0:T(8,128)S(1)}, f32[768,128]{1,0:T(8,128)S(1)}, f32[768,128]{1,0:T(8,128)S(1)}, f32[768,128]{1,0:T(8,128)S(1)}, /*index=5*/f32[768,128]{1,0:T(8,128)S(1)}) custom-call(s32[1]{0:T(128)S(6)} %copy.22.count_ref.refs_0_, s32[1]{0:T(128)} %bitcast.place_ref.refs_1_, ...), custom_call_target="tpu_custom_call" | custom-call | tf_op jit(solution)/shard_map/pallas_call | solution.py:526
  35.6 0.6 collective-permute-start.9
  36.3 1.2 %collective-permute-done.9.refs_2_ = f32[6,96,128]{2,1,0:T(8,128)S(1)} collective-permute-done((f32[6,96,128]{2,1,0:T(8,128)S(1)}, f32[6,96,128]{2,1,0:T(8,128)S(1)}, u32[]{:S(2)}, u32[]{:S(2)}) %collective-permute-start.9) | collective-permute-done | bytes 294944 | tf_op jit(solution)/shard_map/ppermute | solution.py:494
  37.5 1.1 %shard_map.148 = (f32[768,128]{1,0:T(8,128)S(1)}, f32[768,128]{1,0:T(8,128)S(1)}, f32[768,128]{1,0:T(8,128)S(1)}, f32[768,128]{1,0:T(8,128)S(1)}) custom-call(s32[1]{0:T(128)S(6)} %copy.22.count_ref.refs_0_, s32[1]{0:T(128)} %bitcast.place_ref.refs_1_, f32[6,96,128]{2,1,0:T(8,128)S(1)} %collective-permute-done.9.refs_2_, ...), custom_call_target="tpu_custom_call" | custom-call | tf_op jit(solution)/shard_map/pallas_call | solution.py:510
  38.6 4.1 %collective-permute-done.8.refs_2_ = f32[6,96,128]{2,1,0:T(8,128)S(1)} collective-permute-done((f32[6,96,128]{2,1,0:T(8,128)S(1)}, f32[6,96,128]{2,1,0:T(8,128)S(1)}, u32[]{:S(2)}, u32[]{:S(2)}) %collective-permute-start.8) | collective-permute-done | bytes 294944 | tf_op jit(solution)/shard_map/ppermute | solution.py:493
  42.7 2.1 %shard_map.149 = (f32[6,96,128]{2,1,0:T(8,128)S(1)}, f32[6,96,128]{2,1,0:T(8,128)S(1)}, f32[128,256]{1,0:T(8,128)S(1)}) custom-call(s32[1]{0:T(128)S(6)} %copy.22.count_ref.refs_0_, s32[1]{0:T(128)} %bitcast.place_ref.refs_1_, f32[6,96,128]{2,1,0:T(8,128)S(1)} %collective-permute-done.8.refs_2_, f32[768,128]{1,0:T(8,128)S(1)} %get-tuple-element.113.refs_3_, ...), custom_call_target="tpu_custom_call" | custom-call | tf_op jit(solution)/shard_map/pallas_call | solution.py:526
  44.9 0.1 copy.15
  45.0 23.7 %all_to_all.11 = f32[128,1,256]{2,1,0:T(1,128)S(1)} all-to-all(f32[128,1,256]{2,1,0:T(1,128)S(1)} %copy.15), channel_id=1, replica_groups=mesh['grp'=4,'dom'=32] {'grp','dom'}, dimensions={0} | all-to-all | bytes 262144 | tf_op jit(solution)/shard_map/all_to_all | solution.py:533
  68.7 1.2 %shard_map.150 = (f32[6,96,128]{2,1,0:T(8,128)}, f32[6,96,128]{2,1,0:T(8,128)}) custom-call(f32[128,256]{1,0:T(8,128)S(1)} %bitcast.19, f32[16,2048]{1,0:T(8,128)S(1)} %copy-done.2, f32[16,2048]{1,0:T(8,128)S(1)} %collective-permute-done.2.inv_before, bf16[2,96,16]{2,1,0:T(8,128)(2,1)S(1)} %get-tuple-element.126.pick_t, ...), custom_call_target="tpu_custom_call" | custom-call | tf_op jit(solution)/shard_map/pallas_call | solution.py:534
  (15 shorter events, 0.0 us)
Async XLA Ops:
  1.3 5.3 %copy-start.2 = (f32[16,2048]{1,0:T(8,128)S(1)}, f32[16,2048]{1,0:T(8,128)}, u32[]{:S(2)}) copy-start(f32[16,2048]{1,0:T(8,128)} %inv_own.1) | copy-start | bytes 393220
  1.3 7.7 %copy-start = (f32[1,2,96,128]{3,2,1,0:T(8,128)S(1)}, f32[1,2,96,128]{3,2,1,0:T(8,128)}, u32[]{:S(2)}) copy-start(f32[1,2,96,128]{3,2,1,0:T(8,128)} %param.17) | copy-start | bytes 294916
  3.7 4.1 %copy-start.5 = (f32[1,3,16]{2,0,1:T(1,128)S(1)}, f32[1,3,16]{2,0,1:T(1,128)}, u32[]{:S(2)}) copy-start(f32[1,3,16]{2,0,1:T(1,128)} %param.22) | copy-start | bytes 580
  3.8 5.3 %collective-permute-start.1 = (f32[8,96,128]{2,1,0:T(8,128)S(1)}, f32[8,96,128]{2,1,0:T(8,128)S(1)}, u32[]{:S(2)}, u32[]{:S(2)}) collective-permute-start(f32[8,96,128]{2,1,0:T(8,128)S(1)} %get-tuple-element.76), channel_id=1, source_target_pairs={{0,1},{1,0},{2,3},{3,2},{4,5},{5,4},{6,7},{7,6},{8,9},{9,8},{10,11... | collective-permute-start | bytes 1179656 | tf_op jit(solution)/shard_map/ppermute | solution.py:494
  5.2 7.5 %collective-permute-start = (f32[8,96,128]{2,1,0:T(8,128)S(1)}, f32[8,96,128]{2,1,0:T(8,128)S(1)}, u32[]{:S(2)}, u32[]{:S(2)}) collective-permute-start(f32[8,96,128]{2,1,0:T(8,128)S(1)} %get-tuple-element.67), channel_id=1, source_target_pairs={{1,2},{3,4},{5,6},{7,8},{9,10},{11,12},{13,14},{15,16},{17,18},{19... | collective-permute-start | bytes 1179656 | tf_op jit(solution)/shard_map/ppermute | solution.py:493
  6.6 6.0 %collective-permute-start.2 = (f32[16,2048]{1,0:T(8,128)S(1)}, f32[16,2048]{1,0:T(8,128)S(1)}, u32[]{:S(2)}, u32[]{:S(2)}) collective-permute-start(f32[16,2048]{1,0:T(8,128)S(1)} %copy-done.2), channel_id=1, source_target_pairs={{0,32},{32,64},{64,96},{96,0},{1,33},{33,65},{65,97},{97,1},{2,34}... | collective-permute-start | bytes 393224 | tf_op jit(solution)/shard_map/ppermute | solution.py:496
  7.8 4.8 %collective-permute-start.3 = (f32[3,16]{1,0:T(4,128)S(1)}, f32[3,16]{1,0:T(4,128)S(1)}, u32[]{:S(2)}, u32[]{:S(2)}) collective-permute-start(f32[3,16]{1,0:T(4,128)S(1)} %bitcast.23), channel_id=1, source_target_pairs={{0,32},{32,64},{64,96},{96,0},{1,33},{33,65},{65,97},{97,1},{2,34}... | collective-permute-start | bytes 584 | tf_op jit(solution)/shard_map/ppermute | solution.py:497
  12.7 4.7 %copy-start.1 = (f32[1,2,96,128]{3,2,1,0:T(8,128)S(1)}, f32[1,2,96,128]{3,2,1,0:T(8,128)}, u32[]{:S(2)}) copy-start(f32[1,2,96,128]{3,2,1,0:T(8,128)} %param.16) | copy-start | bytes 294916
  15.0 2.5 %copy-start.3 = (s32[1,16]{1,0:T(1,128)S(1)}, s32[1,16]{1,0:T(1,128)}, u32[]{:S(2)}) copy-start(s32[1,16]{1,0:T(1,128)} %own.1) | copy-start | bytes 196
  15.0 2.5 %copy-start.4 = (s32[1,16]{1,0:T(1,128)S(1)}, s32[1,16]{1,0:T(1,128)}, u32[]{:S(2)}) copy-start(s32[1,16]{1,0:T(1,128)} %peer.1) | copy-start | bytes 196
  15.0 3.6 %collective-permute-start.5 = (f32[6,96,128]{2,1,0:T(8,128)S(1)}, f32[6,96,128]{2,1,0:T(8,128)S(1)}, u32[]{:S(2)}, u32[]{:S(2)}) collective-permute-start(f32[6,96,128]{2,1,0:T(8,128)S(1)} %get-tuple-element.87), channel_id=1, source_target_pairs={{0,1},{1,0},{2,3},{3,2},{4,5},{5,4},{6,7},{7,6},{8,9},{9,8},{10,11... | collective-permute-start | bytes 884744 | tf_op jit(solution)/shard_map/ppermute | solution.py:494
  17.4 6.4 %collective-permute-start.4 = (f32[6,96,128]{2,1,0:T(8,128)S(1)}, f32[6,96,128]{2,1,0:T(8,128)S(1)}, u32[]{:S(2)}, u32[]{:S(2)}) collective-permute-start(f32[6,96,128]{2,1,0:T(8,128)S(1)} %get-tuple-element.82), channel_id=1, source_target_pairs={{1,2},{3,4},{5,6},{7,8},{9,10},{11,12},{13,14},{15,16},{17,18},{19... | collective-permute-start | bytes 884744 | tf_op jit(solution)/shard_map/ppermute | solution.py:493
  26.0 2.1 %collective-permute-start.7 = (f32[6,96,128]{2,1,0:T(8,128)S(1)}, f32[6,96,128]{2,1,0:T(8,128)S(1)}, u32[]{:S(2)}, u32[]{:S(2)}) collective-permute-start(f32[6,96,128]{2,1,0:T(8,128)S(1)} %get-tuple-element.107), channel_id=1, source_target_pairs={{0,1},{1,0},{2,3},{3,2},{4,5},{5,4},{6,7},{7,6},{8,9},{9,8},{10,11... | collective-permute-start | bytes 884744 | tf_op jit(solution)/shard_map/ppermute | solution.py:494
  27.0 6.4 %collective-permute-start.6 = (f32[6,96,128]{2,1,0:T(8,128)S(1)}, f32[6,96,128]{2,1,0:T(8,128)S(1)}, u32[]{:S(2)}, u32[]{:S(2)}) collective-permute-start(f32[6,96,128]{2,1,0:T(8,128)S(1)} %get-tuple-element.102), channel_id=1, source_target_pairs={{1,2},{3,4},{5,6},{7,8},{9,10},{11,12},{13,14},{15,16},{17,18},{19... | collective-permute-start | bytes 884744 | tf_op jit(solution)/shard_map/ppermute | solution.py:493
  35.6 1.9 %collective-permute-start.9 = (f32[6,96,128]{2,1,0:T(8,128)S(1)}, f32[6,96,128]{2,1,0:T(8,128)S(1)}, u32[]{:S(2)}, u32[]{:S(2)}) collective-permute-start(f32[6,96,128]{2,1,0:T(8,128)S(1)} %get-tuple-element.117), channel_id=1, source_target_pairs={{0,1},{1,0},{2,3},{3,2},{4,5},{5,4},{6,7},{7,6},{8,9},{9,8},{10,11... | collective-permute-start | bytes 884744 | tf_op jit(solution)/shard_map/ppermute | solution.py:494
  36.3 6.4 %collective-permute-start.8 = (f32[6,96,128]{2,1,0:T(8,128)S(1)}, f32[6,96,128]{2,1,0:T(8,128)S(1)}, u32[]{:S(2)}, u32[]{:S(2)}) collective-permute-start(f32[6,96,128]{2,1,0:T(8,128)S(1)} %get-tuple-element.112), channel_id=1, source_target_pairs={{1,2},{3,4},{5,6},{7,8},{9,10},{11,12},{13,14},{15,16},{17,18},{19... | collective-permute-start | bytes 884744 | tf_op jit(solution)/shard_map/ppermute | solution.py:493
